TPU v7x, 512 devices: a 4x2x32 block of a 4x8x32 slice. The times are simulated.
512 devices in a mesh: groups: 2 (over y), sky: 32 (over z), epoch: 4 (over x), band: 2 (over core).
Axes of the slice: x: 4, y: 2, z: 32, core: 2. Of those that a mesh axis runs over, the one named last changes fastest.
The devices are a block of a 4x8x32 slice.
Arguments:
- slot_pixels: bfloat16 [12288, 6, 32, 512], P(('groups', 'sky', 'epoch'), 'band'), parts along dimension 0, may hold values from -6 to 6
- slot_tile: int32 [12288, 1], P(('groups', 'sky', 'epoch')), parts along dimension 0, may hold values from 0 to 31; in each aligned block of 48 rows (0 to 47, 48 to 95, ...) at most 2 rows name the same one
- slot_offset: int32 [12288, 2], P(('groups', 'sky', 'epoch')), parts along dimension 0, may hold values from -5 to 5
- slot_frac: bfloat16 [12288, 2], P(('groups', 'sky', 'epoch')), parts along dimension 0, may hold values from 0.049804688 to 0.94921875
- slot_sigma: bfloat16 [12288, 6], P(('groups', 'sky', 'epoch'), 'band'), parts along dimension 0, may hold values from 0.5 to 2
- clip_mask: int32 [12288, 6, 16], P(('groups', 'sky', 'epoch')), parts along dimension 0, may hold values 0 or 1
- slot_count: int32 [256], P(('groups', 'sky', 'epoch')), parts along dimension 0, may hold values from 36 to 48
- template: bfloat16 [6, 2048, 512], P('band', ('groups', 'sky')), parts along dimension 1, may hold values from -6 to 6
- prior_weight: float32 [6, 2048], P('band', ('groups', 'sky')), parts along dimension 1, may hold values from 0.5 to 4
Outputs:
- coadd_image: bfloat16 [6, 2048, 512], P('band', ('groups', 'sky'), 'epoch'), parts along dimension 1
- depth_norm: bfloat16 [6, 2048, 512], P('band', ('groups', 'sky'), 'epoch'), parts along dimension 1
There are 2 independent parts, one for each index of `groups`. A program takes and returns all parts, laid end to end along the dimension named above; each array names one. Nothing has to cross between parts.
Inputs may be any that keep to these rules, and one draw needn't show every extreme that they name: `slot_tile`: among the 48 rows of one reading device no owner is named more than 2 times, a bound that some block reaches. `slot_count`: slots of a reading device at or after its count are padding.
All inputs are finite; a program needn't handle non-finite values. No bound on the sum of `clip_mask` on one device may be relied on, other than what follows from the above.
Results may differ from a plain program's by a relative error of at most 0.014.
Values may be sent and summed in bfloat16 or wider, within the bound.
No kernel may reach another device: no remote copies, remote signals or barrier semaphores. Data moves between devices by JAX's collectives and lax.ppermute only.
A program may use at most 64 MiB of HBM per device.

v0:
```python
import functools
import math

import jax
import jax.numpy as jnp
from jax import lax
from jax.sharding import PartitionSpec as P

ROWS_DEV = 32
MARGIN = 8
CAPACITY = 2


CLIP_WIDTH = 3.0


def split_up(shard, dim, size):
    lengths = shard.shape
    parts = shard.reshape(*lengths[:dim], size, lengths[dim] // size, *lengths[dim + 1 :])
    return jnp.moveaxis(parts, dim, 0)


def summed_on_arrival(shard, axis, dim):
    parts = split_up(shard, dim, lax.axis_size(axis))
    arrived = lax.all_to_all(parts, axis, split_axis=0, concat_axis=0, tiled=True)
    return arrived.astype(jnp.float32).sum(axis=0)


def padded(cells, sides, width):
    for axis, dim in sides:
        count = lax.axis_size(axis)
        ends = count - 1
        head = lax.slice_in_dim(cells, 0, width, axis=dim)
        tail = lax.slice_in_dim(cells, cells.shape[dim] - width, cells.shape[dim], axis=dim)
        cells = jnp.concatenate(
            [
                lax.ppermute(tail, axis, [(i, (i + 1) % count) for i in range(ends)]),
                cells,
                lax.ppermute(head, axis, [((i + 1) % count, i) for i in range(ends)]),
            ],
            axis=dim,
        )
    return cells


def side_by_side(arrays, axis, split_dim, concat_dim, along):
    ends, at = ([], 0)
    for a in arrays[:-1]:
        at += a.shape[along]
        ends.append(at)
    both = jnp.concatenate(arrays, axis=along)
    return tuple(
        jnp.split(
            lax.all_to_all(both, axis, split_axis=split_dim, concat_axis=concat_dim, tiled=True),
            ends,
            axis=along,
        )
    )


def one_axis_at_a_time(shard, axes):
    return functools.reduce(lax.psum, axes, shard)


def lanczos(distance):
    inside = jnp.abs(distance) < 3.0
    return jnp.where(inside, jnp.sinc(distance) * jnp.sinc(distance / 3.0), 0.0)


def warp_table(shifts, fractions, length_out, length_in, margin_rows):
    out_index = lax.broadcasted_iota(jnp.int32, (1, length_out, length_in), 1)
    in_index = lax.broadcasted_iota(jnp.int32, (1, length_out, length_in), 2)
    gap_index = out_index - margin_rows - shifts[:, None, None] - in_index
    distance = gap_index.astype(jnp.float32) - fractions[:, None, None]
    return lanczos(distance).astype(jnp.bfloat16)


def warp_columns(pixels, shifts, fractions):
    tile_cols = pixels.shape[3]
    kernel_table = warp_table(shifts, fractions, tile_cols, tile_cols, 0)
    warped = jnp.einsum("sbrk,sjk->sbrj", pixels, kernel_table, preferred_element_type=jnp.float32)
    return warped.astype(jnp.bfloat16)


def column_cover(shifts, fractions, tile_cols):
    column_index = lax.broadcasted_iota(jnp.int32, (1, tile_cols), 1)
    cover = jnp.zeros((shifts.shape[0], tile_cols), jnp.float32)
    for step_back in range(-3, 3):
        rounded = lanczos(jnp.float32(-step_back) - fractions).astype(jnp.bfloat16)
        weight_tap = lax.optimization_barrier(rounded).astype(jnp.float32)
        source_col = column_index - shifts[:, None] + step_back
        inside = (source_col >= 0) & (source_col < tile_cols)
        cover = cover + jnp.where(inside, weight_tap[:, None], 0.0)
    return jnp.clip(cover, 0.0, 1.0)


def epoch_sum(totals):
    return summed_on_arrival(totals.astype(jnp.bfloat16), "epoch", 3)


def add_seams(totals):
    rims = jnp.concatenate([totals[:, :, :MARGIN], totals[:, :, -MARGIN:]], 2)
    framed_rims = padded(rims.astype(jnp.bfloat16), (("sky", 2),), MARGIN).astype(rims.dtype)
    own_rows = totals[:, :, MARGIN : MARGIN + ROWS_DEV]
    own_rows = own_rows.at[:, :, :MARGIN].add(framed_rims[:, :, :MARGIN])
    own_rows = own_rows.at[:, :, ROWS_DEV - MARGIN :].add(framed_rims[:, :, 3 * MARGIN :])
    return own_rows


def on_device(
    slot_pixels,
    slot_tile,
    slot_offset,
    slot_frac,
    slot_sigma,
    clip_mask,
    slot_count,
    template,
    prior_weight,
):
    sky_count = lax.axis_size("sky")
    held = slot_pixels.shape[0]
    tile_cols = slot_pixels.shape[3]
    local_bands = slot_pixels.shape[1]
    canvas_rows = ROWS_DEV + 2 * MARGIN
    routes_total = sky_count * CAPACITY
    target = slot_tile[:, 0]
    owners = jnp.arange(sky_count, dtype=jnp.int32)
    onehot = (target[:, None] == owners[None, :]).astype(jnp.int32)
    slot_rank = jnp.sum(jnp.cumsum(onehot, 0) * onehot, 1) - 1
    position = target * CAPACITY + slot_rank
    held_index = jnp.arange(held, dtype=jnp.int32)
    is_live = held_index < slot_count[0]
    chooser = position[None, :] == jnp.arange(routes_total, dtype=jnp.int32)[:, None]
    source = jnp.sum(jnp.where(chooser, held_index[None, :], 0), 1)
    filled = jnp.any(chooser & is_live[None, :], 1).astype(jnp.int32)

    def pack(array):
        taken = jnp.take(array, source, axis=0)
        return taken.reshape((sky_count, CAPACITY) + array.shape[1:])

    packed_mask = pack(clip_mask) * filled.reshape(sky_count, CAPACITY)[:, :, None, None]
    received = (
        lax.all_to_all(pack(slot_pixels), "sky", split_axis=0, concat_axis=0, tiled=True),
        lax.all_to_all(pack(slot_offset), "sky", split_axis=0, concat_axis=0, tiled=True),
        *side_by_side((pack(slot_frac), pack(slot_sigma)), "sky", 0, 0, 2),
        lax.all_to_all(packed_mask, "sky", split_axis=0, concat_axis=0, tiled=True),
    )
    received = tuple((array.reshape((routes_total,) + array.shape[2:]) for array in received))
    framed = padded(template, (("sky", 1),), MARGIN).astype(jnp.float32)

    def accumulate(totals, pieces):
        pixels, offsets, fractions, sigmas, masks = pieces
        fractions = fractions.astype(jnp.float32)
        columns = warp_columns(pixels, offsets[:, 1], fractions[:, 1])
        row_table = warp_table(offsets[:, 0], fractions[:, 0], canvas_rows, ROWS_DEV, MARGIN)
        warped = jnp.einsum(
            "sir,sbrj->sbij", row_table, columns, preferred_element_type=jnp.float32
        )
        row_cover = jnp.clip(jnp.sum(row_table.astype(jnp.float32), 2), 0.0, 1.0)
        col_cover = column_cover(offsets[:, 1], fractions[:, 1], tile_cols)
        block_slots = masks.shape[0]
        block_mask = masks.astype(jnp.float32)
        expanded = jnp.broadcast_to(
            block_mask[:, :, None, :, None], (block_slots, canvas_rows // 8, 8, tile_cols // 32, 32)
        )
        expanded = expanded.reshape(block_slots, canvas_rows, tile_cols)
        plane = expanded * row_cover[:, :, None] * col_cover[:, None, :]
        sigma_values = sigmas.astype(jnp.float32)
        weight = plane[:, None] / (sigma_values * sigma_values)[:, :, None, None]
        scale = CLIP_WIDTH * sigma_values[:, :, None, None]
        clipped = framed[None] + scale * jnp.tanh((warped - framed[None]) / scale)
        flux_part = jnp.sum(weight * clipped, 0)
        weight_part = jnp.sum(weight, 0)
        return (totals + jnp.stack([flux_part, weight_part], 0), None)

    block_slots = math.gcd(8, routes_total)
    blocked = tuple(
        (
            array.reshape((routes_total // block_slots, block_slots) + array.shape[1:])
            for array in received
        )
    )
    initial = jnp.zeros((2, local_bands, canvas_rows, tile_cols), jnp.float32)
    totals, _ = lax.scan(accumulate, initial, blocked)
    own_rows = add_seams(epoch_sum(totals))
    flux_sum = own_rows[0]
    weight_sum = own_rows[1]
    part_width = own_rows.shape[3]
    epoch_position = lax.axis_index("epoch")
    template_part = lax.dynamic_slice_in_dim(
        template, epoch_position * part_width, part_width, 2
    ).astype(jnp.float32)
    prior = prior_weight[:, :, None]
    coadd_image = ((flux_sum + prior * template_part) / (weight_sum + prior)).astype(jnp.bfloat16)
    depth_map = weight_sum + prior
    band_total = one_axis_at_a_time(jnp.sum(depth_map, axis=(1, 2)), ("sky", "epoch"))
    band_mean = band_total / (ROWS_DEV * sky_count * tile_cols)
    depth_norm = (depth_map / band_mean[:, None, None]).astype(jnp.bfloat16)
    return (coadd_image, depth_norm)


def solution(mesh):
    in_specs = (
        P(("groups", "sky", "epoch"), "band", None, None),
        P(("groups", "sky", "epoch"), None),
        P(("groups", "sky", "epoch"), None),
        P(("groups", "sky", "epoch"), None),
        P(("groups", "sky", "epoch"), "band"),
        P(("groups", "sky", "epoch"), None, None),
        P(("groups", "sky", "epoch")),
        P("band", ("groups", "sky"), None),
        P("band", ("groups", "sky")),
    )
    out_specs = (P("band", ("groups", "sky"), "epoch"), P("band", ("groups", "sky"), "epoch"))
    return jax.shard_map(
        on_device, mesh=mesh, in_specs=in_specs, out_specs=out_specs, check_vma=False
    )
```

profile of v0, /device:TPU:40, one launch (start us, length us, event | category | flops | bytes accessed | tf_op | source)
XLA Modules:
  0.0 1011.3 jit_solution(4690587157069409075)
XLA Ops:
  5.5 45.8 %all-to-all-start.1 = ((s32[32,2,2]{1,2,0:T(2,128)}), s32[32,2,2]{1,2,0:T(2,128)S(1)}, u32[]{:S(2)}, u32[]{:S(2)}) async-start(s32[32,2,2]{1,2,0:T(2,128)} %copy.89), calls=%async_computation.1 | async-start | bytes 65536 | tf_op jit(solution)/shard_map/all_to_all | solution.py:145
  58.0 15.7 %all-to-all-done.1 = s32[32,2,2]{1,2,0:T(2,128)S(1)} async-done(((s32[32,2,2]{1,2,0:T(2,128)}), s32[32,2,2]{1,2,0:T(2,128)S(1)}, u32[]{:S(2)}, u32[]{:S(2)}) %all-to-all-start.1) | async-done | bytes 544 | tf_op jit(solution)/shard_map/all_to_all | solution.py:145
  73.8 6.3 all-to-all-start.2
  81.1 5.9 gather_fusion.4
  87.0 14.7 %all-to-all-done.2 = bf16[32,2,5]{2,1,0:T(2,128)(2,1)S(1)} async-done(((bf16[32,2,5]{2,1,0:T(2,128)(2,1)}), bf16[32,2,5]{2,1,0:T(2,128)(2,1)S(1)}, u32[]{:S(2)}, u32[]{:S(2)}) %all-to-all-start.2) | async-done | bytes 672 | tf_op jit(solution)/shard_map/all_to_all | solution.py:54
  101.7 7.3 all-to-all-start
  109.1 6.1 broadcast_select_fusion
  115.2 16.3 %all-to-all-done = s32[32,1,192]{2,1,0:T(1,128)S(1)} async-done(((s32[32,1,192]{2,1,0:T(1,128)}), s32[32,1,192]{2,1,0:T(1,128)S(1)}, u32[]{:S(2)}, u32[]{:S(2)}) %all-to-all-start) | async-done | bytes 24608 | tf_op jit(solution)/shard_map/all_to_all | solution.py:147
  131.5 5.8 all-to-all-start.3
  137.4 3.3 collective-permute-start
  142.4 518.0 %collective-permute-done = bf16[3,8,512]{2,1,0:T(8,128)(2,1)S(1)} collective-permute-done((bf16[3,8,512]{2,1,0:T(8,128)(2,1)S(1)}, bf16[3,8,512]{2,1,0:T(8,128)(2,1)S(1)}, u32[]{:S(2)}, u32[]{:S(2)}) %collective-permute-start) | collective-permute-done | bytes 24608 | tf_op jit(solution)/shard_map/ppermute | solution.py:37
  660.5 12.7 %collective-permute-done.1 = bf16[3,8,512]{2,1,0:T(8,128)(2,1)S(1)} collective-permute-done((bf16[3,8,512]{2,1,0:T(8,128)(2,1)S(1)}, bf16[3,8,512]{2,1,0:T(8,128)(2,1)S(1)}, u32[]{:S(2)}, u32[]{:S(2)}) %collective-permute-start.1) | collective-permute-done | bytes 24608 | tf_op jit(solution)/shard_map/ppermute | solution.py:39
  675.5 3.7 all-to-all-done.3
  679.1 231.2 %while.15 = (s32[]{:T(128)}, f32[2,3,48,512]{3,2,1,0:T(8,128)}, s32[8,8,6,16]{3,1,0,2:T(8,128)S(1)}, s32[8,8,2]{1,0,2:T(8,128)S(1)}, bf16[8,8,2]{1,2,0:T(2,128)(...) while((s32[]{:T(128)}, f32[2,3,48,512]{3,2,1,0:T(8,128)}, ...), condition=%wide.region_8.12_spmd.clone, body=%wide.region_4.11_spmd.clone.sunk | while | flops 606097728 | bytes 13722023 | solution.py:185
  680.2 2.1 reshape.369
  683.7 23.0 %fusion.228 = f32[3,48,512]{2,1,0:T(8,128)S(1)} fusion(f32[8,3]{1,0:T(8,128)S(1)} %copy.121, f32[3,48,512]{2,1,0:T(8,128)} %get-tuple-element.331, f32[8,3]{1,0:T(8,128)S(1)} %copy.120, f32[8,48,512]{2,1,0:T(8,128)S(1)} %multiply_multiply_fusion.30, f32[8]{0:T(128)S(1)} %get-tuple-element.304, s32[8]{0:T(128)S(1)} %get-tuple-element.300, ...), kind=kOutput, calls=%fused_computation.69.clone.1 | convolution fusion | flops 603058176 | bytes 2163712 | tf_op jit(solution)/shard_map/while/body/eval_jaxpr/sir,sbrj->sbij/dot_general | solution.py:157
  709.1 2.1 reshape.369
  712.6 23.0 %fusion.228 = f32[3,48,512]{2,1,0:T(8,128)S(1)} fusion(f32[8,3]{1,0:T(8,128)S(1)} %copy.121, f32[3,48,512]{2,1,0:T(8,128)} %get-tuple-element.331, f32[8,3]{1,0:T(8,128)S(1)} %copy.120, f32[8,48,512]{2,1,0:T(8,128)S(1)} %multiply_multiply_fusion.30, f32[8]{0:T(128)S(1)} %get-tuple-element.304, s32[8]{0:T(128)S(1)} %get-tuple-element.300, ...), kind=kOutput, calls=%fused_computation.69.clone.1 | convolution fusion | flops 603058176 | bytes 2163712 | tf_op jit(solution)/shard_map/while/body/eval_jaxpr/sir,sbrj->sbij/dot_general | solution.py:157
  738.0 2.1 reshape.369
  741.5 23.0 %fusion.228 = f32[3,48,512]{2,1,0:T(8,128)S(1)} fusion(f32[8,3]{1,0:T(8,128)S(1)} %copy.121, f32[3,48,512]{2,1,0:T(8,128)} %get-tuple-element.331, f32[8,3]{1,0:T(8,128)S(1)} %copy.120, f32[8,48,512]{2,1,0:T(8,128)S(1)} %multiply_multiply_fusion.30, f32[8]{0:T(128)S(1)} %get-tuple-element.304, s32[8]{0:T(128)S(1)} %get-tuple-element.300, ...), kind=kOutput, calls=%fused_computation.69.clone.1 | convolution fusion | flops 603058176 | bytes 2163712 | tf_op jit(solution)/shard_map/while/body/eval_jaxpr/sir,sbrj->sbij/dot_general | solution.py:157
  766.9 2.1 reshape.369
  770.4 23.0 %fusion.228 = f32[3,48,512]{2,1,0:T(8,128)S(1)} fusion(f32[8,3]{1,0:T(8,128)S(1)} %copy.121, f32[3,48,512]{2,1,0:T(8,128)} %get-tuple-element.331, f32[8,3]{1,0:T(8,128)S(1)} %copy.120, f32[8,48,512]{2,1,0:T(8,128)S(1)} %multiply_multiply_fusion.30, f32[8]{0:T(128)S(1)} %get-tuple-element.304, s32[8]{0:T(128)S(1)} %get-tuple-element.300, ...), kind=kOutput, calls=%fused_computation.69.clone.1 | convolution fusion | flops 603058176 | bytes 2163712 | tf_op jit(solution)/shard_map/while/body/eval_jaxpr/sir,sbrj->sbij/dot_general | solution.py:157
  799.3 23.0 %fusion.228 = f32[3,48,512]{2,1,0:T(8,128)S(1)} fusion(f32[8,3]{1,0:T(8,128)S(1)} %copy.121, f32[3,48,512]{2,1,0:T(8,128)} %get-tuple-element.331, f32[8,3]{1,0:T(8,128)S(1)} %copy.120, f32[8,48,512]{2,1,0:T(8,128)S(1)} %multiply_multiply_fusion.30, f32[8]{0:T(128)S(1)} %get-tuple-element.304, s32[8]{0:T(128)S(1)} %get-tuple-element.300, ...), kind=kOutput, calls=%fused_computation.69.clone.1 | convolution fusion | flops 603058176 | bytes 2163712 | tf_op jit(solution)/shard_map/while/body/eval_jaxpr/sir,sbrj->sbij/dot_general | solution.py:157
  828.2 23.0 %fusion.228 = f32[3,48,512]{2,1,0:T(8,128)S(1)} fusion(f32[8,3]{1,0:T(8,128)S(1)} %copy.121, f32[3,48,512]{2,1,0:T(8,128)} %get-tuple-element.331, f32[8,3]{1,0:T(8,128)S(1)} %copy.120, f32[8,48,512]{2,1,0:T(8,128)S(1)} %multiply_multiply_fusion.30, f32[8]{0:T(128)S(1)} %get-tuple-element.304, s32[8]{0:T(128)S(1)} %get-tuple-element.300, ...), kind=kOutput, calls=%fused_computation.69.clone.1 | convolution fusion | flops 603058176 | bytes 2163712 | tf_op jit(solution)/shard_map/while/body/eval_jaxpr/sir,sbrj->sbij/dot_general | solution.py:157
  853.6 2.1 reshape.369
  857.1 23.0 %fusion.228 = f32[3,48,512]{2,1,0:T(8,128)S(1)} fusion(f32[8,3]{1,0:T(8,128)S(1)} %copy.121, f32[3,48,512]{2,1,0:T(8,128)} %get-tuple-element.331, f32[8,3]{1,0:T(8,128)S(1)} %copy.120, f32[8,48,512]{2,1,0:T(8,128)S(1)} %multiply_multiply_fusion.30, f32[8]{0:T(128)S(1)} %get-tuple-element.304, s32[8]{0:T(128)S(1)} %get-tuple-element.300, ...), kind=kOutput, calls=%fused_computation.69.clone.1 | convolution fusion | flops 603058176 | bytes 2163712 | tf_op jit(solution)/shard_map/while/body/eval_jaxpr/sir,sbrj->sbij/dot_general | solution.py:157
  886.0 23.0 %fusion.228 = f32[3,48,512]{2,1,0:T(8,128)S(1)} fusion(f32[8,3]{1,0:T(8,128)S(1)} %copy.121, f32[3,48,512]{2,1,0:T(8,128)} %get-tuple-element.331, f32[8,3]{1,0:T(8,128)S(1)} %copy.120, f32[8,48,512]{2,1,0:T(8,128)S(1)} %multiply_multiply_fusion.30, f32[8]{0:T(128)S(1)} %get-tuple-element.304, s32[8]{0:T(128)S(1)} %get-tuple-element.300, ...), kind=kOutput, calls=%fused_computation.69.clone.1 | convolution fusion | flops 603058176 | bytes 2163712 | tf_op jit(solution)/shard_map/while/body/eval_jaxpr/sir,sbrj->sbij/dot_general | solution.py:157
  911.6 11.2 %all_to_all.25 = bf16[4,2,3,48,128]{4,3,2,1,0:T(8,128)(2,1)S(1)} all-to-all(bf16[4,2,3,48,128]{4,3,2,1,0:T(8,128)(2,1)S(1)} %copy.101), channel_id=1, replica_groups=mesh['groups'=2,'sky'=32,'epoch'=4,'band'=2] {'epoch'}, dimensions={0} | all-to-all | bytes 589824 | tf_op jit(solution)/shard_map/all_to_all | solution.py:25
  922.9 16.4 %collective-permute-start.2 = (bf16[2,3,8,128]{3,2,1,0:T(8,128)(2,1)S(1)}, bf16[2,3,8,128]{3,2,1,0:T(8,128)(2,1)S(1)}, u32[]{:S(2)}, u32[]{:S(2)}) collective-permute-start(bf16[2,3,8,128]{3,2,1,0:T(8,128)(2,1)S(1)} %get-tuple-element.230), channel_id=1, source_target_pairs={{0,8},{8,16},{16,24},{24,32},{32,40},{40,48},{48,56},{56,64},{64,7... | collective-permute-start | bytes 36872 | tf_op jit(solution)/shard_map/ppermute | solution.py:37
  940.7 4.2 collective-permute-done.3
  945.1 55.8 %psum.14 = f32[3]{0:T(128)S(1)} all-reduce(f32[3]{0:T(128)S(1)} %fusion.204), channel_id=1, replica_groups=mesh['groups'=2,'sky'=32,'epoch'=4,'band'=2] {'sky'}, use_global_device_ids=true, to_apply=%region_11.15 | all-reduce | flops 3 | bytes 24 | tf_op jit(solution)/shard_map/psum | solution.py:62
  1000.9 8.9 psum.15
  (290 shorter events, 55.4 us)
Async XLA Ops:
  5.5 68.3 %all-to-all-start.1 = ((s32[32,2,2]{1,2,0:T(2,128)}), s32[32,2,2]{1,2,0:T(2,128)S(1)}, u32[]{:S(2)}, u32[]{:S(2)}) async-start(s32[32,2,2]{1,2,0:T(2,128)} %copy.89), calls=%async_computation.1 | async-start | bytes 65536 | tf_op jit(solution)/shard_map/all_to_all | solution.py:145
  73.8 28.0 %all-to-all-start.2 = ((bf16[32,2,5]{2,1,0:T(2,128)(2,1)}), bf16[32,2,5]{2,1,0:T(2,128)(2,1)S(1)}, u32[]{:S(2)}, u32[]{:S(2)}) async-start(bf16[32,2,5]{2,1,0:T(2,128)(2,1)} %pad_maximum_fusion), calls=%async_computation.2 | async-start | bytes 32768 | tf_op jit(solution)/shard_map/all_to_all | solution.py:54
  101.7 29.8 %all-to-all-start = ((s32[32,1,192]{2,1,0:T(1,128)}), s32[32,1,192]{2,1,0:T(1,128)S(1)}, u32[]{:S(2)}, u32[]{:S(2)}) async-start(s32[32,1,192]{2,1,0:T(1,128)} %reshape.366), calls=%async_computation | async-start | bytes 65536 | tf_op jit(solution)/shard_map/all_to_all | solution.py:147
  115.2 22.2 %copy-start.2 = (bf16[3,32,512]{2,1,0:T(8,128)(2,1)S(1)}, bf16[3,32,512]{2,1,0:T(8,128)(2,1)}, u32[]{:S(2)}) copy-start(bf16[3,32,512]{2,1,0:T(8,128)(2,1)} %param.25) | copy-start | bytes 294916
  131.5 547.6 %all-to-all-start.3 = ((bf16[32,2,3,32,512]{4,3,2,1,0:T(8,128)(2,1)}), bf16[32,2,3,32,512]{4,3,2,1,0:T(8,128)(2,1)}, u32[]{:S(2)}, u32[]{:S(2)}) async-start(bf16[32,2,3,32,512]{4,3,2,1,0:T(8,128)(2,1)} %broadcast_select_fusion), calls=%async_computation.3 | async-start | bytes 12582912 | tf_op jit(solution)/shard_map/all_to_all | solution.py:144
  137.4 523.1 %collective-permute-start = (bf16[3,8,512]{2,1,0:T(8,128)(2,1)S(1)}, bf16[3,8,512]{2,1,0:T(8,128)(2,1)S(1)}, u32[]{:S(2)}, u32[]{:S(2)}) collective-permute-start(bf16[3,8,512]{2,1,0:T(8,128)(2,1)S(1)} %get-tuple-element.228), channel_id=1, source_target_pairs={{0,8},{8,16},{16,24},{24,32},{32,40},{40,48},{48,56},{56,64},{64,7... | collective-permute-start | bytes 73736 | tf_op jit(solution)/shard_map/ppermute | solution.py:37
  140.7 532.5 %collective-permute-start.1 = (bf16[3,8,512]{2,1,0:T(8,128)(2,1)S(1)}, bf16[3,8,512]{2,1,0:T(8,128)(2,1)S(1)}, u32[]{:S(2)}, u32[]{:S(2)}) collective-permute-start(bf16[3,8,512]{2,1,0:T(8,128)(2,1)S(1)} %get-tuple-element.229), channel_id=1, source_target_pairs={{8,0},{16,8},{24,16},{32,24},{40,32},{48,40},{56,48},{64,56},{72,6... | collective-permute-start | bytes 73736 | tf_op jit(solution)/shard_map/ppermute | solution.py:39
  679.1 265.8 %copy-start.3 = (f32[3,32]{1,0:T(4,128)S(1)}, f32[3,32]{1,0:T(4,128)}, u32[]{:S(2)}) copy-start(f32[3,32]{1,0:T(4,128)} %param.26) | copy-start | bytes 1156
  683.7 23.3 %copy-start = (f32[2,3,48,512]{3,2,1,0:T(8,128)S(1)}, f32[2,3,48,512]{3,2,1,0:T(8,128)}, u32[]{:S(2)}) copy-start(f32[2,3,48,512]{3,2,1,0:T(8,128)} %get-tuple-element.316) | copy-start | bytes 1769476 | tf_op jit(solution)/shard_map/while
  707.2 0.8 copy-start.1
  712.6 23.3 %copy-start = (f32[2,3,48,512]{3,2,1,0:T(8,128)S(1)}, f32[2,3,48,512]{3,2,1,0:T(8,128)}, u32[]{:S(2)}) copy-start(f32[2,3,48,512]{3,2,1,0:T(8,128)} %get-tuple-element.316) | copy-start | bytes 1769476 | tf_op jit(solution)/shard_map/while
  736.1 0.8 copy-start.1
  741.5 23.3 %copy-start = (f32[2,3,48,512]{3,2,1,0:T(8,128)S(1)}, f32[2,3,48,512]{3,2,1,0:T(8,128)}, u32[]{:S(2)}) copy-start(f32[2,3,48,512]{3,2,1,0:T(8,128)} %get-tuple-element.316) | copy-start | bytes 1769476 | tf_op jit(solution)/shard_map/while
  765.0 0.8 copy-start.1
  770.4 23.3 %copy-start = (f32[2,3,48,512]{3,2,1,0:T(8,128)S(1)}, f32[2,3,48,512]{3,2,1,0:T(8,128)}, u32[]{:S(2)}) copy-start(f32[2,3,48,512]{3,2,1,0:T(8,128)} %get-tuple-element.316) | copy-start | bytes 1769476 | tf_op jit(solution)/shard_map/while
  793.9 0.8 copy-start.1
  799.3 23.3 %copy-start = (f32[2,3,48,512]{3,2,1,0:T(8,128)S(1)}, f32[2,3,48,512]{3,2,1,0:T(8,128)}, u32[]{:S(2)}) copy-start(f32[2,3,48,512]{3,2,1,0:T(8,128)} %get-tuple-element.316) | copy-start | bytes 1769476 | tf_op jit(solution)/shard_map/while
  822.8 0.8 copy-start.1
  828.2 23.3 %copy-start = (f32[2,3,48,512]{3,2,1,0:T(8,128)S(1)}, f32[2,3,48,512]{3,2,1,0:T(8,128)}, u32[]{:S(2)}) copy-start(f32[2,3,48,512]{3,2,1,0:T(8,128)} %get-tuple-element.316) | copy-start | bytes 1769476 | tf_op jit(solution)/shard_map/while
  851.7 0.8 copy-start.1
  857.1 23.3 %copy-start = (f32[2,3,48,512]{3,2,1,0:T(8,128)S(1)}, f32[2,3,48,512]{3,2,1,0:T(8,128)}, u32[]{:S(2)}) copy-start(f32[2,3,48,512]{3,2,1,0:T(8,128)} %get-tuple-element.316) | copy-start | bytes 1769476 | tf_op jit(solution)/shard_map/while
  880.6 0.8 copy-start.1
  886.0 23.3 %copy-start = (f32[2,3,48,512]{3,2,1,0:T(8,128)S(1)}, f32[2,3,48,512]{3,2,1,0:T(8,128)}, u32[]{:S(2)}) copy-start(f32[2,3,48,512]{3,2,1,0:T(8,128)} %get-tuple-element.316) | copy-start | bytes 1769476 | tf_op jit(solution)/shard_map/while
  909.5 0.8 copy-start.1
  922.9 17.8 %collective-permute-start.2 = (bf16[2,3,8,128]{3,2,1,0:T(8,128)(2,1)S(1)}, bf16[2,3,8,128]{3,2,1,0:T(8,128)(2,1)S(1)}, u32[]{:S(2)}, u32[]{:S(2)}) collective-permute-start(bf16[2,3,8,128]{3,2,1,0:T(8,128)(2,1)S(1)} %get-tuple-element.230), channel_id=1, source_target_pairs={{0,8},{8,16},{16,24},{24,32},{32,40},{40,48},{48,56},{56,64},{64,7... | collective-permute-start | bytes 36872 | tf_op jit(solution)/shard_map/ppermute | solution.py:37
  939.3 5.6 collective-permute-start.3
where the time goes:
time: 1010 us
  waiting for transfers between devices  585 us (58%)
  matrix products  184 us (18%)
  starting transfers between devices  87.5 us (9%)
  blocking collectives  76 us (8%)
  local copies, waits for them, and re-layouts  42.7 us (4%)
  other arithmetic  32.6 us (3%)
    ppermute x2, waiting for transfers between devices, padded(): lax.ppermute(tail, axis, [(i, (i + 1) % count) for i in range(ends)])  518 us
    dot_general x8, matrix products, accumulate(): jnp.einsum('sir,sbrj->sbij', row_table, columns, preferred_element_type=j...  184 us
    psum x2, blocking collectives, one_axis_at_a_time(): return functools.reduce(lax.psum, axes, shard)  64.7 us
    all_to_all x1, starting transfers between devices, on_device(): lax.all_to_all(pack(slot_offset), 'sky', split_axis=0, concat_axis=0, til...  45.8 us
  transfers between devices with their start and end apart: 8, of which 7 were waited for; matrix products, arithmetic and copies ran while one was open for 2% of the time, Pallas kernels for 0%

commit v1 on v0

v1 whole, which is shorter than its diff:
```python
import functools

import jax
import jax.numpy as jnp
from jax import lax
from jax.experimental import pallas as pl
from jax.experimental.pallas import tpu as pltpu
from jax.sharding import PartitionSpec as P

MARGIN = 8
CAPACITY = 2
CLIP_WIDTH = 3.0
TAPS = 6
ROW_BLOCK = 8
LANES = 128
GROUP = 8


def lanczos(distance):
    inside = jnp.abs(distance) < 3.0
    return jnp.where(inside, jnp.sinc(distance) * jnp.sinc(distance / 3.0), 0.0)


def tap_weights(fractions):
    gaps = 3.0 - jnp.arange(TAPS, dtype=jnp.float32)
    rounded = lanczos(gaps - fractions[..., None]).astype(jnp.bfloat16)
    return lax.optimization_barrier(rounded).astype(jnp.float32)


def cover(shifts, taps, index, length_in):
    total = jnp.zeros((shifts.shape[0], index.shape[0]), jnp.float32)
    for tap in range(TAPS):
        source = index[None, :] - shifts[:, None] + (tap - 3)
        inside = (source >= 0) & (source < length_in)
        total = total + jnp.where(inside, taps[:, tap][:, None], 0.0)
    return jnp.clip(total, 0.0, 1.0)


def column_kernel(ints, floats, pixels, out, tables):
    step = pl.program_id(0)
    slots, bands, rows, cols = pixels.shape
    blocks = cols // LANES
    edge = 16

    @pl.when(step == 0)
    def _():
        tables[...] = jnp.zeros_like(tables)

    def gap_base(first_row, count, offset):
        k = lax.broadcasted_iota(jnp.int32, (count, LANES), 0) + first_row
        j = lax.broadcasted_iota(jnp.int32, (count, LANES), 1)
        return j - k + offset

    def one(slot, table):
        at = step * slots + slot
        shift = ints[at]
        weights = [floats[at * TAPS + tap] for tap in range(TAPS)]

        def band_of(base):
            gap = base - shift
            value = jnp.zeros(base.shape, jnp.float32)
            for tap in range(TAPS):
                value = jnp.where(gap == 3 - tap, weights[tap], value)
            return value.astype(jnp.bfloat16)

        diagonal = band_of(gap_base(0, LANES, 0))
        upper = band_of(gap_base(LANES - edge, edge, LANES))
        lower = band_of(gap_base(0, edge, -LANES))
        for block in range(blocks):
            low, high = block * LANES, (block + 1) * LANES
            table[low:high, low:high] = diagonal
            if block + 1 < blocks:
                table[high - edge : high, high : high + LANES] = upper
                table[high : high + edge, low:high] = lower
        source = pixels[slot].reshape(bands * rows, cols)
        warped = jnp.dot(source, table[...], preferred_element_type=jnp.float32)
        out[slot] = warped.astype(out.dtype).reshape(bands, rows, cols)

    def pair(index, carry):
        for half in range(2):
            one(index * 2 + half, tables.at[half])
        return carry

    lax.fori_loop(0, slots // 2, pair, 0)


def warp_columns(pixels, shifts, taps):
    held, bands, rows, cols = pixels.shape
    return pl.pallas_call(
        column_kernel,
        grid=(held // GROUP,),
        out_shape=jax.ShapeDtypeStruct(pixels.shape, jnp.bfloat16),
        in_specs=[
            pl.BlockSpec(memory_space=pltpu.SMEM),
            pl.BlockSpec(memory_space=pltpu.SMEM),
            pl.BlockSpec((GROUP, bands, rows, cols), lambda g: (g, 0, 0, 0)),
        ],
        out_specs=pl.BlockSpec((GROUP, bands, rows, cols), lambda g: (g, 0, 0, 0)),
        scratch_shapes=[pltpu.VMEM((2, cols, cols), jnp.bfloat16)],
        compiler_params=pltpu.CompilerParams(dimension_semantics=("arbitrary",)),
        cost_estimate=pl.CostEstimate(
            flops=2 * held * bands * rows * cols * cols,
            bytes_accessed=4 * held * bands * rows * cols,
            transcendentals=0,
        ),
        name="columns",
    )(shifts, taps.reshape(-1), pixels)


def clip_kernel(ints, floats, columns, tables, row_cover, plane, template, out, framed, sums):
    step = pl.program_id(0)
    slots, bands, rows, cols = columns.shape
    owners = template.shape[0]
    canvas_rows = row_cover.shape[1]
    quarters = out.shape[0]
    width = cols // quarters

    @pl.when(step == 0)
    def _():
        ends = framed.shape[1]
        for band in range(bands):
            framed[band, 0:MARGIN, :] = jnp.zeros((MARGIN, cols), jnp.float32)
            framed[band, ends - MARGIN : ends, :] = jnp.zeros((MARGIN, cols), jnp.float32)

        def fill(owner, carry):
            start = pl.multiple_of(owner * rows + MARGIN, MARGIN)
            first = pl.multiple_of(owner * rows, rows)
            for band in range(bands):
                framed[band, pl.ds(start, rows), :] = template[owner, band].astype(jnp.float32)
                sums[band, pl.ds(first, rows), :] = jnp.zeros((rows, cols), jnp.float32)
            return carry

        lax.fori_loop(0, owners, fill, 0)
        for band in range(bands):
            tail = jnp.zeros((2 * MARGIN, cols), jnp.float32)
            sums[band, ends - 2 * MARGIN : ends, :] = tail

    def one(slot, carry):
        at = step * slots + slot
        first = pl.multiple_of(ints[at], ROW_BLOCK)
        source = columns[slot].reshape(bands * rows, cols)
        warped = jnp.dot(tables[slot], source, preferred_element_type=jnp.float32)
        for block in range(canvas_rows // ROW_BLOCK):
            low = block * ROW_BLOCK
            cover_rows = row_cover[slot, low : low + ROW_BLOCK, :]
            cover_rows = jnp.concatenate([cover_rows] * (cols // LANES), axis=1)
            weight = cover_rows * plane[slot, block : block + 1, :]
            for band in range(bands):
                where = pl.ds(first + low, ROW_BLOCK)
                base = band * canvas_rows + low
                prior = framed[band, where, :]
                inverse = floats[(at * bands + band) * 3]
                over = floats[(at * bands + band) * 3 + 1]
                ratio = floats[(at * bands + band) * 3 + 2]
                pull = jnp.tanh((warped[base : base + ROW_BLOCK, :] - prior) * inverse)
                sums[band, where, :] += weight * (prior * over + pull * ratio)
        return carry

    lax.fori_loop(0, slots, one, 0)

    @pl.when(step == pl.num_programs(0) - 1)
    def _():
        def give(owner, carry):
            start = pl.multiple_of(owner * rows + MARGIN, MARGIN)
            for band in range(bands):
                value = sums[band, pl.ds(start, rows), :].astype(out.dtype)
                for quarter in range(quarters):
                    part = value[:, quarter * width : (quarter + 1) * width]
                    out[quarter, owner, band] = part
            return carry

        lax.fori_loop(0, owners, give, 0)


def clip_and_sum(starts, scales, columns, tables, row_cover, plane, template, quarters):
    held, bands, rows, cols = columns.shape
    owners = template.shape[0]
    canvas_rows = row_cover.shape[1]
    height = owners * rows + 2 * MARGIN
    out_shape = (quarters, owners, bands, rows, cols // quarters)

    def by_slot(*shape):
        return pl.BlockSpec((GROUP,) + shape, lambda g: (g,) + (0,) * len(shape))

    return pl.pallas_call(
        clip_kernel,
        grid=(held // GROUP,),
        out_shape=jax.ShapeDtypeStruct(out_shape, jnp.bfloat16),
        in_specs=[
            pl.BlockSpec(memory_space=pltpu.SMEM),
            pl.BlockSpec(memory_space=pltpu.SMEM),
            by_slot(bands, rows, cols),
            by_slot(*tables.shape[1:]),
            by_slot(*row_cover.shape[1:]),
            by_slot(*plane.shape[1:]),
            pl.BlockSpec(template.shape, lambda g: (0, 0, 0, 0)),
        ],
        out_specs=pl.BlockSpec(out_shape, lambda g: (0, 0, 0, 0, 0)),
        scratch_shapes=[
            pltpu.VMEM((bands, height, cols), jnp.float32),
            pltpu.VMEM((bands, height, cols), jnp.float32),
        ],
        compiler_params=pltpu.CompilerParams(
            dimension_semantics=("arbitrary",), vmem_limit_bytes=48 * 1024 * 1024
        ),
        cost_estimate=pl.CostEstimate(
            flops=20 * held * bands * canvas_rows * cols,
            bytes_accessed=2 * held * bands * rows * cols,
            transcendentals=held * bands * canvas_rows * cols,
        ),
        name="clip",
    )(starts, scales, columns, tables, row_cover, plane, template)


def row_tables(shifts, taps, bands, rows, canvas_rows):
    shape = (1, bands * canvas_rows, bands * rows)
    i = lax.broadcasted_iota(jnp.int32, shape, 1)
    k = lax.broadcasted_iota(jnp.int32, shape, 2)
    gap = i % canvas_rows - MARGIN - k % rows - shifts[:, None, None]
    value = jnp.zeros(gap.shape, jnp.float32)
    for tap in range(TAPS):
        value = jnp.where(gap == 3 - tap, taps[:, tap][:, None, None], value)
    return jnp.where(i // canvas_rows == k // rows, value, 0.0).astype(jnp.bfloat16)


def spread(index, block_count, block):
    which = jnp.arange(block_count, dtype=jnp.int32)[:, None] == (index // block)[None, :]
    return which.astype(jnp.float32)


def on_device(
    slot_pixels,
    slot_tile,
    slot_offset,
    slot_frac,
    slot_sigma,
    clip_mask,
    slot_count,
    template,
    prior_weight,
):
    sky_count = lax.axis_size("sky")
    epoch_count = lax.axis_size("epoch")
    held, bands, rows, cols = slot_pixels.shape
    canvas_rows = rows + 2 * MARGIN
    row_blocks, col_blocks = clip_mask.shape[1:]
    part_width = cols // epoch_count
    high = lax.Precision.HIGHEST

    whole_template = lax.all_gather(template, "sky", axis=0, tiled=False)

    target = slot_tile[:, 0]
    shift_y, shift_x = slot_offset[:, 0], slot_offset[:, 1]
    taps = tap_weights(slot_frac.astype(jnp.float32))
    taps_y, taps_x = taps[:, 0], taps[:, 1]
    sigmas = slot_sigma.astype(jnp.float32)
    over = 1.0 / (sigmas * sigmas)
    live = (jnp.arange(held, dtype=jnp.int32) < slot_count[0]).astype(jnp.float32)
    masks = clip_mask.astype(jnp.float32) * live[:, None, None]

    columns = warp_columns(slot_pixels, shift_x, taps_x)

    row_index = jnp.arange(canvas_rows, dtype=jnp.int32) - MARGIN
    col_index = jnp.arange(cols, dtype=jnp.int32)
    row_cover = cover(shift_y, taps_y, row_index, rows)
    col_cover = cover(shift_x, taps_x, col_index, cols)
    expand = spread(col_index, col_blocks, cols // col_blocks)
    plane = jnp.einsum("sik,kj->sij", masks, expand, precision=high) * col_cover[:, None, :]
    tables = row_tables(shift_y, taps_y, bands, rows, canvas_rows)
    wide_cover = jnp.broadcast_to(row_cover[:, :, None], (held, canvas_rows, LANES))
    scale = CLIP_WIDTH * sigmas
    scales = jnp.stack([1.0 / scale, over, scale * over], 2).reshape(-1)

    block_rows = row_cover.reshape(held, row_blocks, canvas_rows // row_blocks).sum(2)
    block_cols = col_cover.reshape(held, col_blocks, cols // col_blocks).sum(2)
    block = jnp.arange(row_blocks, dtype=jnp.int32)[None, :]
    above = (target[:, None] == 0) & (block == 0)
    below = (target[:, None] == sky_count - 1) & (block == row_blocks - 1)
    block_rows = jnp.where(above | below, 0.0, block_rows)
    tile_total = jnp.sum(masks * block_rows[:, :, None] * block_cols[:, None, :], (1, 2))
    band_part = jnp.sum(tile_total[:, None] * over, 0)
    band_part = band_part + jnp.sum(prior_weight, 1) * (cols / epoch_count)

    owners = jnp.arange(sky_count, dtype=jnp.int32)
    onehot = (target[:, None] == owners[None, :]).astype(jnp.int32)
    rank = jnp.sum(jnp.cumsum(onehot, 0) * onehot, 1) - 1
    position = target * CAPACITY + rank
    routes = jnp.arange(sky_count * CAPACITY, dtype=jnp.int32)
    chooser = (position[None, :] == routes[:, None]).astype(jnp.float32)
    cells = row_blocks * col_blocks
    described = jnp.concatenate(
        [
            masks.reshape(held, cells),
            slot_offset.astype(jnp.float32),
            slot_frac.astype(jnp.float32),
            sigmas,
        ],
        1,
    )
    chosen = jnp.dot(chooser, described, precision=high)
    totals = jnp.broadcast_to(band_part[None, :], (chosen.shape[0], bands))
    message = jnp.concatenate([chosen, totals], 1)
    message = jnp.pad(message, ((0, 0), (0, LANES - message.shape[1])))
    message = message.reshape(sky_count, CAPACITY, LANES)
    arrived = lax.all_to_all(message, "sky", split_axis=0, concat_axis=0, tiled=True)
    arrived = lax.all_gather(arrived, "epoch", axis=0, tiled=True)
    band_total = jnp.sum(arrived[:, 0, cells + 4 + bands : cells + 4 + 2 * bands], 0)
    arrived = arrived.reshape(-1, LANES)

    epoch_position = lax.axis_index("epoch")
    own_masks = arrived[:, :cells].reshape(-1, row_blocks, col_blocks)
    own_shift = arrived[:, cells : cells + 2].astype(jnp.int32)
    own_taps = tap_weights(arrived[:, cells + 2 : cells + 4])
    own_sigmas = arrived[:, cells + 4 : cells + 4 + bands]
    own_sigmas = jnp.where(own_sigmas > 0.0, own_sigmas, 1.0)
    own_over = 1.0 / (own_sigmas * own_sigmas)
    own_index = epoch_position * part_width + jnp.arange(part_width, dtype=jnp.int32)
    own_rows = cover(own_shift[:, 0], own_taps[:, 0], row_index, rows)
    own_cols = cover(own_shift[:, 1], own_taps[:, 1], own_index, cols)
    own_expand = spread(own_index, col_blocks, cols // col_blocks)
    own_plane = jnp.einsum("sik,kj->isj", own_masks, own_expand, precision=high)
    own_plane = own_plane * own_cols[None]
    left = own_over[:, :, None, None] * own_rows.reshape(-1, 1, row_blocks, ROW_BLOCK)
    weights = jnp.einsum("sbir,isj->birj", left, own_plane, precision=high)
    weights = weights.reshape(bands, canvas_rows, part_width)
    ring = [(i, i + 1) for i in range(sky_count - 1)]
    from_above = lax.ppermute(weights[:, canvas_rows - MARGIN :], "sky", ring)
    from_below = lax.ppermute(weights[:, :MARGIN], "sky", [(j, i) for i, j in ring])
    weight_sum = weights[:, MARGIN : MARGIN + rows]
    weight_sum = weight_sum.at[:, :MARGIN].add(from_above)
    weight_sum = weight_sum.at[:, rows - MARGIN :].add(from_below)

    partial = clip_and_sum(
        target * rows, scales, columns, tables, wide_cover, plane, whole_template, epoch_count
    )
    flux = lax.psum_scatter(partial, "epoch", scatter_dimension=0, tiled=False)
    flux = lax.psum_scatter(flux, "sky", scatter_dimension=0, tiled=False)
    flux_sum = flux.astype(jnp.float32)

    template_part = lax.dynamic_slice_in_dim(
        template, epoch_position * part_width, part_width, 2
    ).astype(jnp.float32)
    prior = prior_weight[:, :, None]
    depth_map = weight_sum + prior
    coadd_image = ((flux_sum + prior * template_part) / depth_map).astype(jnp.bfloat16)
    band_mean = band_total / (rows * sky_count * cols)
    depth_norm = (depth_map / band_mean[:, None, None]).astype(jnp.bfloat16)
    return (coadd_image, depth_norm)


def solution(mesh):
    in_specs = (
        P(("groups", "sky", "epoch"), "band", None, None),
        P(("groups", "sky", "epoch"), None),
        P(("groups", "sky", "epoch"), None),
        P(("groups", "sky", "epoch"), None),
        P(("groups", "sky", "epoch"), "band"),
        P(("groups", "sky", "epoch"), None, None),
        P(("groups", "sky", "epoch")),
        P("band", ("groups", "sky"), None),
        P("band", ("groups", "sky")),
    )
    out_specs = (P("band", ("groups", "sky"), "epoch"), P("band", ("groups", "sky"), "epoch"))
    return jax.shard_map(
        on_device, mesh=mesh, in_specs=in_specs, out_specs=out_specs, check_vma=False
    )
```

time: 1010 us -> 382 us (0.38)
  waiting for transfers between devices: 585 us -> 290 us
  matrix products: 184 us -> 1.98 us
  starting transfers between devices: 87.5 us -> 17.3 us
  blocking collectives: 76 us -> 12.5 us
  local copies, waits for them, and re-layouts: 42.7 us -> 5.38 us
  Pallas kernels: 0 us -> 27.1 us
  other arithmetic: 32.6 us -> 11.9 us
  between operations: 1.57 us -> 14.8 us
    ppermute x4 -> x2, waiting for transfers between devices: 535 us -> 4.28 us  [the longest x1 4.28 us: on_device(): lax.ppermute(weights[:, :MARGIN], 'sky', [(j, i) for i, j in ring])]
    dot_general x8 -> x4, matrix products: 184 us -> 1.98 us  [the longest x1 0.79 us: on_device(): weights = jnp.einsum('sbir,isj->birj', left, own_plane, precision=high)]
    all_gather x0 -> x1, waiting for transfers between devices: none -> 142 us  [on_device(): whole_template = lax.all_gather(template, 'sky', axis=0, tiled=False)]
    reduce_scatter x0 -> x2, waiting for transfers between devices: none -> 121 us  [the longest x1 121 us: on_device(): flux = lax.psum_scatter(flux, 'sky', scatter_dimension=0, tiled=False)]
    psum x2 -> x0, blocking collectives: 64.7 us -> none  [one_axis_at_a_time(): return functools.reduce(lax.psum, axes, shard)]
    all_to_all x4 -> x1, starting transfers between devices: 65.3 us -> 13.3 us  [on_device(): lax.all_to_all(message, 'sky', split_axis=0, concat_axis=0, tiled=True)]
    all_to_all x4 -> x1, waiting for transfers between devices: 50.4 us -> 22.3 us  [on_device(): lax.all_to_all(message, 'sky', split_axis=0, concat_axis=0, tiled=True)]
    pallas_call x0 -> x2, Pallas kernels: none -> 27.1 us  [the longest x1 16.8 us: clip_and_sum(): pl.pallas_call(clip_kernel, grid=(held // GROUP,), out_shape=jax.ShapeDty...]
  transfers between devices with their start and end apart: 8 -> 6, of which waited for: 7 -> 4; matrix products, arithmetic and copies ran while one was open for 2% -> 4% of each run, Pallas kernels for 0% -> 3%
where the time goes in v1:
time: 382 us; the launch traced here: 381 us
  waiting for transfers between devices  290 us (76%)
  Pallas kernels  27.1 us (7%)
  starting transfers between devices  17.3 us (5%)
  between operations  14.8 us (4%)
  blocking collectives  12.5 us (3%)
  other arithmetic  11.9 us (3%)
  local copies, waits for them, and re-layouts  5.38 us (1%)
    all_gather x1, waiting for transfers between devices, on_device(): whole_template = lax.all_gather(template, 'sky', axis=0, tiled=False)  142 us
    reduce_scatter x1, waiting for transfers between devices, on_device(): flux = lax.psum_scatter(flux, 'sky', scatter_dimension=0, tiled=False)  121 us
    all_to_all x1, waiting for transfers between devices, on_device(): lax.all_to_all(message, 'sky', split_axis=0, concat_axis=0, tiled=True)  22.3 us
    pallas_call x1, Pallas kernels, clip_and_sum(): pl.pallas_call(clip_kernel, grid=(held // GROUP,), out_shape=jax.ShapeDty...  16.8 us
    all_to_all x1, starting transfers between devices, on_device(): lax.all_to_all(message, 'sky', split_axis=0, concat_axis=0, tiled=True)  13.3 us
    all_gather x1, blocking collectives, on_device(): arrived = lax.all_gather(arrived, 'epoch', axis=0, tiled=True)  12.5 us
    pallas_call x1, Pallas kernels, warp_columns(): pl.pallas_call(column_kernel, grid=(held // GROUP,), out_shape=jax.ShapeD...  10.3 us
  transfers between devices with their start and end apart: 6, of which 4 were waited for; matrix products, arithmetic and copies ran while one was open for 4% of the time, Pallas kernels for 3%

profile of v1, /device:TPU:40, one launch (start us, length us, event | category | flops | bytes accessed | tf_op | source)
XLA Modules:
  0.0 381.0 jit_solution(4314064924760879850)
XLA Ops:
  7.2 0.7 all-gather.3.cloned.1.call-update
  8.1 0.7 convert_element_type.68
  9.5 0.8 copy.65
  10.4 0.7 reshape_squeeze.3.floats
  11.1 0.8 slice_bitcast_fusion.15
  12.0 0.4 clamp_reduce_fusion
  12.4 0.7 compare_bitcast_fusion.1
  13.1 0.8 multiply_reduce_fusion
  14.1 0.4 copy.66
  14.7 0.7 fusion.122
  15.6 0.8 select_reduce_fusion
  16.4 0.7 broadcast_multiply_fusion.1
  17.5 10.3 %columns.1 = bf16[48,3,32,512]{3,2,1,0:T(8,128)(2,1)} custom-call(s32[48]{0:T(128)} %copy-done.1, f32[288]{0:T(512)} %reshape_squeeze.3.floats, bf16[48,3,32,512]{3,2,1,0:T(8,128)(2,1)} %pixels.1), custom_call_target="tpu_custom_call" | custom-call | flops 2415919104 | bytes 9437184 | tf_op jit(solution)/shard_map/columns/pallas_call | solution.py:89
  27.8 0.8 add_clamp_fusion.1
  28.6 0.4 fusion.109
  29.1 0.4 copy_multiply_fusion.plane
  29.4 2.4 select_convert_fusion.tables
  31.9 141.7 %all-gather.3.cloned.1.call-done = bf16[96,32,512]{2,1,0:T(8,128)(2,1)} async-done(((bf16[3,32,512]{2,1,0:T(8,128)(2,1)}), bf16[96,32,512]{2,1,0:T(8,128)(2,1)}) %all-gather.3.cloned.1.call-update) | async-done | bytes 3145744 | tf_op jit(solution)/shard_map/all_gather | solution.py:250
  173.5 0.4 broadcast_in_dim.364.row_cover
  173.9 16.8 %clip.1 = bf16[4,32,3,32,128]{4,3,2,1,0:T(8,128)(2,1)} custom-call(s32[48]{0:T(128)S(1)} %get-tuple-element.72.ints, f32[432]{0:T(512)S(1)} %reshape.1003.floats, bf16[48,3,32,512]{3,2,1,0:T(8,128)(2,1)} %columns.1, bf16[48,144,96]{2,1,0:T(8,128)(2,1)S(1)} %select_convert_fusion.tables, f32[48,48,128]{2,1,0:T(8,128)S(1)} %broadcast_in_dim.364.row_cover, ...), custom_call_target="tpu_custom_call" | custom-call | flops 70778880 | bytes 4718592 | tf_op jit(solution)/shard_map/clip/pallas_call | solution.py:185
  190.8 0.6 copy-done.2
  192.1 0.6 pad.8
  192.7 13.3 %all-to-all-start = ((f32[32,2,128]{2,1,0:T(2,128)}), f32[32,2,128]{2,1,0:T(2,128)S(1)}, u32[]{:S(2)}, u32[]{:S(2)}) async-start(f32[32,2,128]{2,1,0:T(2,128)} %bitcast.29), calls=%async_computation.2 | async-start | bytes 65536 | tf_op jit(solution)/shard_map/all_to_all | solution.py:305
  206.2 22.3 %all-to-all-done = f32[32,2,128]{2,1,0:T(2,128)S(1)} async-done(((f32[32,2,128]{2,1,0:T(2,128)}), f32[32,2,128]{2,1,0:T(2,128)S(1)}, u32[]{:S(2)}, u32[]{:S(2)}) %all-to-all-start) | async-done | bytes 32800 | tf_op jit(solution)/shard_map/all_to_all | solution.py:305
  228.5 12.5 %all_gather.11 = f32[128,2,128]{2,1,0:T(2,128)S(1)} all-gather(f32[32,2,128]{2,1,0:T(2,128)S(1)} %all-to-all-done), channel_id=1, replica_groups=mesh['groups'=2,'sky'=32,'epoch'=4,'band'=2] {'epoch'}, dimensions={0}, use_global_device_ids=true | all-gather | bytes 163840 | tf_op jit(solution)/shard_map/all_gather | solution.py:306
  242.2 0.5 fusion.1
  242.9 0.8 convolution_bitcast_fusion.1
  243.7 2.5 collective-permute-start
  246.5 1.3 collective-permute-start.1
  247.8 4.3 %collective-permute-done.1 = f32[3,8,128]{2,1,0:T(8,128)S(1)} collective-permute-done((f32[3,8,128]{2,1,0:T(8,128)S(1)}, f32[3,8,128]{2,1,0:T(8,128)S(1)}, u32[]{:S(2)}, u32[]{:S(2)}) %collective-permute-start.1) | collective-permute-done | bytes 12320 | tf_op jit(solution)/shard_map/ppermute | solution.py:328
  252.1 120.9 %reduce-scatter.5.cloned.1.call-done = bf16[1,3,32,128]{3,2,1,0:T(8,128)(2,1)} async-done(((bf16[32,3,32,128]{3,2,1,0:T(8,128)(2,1)}), bf16[1,3,32,128]{3,2,1,0:T(8,128)(2,1)}) %reduce-scatter.5.cloned.1.call-update) | async-done | bytes 24592 | tf_op jit(solution)/shard_map/reduce_scatter | solution.py:337
  373.0 1.5 divide_convert_fusion
  (74 shorter events, 3.7 us)
Async XLA Ops:
  7.2 166.4 %all-gather.3.cloned.1.call-start = ((), (), s32[]{:S(2)}) async-start(), calls=%async_computation.5 | async-start | bytes 3244032 | tf_op jit(solution)/shard_map/all_gather | solution.py:250
  8.0 234.2 %reduce-scatter.3.cloned.1.call-start = ((), (), s32[]{:S(2)}) async-start(), calls=%async_computation.3 | async-start | bytes 3932160 | tf_op jit(solution)/shard_map/reduce_scatter | solution.py:336
  11.9 5.6 %copy-start.1 = (s32[48]{0:T(128)}, s32[48]{0:T(128)S(1)}, u32[]{:S(2)}) copy-start(s32[48]{0:T(128)S(1)} %get-tuple-element.71.ints) | copy-start | bytes 580
  190.7 0.7 copy-start.2
  190.7 0.7 copy-start.3
  190.7 0.9 copy-start
  192.7 35.8 %all-to-all-start = ((f32[32,2,128]{2,1,0:T(2,128)}), f32[32,2,128]{2,1,0:T(2,128)S(1)}, u32[]{:S(2)}, u32[]{:S(2)}) async-start(f32[32,2,128]{2,1,0:T(2,128)} %bitcast.29), calls=%async_computation.2 | async-start | bytes 65536 | tf_op jit(solution)/shard_map/all_to_all | solution.py:305
  206.1 167.0 %reduce-scatter.5.cloned.1.call-start = ((), (), s32[]{:S(2)}) async-start(), calls=%async_computation.4 | async-start | bytes 811008 | tf_op jit(solution)/shard_map/reduce_scatter | solution.py:337
  243.7 4.1 %collective-permute-start = (f32[3,8,128]{2,1,0:T(8,128)S(1)}, f32[3,8,128]{2,1,0:T(8,128)S(1)}, u32[]{:S(2)}, u32[]{:S(2)}) collective-permute-start(f32[3,8,128]{2,1,0:T(8,128)S(1)} %get-tuple-element.35), channel_id=1, source_target_pairs={{0,8},{8,16},{16,24},{24,32},{32,40},{40,48},{48,56},{56,64},{64,7... | collective-permute-start | bytes 36872 | tf_op jit(solution)/shard_map/ppermute | solution.py:327
  246.5 5.6 %collective-permute-start.1 = (f32[3,8,128]{2,1,0:T(8,128)S(1)}, f32[3,8,128]{2,1,0:T(8,128)S(1)}, u32[]{:S(2)}, u32[]{:S(2)}) collective-permute-start(f32[3,8,128]{2,1,0:T(8,128)S(1)} %get-tuple-element.34), channel_id=1, source_target_pairs={{8,0},{16,8},{24,16},{32,24},{40,32},{48,40},{56,48},{64,56},{72,6... | collective-permute-start | bytes 36872 | tf_op jit(solution)/shard_map/ppermute | solution.py:328
Sparse Core Ops, SparseCore 0:
  10.1 163.3 all-gather.2
  190.9 45.8 reduce-scatter.2
  242.3 130.6 reduce-scatter.4

commit v2 on v1

v2 whole, which is shorter than its diff:
```python
import functools

import jax
import jax.numpy as jnp
from jax import lax
from jax.experimental import pallas as pl
from jax.experimental.pallas import tpu as pltpu
from jax.sharding import PartitionSpec as P


MARGIN = 8
CAPACITY = 2
CLIP_WIDTH = 3.0
TAPS = 6
ROW_BLOCK = 8
LANES = 128
GROUP = 8
CLIP_GROUP = 48
UNROLL = 4
NEAR = 4


def lanczos(distance):
    inside = jnp.abs(distance) < 3.0
    return jnp.where(inside, jnp.sinc(distance) * jnp.sinc(distance / 3.0), 0.0)


def tap_weights(fractions):
    gaps = 3.0 - jnp.arange(TAPS, dtype=jnp.float32)
    rounded = lanczos(gaps - fractions[..., None]).astype(jnp.bfloat16)
    return lax.optimization_barrier(rounded).astype(jnp.float32)


def cover(shifts, taps, index, length_in):
    total = jnp.zeros((shifts.shape[0], index.shape[0]), jnp.float32)
    for tap in range(TAPS):
        source = index[None, :] - shifts[:, None] + (tap - 3)
        inside = (source >= 0) & (source < length_in)
        total = total + jnp.where(inside, taps[:, tap][:, None], 0.0)
    return jnp.clip(total, 0.0, 1.0)


def column_kernel(ints, floats, after, pixels, out, tables):
    step = pl.program_id(0)
    slots, bands, rows, cols = pixels.shape
    blocks = cols // LANES
    edge = 16
    parts = out.shape[0]
    width = cols // parts

    @pl.when(step == 0)
    def _():
        tables[...] = jnp.zeros_like(tables)

    def gap_base(first_row, count, offset):
        k = lax.broadcasted_iota(jnp.int32, (count, LANES), 0) + first_row
        j = lax.broadcasted_iota(jnp.int32, (count, LANES), 1)
        return j - k + offset

    def one(slot, table):
        at = step * slots + slot
        shift = ints[at]
        weights = [floats[at * TAPS + tap] for tap in range(TAPS)]

        def band_of(base):
            gap = base - shift
            value = jnp.zeros(base.shape, jnp.float32)
            for tap in range(TAPS):
                value = jnp.where(gap == 3 - tap, weights[tap], value)
            return value.astype(jnp.bfloat16)

        diagonal = band_of(gap_base(0, LANES, 0))
        upper = band_of(gap_base(LANES - edge, edge, LANES))
        lower = band_of(gap_base(0, edge, -LANES))
        for block in range(blocks):
            low, high = block * LANES, (block + 1) * LANES
            table[low:high, low:high] = diagonal
            if block + 1 < blocks:
                table[high - edge : high, high : high + LANES] = upper
                table[high : high + edge, low:high] = lower
        source = pixels[slot].reshape(bands * rows, cols)
        warped = jnp.dot(source, table[...], preferred_element_type=jnp.float32)
        warped = warped.astype(out.dtype)
        for part in range(parts):
            for band in range(bands):
                piece = warped[band * rows : (band + 1) * rows, part * width : (part + 1) * width]
                out[part, slot, :, band * width : (band + 1) * width] = piece

    def pair(index, carry):
        for half in range(2):
            one(index * 2 + half, tables.at[half])
        return carry

    lax.fori_loop(0, slots // 2, pair, 0)


def warp_columns(pixels, shifts, taps, after, parts):
    held, bands, rows, cols = pixels.shape
    width = bands * cols // parts
    return pl.pallas_call(
        column_kernel,
        grid=(held // GROUP,),
        out_shape=jax.ShapeDtypeStruct((parts, held, rows, width), jnp.bfloat16),
        in_specs=[
            pl.BlockSpec(memory_space=pltpu.SMEM),
            pl.BlockSpec(memory_space=pltpu.SMEM),
            pl.BlockSpec(memory_space=pl.ANY),
            pl.BlockSpec((GROUP, bands, rows, cols), lambda g: (g, 0, 0, 0)),
        ],
        out_specs=pl.BlockSpec((parts, GROUP, rows, width), lambda g: (0, g, 0, 0)),
        scratch_shapes=[pltpu.VMEM((2, cols, cols), jnp.bfloat16)],
        compiler_params=pltpu.CompilerParams(dimension_semantics=("arbitrary",)),
        cost_estimate=pl.CostEstimate(
            flops=2 * held * bands * rows * cols * cols,
            bytes_accessed=4 * held * bands * rows * cols,
            transcendentals=0,
        ),
        name="columns",
    )(shifts, taps.reshape(-1), after, pixels)


def clip_kernel(ints, floats, columns, plane, template, out, framed, sums):
    step = pl.program_id(0)
    slots, rows, width = columns.shape
    owners = out.shape[0]
    bands = width // LANES
    canvas_rows = rows + 2 * MARGIN
    total = pl.num_programs(0) * slots

    @pl.when(step == 0)
    def _():
        ends = framed.shape[0]
        framed[0:MARGIN, :] = jnp.zeros((MARGIN, width), jnp.float32)
        framed[ends - MARGIN : ends, :] = jnp.zeros((MARGIN, width), jnp.float32)

        def fill(owner, carry):
            start = pl.multiple_of(owner * rows + MARGIN, MARGIN)
            first = pl.multiple_of(owner * rows, rows)
            framed[pl.ds(start, rows), :] = template[owner, 0:rows, :].astype(jnp.float32)
            sums[pl.ds(first, rows), :] = jnp.zeros((rows, width), jnp.float32)
            return carry

        lax.fori_loop(0, owners, fill, 0)
        sums[ends - 2 * MARGIN : ends, :] = jnp.zeros((2 * MARGIN, width), jnp.float32)

    i = lax.broadcasted_iota(jnp.int32, (canvas_rows, LANES), 0)
    k = lax.broadcasted_iota(jnp.int32, (canvas_rows, LANES), 1)
    base = i - MARGIN - k
    ones = jnp.ones((rows, LANES), columns.dtype)

    def one(slot):
        at = step * slots + slot
        first = pl.multiple_of(ints[at], ROW_BLOCK)
        gap = base - ints[total + at]
        table = jnp.zeros(gap.shape, jnp.float32)
        per_slot = TAPS + 3 * bands
        for tap in range(TAPS):
            table = jnp.where(gap == 3 - tap, floats[at * per_slot + tap], table)
        table = table.astype(columns.dtype)[:, :rows]
        source = jnp.concatenate([columns[slot], ones], axis=1)
        warped = jnp.dot(table, source, preferred_element_type=jnp.float32)
        for block in range(canvas_rows // ROW_BLOCK):
            low = block * ROW_BLOCK
            where = pl.ds(first + low, ROW_BLOCK)
            row_cover = jnp.clip(warped[low : low + ROW_BLOCK, width:], 0.0, 1.0)
            weight = row_cover * plane[slot, block : block + 1, :]
            for band in range(bands):
                lanes = slice(band * LANES, (band + 1) * LANES)
                prior = framed[where, lanes]
                scale = at * per_slot + TAPS + 3 * band
                pull = (warped[low : low + ROW_BLOCK, lanes] - prior) * floats[scale]
                value = prior * floats[scale + 1] + jnp.tanh(pull) * floats[scale + 2]
                sums[where, lanes] += weight * value

    def several(index, carry):
        for part in range(UNROLL):
            one(index * UNROLL + part)
        return carry

    lax.fori_loop(0, slots // UNROLL, several, 0)

    @pl.when(step == pl.num_programs(0) - 1)
    def _():
        def give(owner, carry):
            start = pl.multiple_of(owner * rows + MARGIN, MARGIN)
            out[owner] = sums[pl.ds(start, rows), :].astype(out.dtype)
            return carry

        lax.fori_loop(0, owners, give, 0)


def clip_and_sum(ints, floats, columns, plane, template):
    tiles, rows, width = columns.shape
    owners = template.shape[0]
    height = owners * rows + 2 * MARGIN
    out_shape = (owners, rows, width)
    return pl.pallas_call(
        clip_kernel,
        grid=(tiles // CLIP_GROUP,),
        out_shape=jax.ShapeDtypeStruct(out_shape, jnp.bfloat16),
        in_specs=[
            pl.BlockSpec(memory_space=pltpu.SMEM),
            pl.BlockSpec(memory_space=pltpu.SMEM),
            pl.BlockSpec((CLIP_GROUP, rows, width), lambda g: (g, 0, 0)),
            pl.BlockSpec((CLIP_GROUP,) + plane.shape[1:], lambda g: (g, 0, 0)),
            pl.BlockSpec(template.shape, lambda g: (0, 0, 0)),
        ],
        out_specs=pl.BlockSpec(out_shape, lambda g: (0, 0, 0)),
        scratch_shapes=[
            pltpu.VMEM((height, width), jnp.float32),
            pltpu.VMEM((height, width), jnp.float32),
        ],
        compiler_params=pltpu.CompilerParams(
            dimension_semantics=("arbitrary",), vmem_limit_bytes=32 * 1024 * 1024
        ),
        cost_estimate=pl.CostEstimate(
            flops=30 * tiles * (rows + 2 * MARGIN) * width,
            bytes_accessed=2 * tiles * rows * width,
            transcendentals=tiles * (rows + 2 * MARGIN) * width,
        ),
        name="clip",
    )(ints, floats, columns, plane, template)


def spread(index, block_count, block):
    which = jnp.arange(block_count, dtype=jnp.int32)[:, None] == (index // block)[None, :]
    return which.astype(jnp.float32)


def summed_on_arrival(parts, axis, groups=None):
    arrived = lax.all_to_all(
        parts, axis, split_axis=0, concat_axis=0, tiled=True, axis_index_groups=groups
    )
    return functools.reduce(jnp.add, [part.astype(jnp.float32) for part in arrived])


def sum_over_sky(parts):
    count = parts.shape[0]
    if NEAR == 1 or count % NEAR:
        return summed_on_arrival(parts, "sky")
    far = count // NEAR
    near_groups = [[f * NEAR + n for n in range(NEAR)] for f in range(far)]
    far_groups = [[f * NEAR + n for f in range(far)] for n in range(NEAR)]
    parts = jnp.swapaxes(parts.reshape((far, NEAR) + parts.shape[1:]), 0, 1)
    parts = summed_on_arrival(parts, "sky", near_groups).astype(jnp.bfloat16)
    return summed_on_arrival(parts, "sky", far_groups)


def on_device(
    slot_pixels,
    slot_tile,
    slot_offset,
    slot_frac,
    slot_sigma,
    clip_mask,
    slot_count,
    template,
    prior_weight,
):
    sky_count = lax.axis_size("sky")
    epoch_count = lax.axis_size("epoch")
    epoch_position = lax.axis_index("epoch")
    held, bands, rows, cols = slot_pixels.shape
    canvas_rows = rows + 2 * MARGIN
    row_blocks, col_blocks = clip_mask.shape[1:]
    cells = row_blocks * col_blocks
    part_width = cols // epoch_count
    high = lax.Precision.HIGHEST

    template_part = lax.dynamic_slice_in_dim(
        template, epoch_position * part_width, part_width, 2
    )
    sent = jnp.swapaxes(template_part, 0, 1).reshape(rows, bands * part_width)
    sent = jnp.pad(sent, ((0, rows // 2), (0, 0)))
    whole_template = lax.all_gather(sent, "sky", axis=0, tiled=False)

    taps_x = tap_weights(slot_frac[:, 1].astype(jnp.float32))
    columns = warp_columns(slot_pixels, slot_offset[:, 1], taps_x, sent, epoch_count)
    columns = lax.all_to_all(columns, "epoch", split_axis=0, concat_axis=0, tiled=True)
    columns = columns.reshape((-1,) + columns.shape[2:])

    live = (jnp.arange(held, dtype=jnp.int32) < slot_count[0]).astype(jnp.float32)
    described = jnp.concatenate(
        [
            clip_mask.astype(jnp.float32).reshape(held, cells) * live[:, None],
            slot_offset.astype(jnp.float32),
            slot_frac.astype(jnp.float32),
            slot_sigma.astype(jnp.float32),
            slot_tile.astype(jnp.float32),
        ],
        1,
    )
    described = jnp.pad(described, ((0, 0), (0, LANES - described.shape[1])))
    described = lax.all_gather(described, "epoch", axis=0, tiled=True)
    tiles = described.shape[0]

    def unpack(table):
        masks = table[:, :cells].reshape(-1, row_blocks, col_blocks)
        shifts = table[:, cells : cells + 2].astype(jnp.int32)
        taps = tap_weights(table[:, cells + 2 : cells + 4])
        sigmas = table[:, cells + 4 : cells + 4 + bands]
        sigmas = jnp.where(sigmas > 0.0, sigmas, 1.0)
        return masks, shifts, taps, sigmas

    row_index = jnp.arange(canvas_rows, dtype=jnp.int32) - MARGIN
    col_index = epoch_position * part_width + jnp.arange(part_width, dtype=jnp.int32)
    all_index = jnp.arange(cols, dtype=jnp.int32)
    expand = spread(col_index, col_blocks, cols // col_blocks)

    masks, shifts, taps, sigmas = unpack(described)
    target = described[:, cells + 4 + bands].astype(jnp.int32)
    over = 1.0 / (sigmas * sigmas)
    row_cover = cover(shifts[:, 0], taps[:, 0], row_index, rows)
    col_cover = cover(shifts[:, 1], taps[:, 1], all_index, cols)
    own_cover = lax.dynamic_slice_in_dim(col_cover, epoch_position * part_width, part_width, 1)
    plane = jnp.einsum("sik,kj->sij", masks, expand, precision=high) * own_cover[:, None, :]
    scale = CLIP_WIDTH * sigmas
    scales = jnp.stack([1.0 / scale, over, scale * over], 2).reshape(tiles, 3 * bands)
    floats = jnp.concatenate([taps[:, 0], scales], 1).reshape(-1)
    ints = jnp.concatenate([target * rows, shifts[:, 0]])

    block_rows = row_cover.reshape(tiles, row_blocks, canvas_rows // row_blocks).sum(2)
    block_cols = col_cover.reshape(tiles, col_blocks, cols // col_blocks).sum(2)
    block = jnp.arange(row_blocks, dtype=jnp.int32)[None, :]
    above = (target[:, None] == 0) & (block == 0)
    below = (target[:, None] == sky_count - 1) & (block == row_blocks - 1)
    block_rows = jnp.where(above | below, 0.0, block_rows)
    tile_total = jnp.sum(masks * block_rows[:, :, None] * block_cols[:, None, :], (1, 2))
    band_part = jnp.sum(tile_total[:, None] * over, 0) + jnp.sum(prior_weight, 1) * cols

    owners = jnp.arange(sky_count, dtype=jnp.int32)
    onehot = (target[:, None] == owners[None, :]).astype(jnp.int32)
    onehot = onehot.reshape(epoch_count, held, sky_count)
    rank = jnp.sum(jnp.cumsum(onehot, 1) * onehot, 2) - 1
    rank = rank + CAPACITY * jnp.arange(epoch_count, dtype=jnp.int32)[:, None]
    routes = CAPACITY * epoch_count
    position = target * routes + rank.reshape(-1)
    slots = jnp.arange(sky_count * routes, dtype=jnp.int32)
    chooser = (position[None, :] == slots[:, None]).astype(jnp.float32)
    chosen = jnp.dot(chooser, described[:, : cells + 4 + bands], precision=high)
    totals = jnp.broadcast_to(band_part[None, :], (chosen.shape[0], bands))
    message = jnp.concatenate([chosen, totals], 1)
    message = jnp.pad(message, ((0, 0), (0, LANES - message.shape[1])))
    message = message.reshape(sky_count, routes, LANES)
    arrived = lax.all_to_all(message, "sky", split_axis=0, concat_axis=0, tiled=True)
    band_total = jnp.sum(arrived[:, 0, cells + 4 + bands : cells + 4 + 2 * bands], 0)

    own_masks, own_shift, own_taps, own_sigmas = unpack(arrived.reshape(-1, LANES))
    own_over = 1.0 / (own_sigmas * own_sigmas)
    own_rows = cover(own_shift[:, 0], own_taps[:, 0], row_index, rows)
    own_cols = cover(own_shift[:, 1], own_taps[:, 1], col_index, cols)
    own_plane = jnp.einsum("sik,kj->isj", own_masks, expand, precision=high) * own_cols[None]
    left = own_over[:, :, None, None] * own_rows.reshape(-1, 1, row_blocks, ROW_BLOCK)
    weights = jnp.einsum("sbir,isj->birj", left, own_plane, precision=high)
    weights = weights.reshape(bands, canvas_rows, part_width)
    ring = [(i, i + 1) for i in range(sky_count - 1)]
    from_above = lax.ppermute(weights[:, canvas_rows - MARGIN :], "sky", ring)
    from_below = lax.ppermute(weights[:, :MARGIN], "sky", [(j, i) for i, j in ring])
    weight_sum = weights[:, MARGIN : MARGIN + rows]
    weight_sum = weight_sum.at[:, :MARGIN].add(from_above)
    weight_sum = weight_sum.at[:, rows - MARGIN :].add(from_below)

    flux = sum_over_sky(clip_and_sum(ints, floats, columns, plane, whole_template))
    flux_sum = jnp.swapaxes(flux.reshape(rows, bands, part_width), 0, 1)

    prior = prior_weight[:, :, None]
    depth_map = weight_sum + prior
    coadd_image = (flux_sum + prior * template_part.astype(jnp.float32)) / depth_map
    band_mean = band_total / (rows * sky_count * cols)
    depth_norm = (depth_map / band_mean[:, None, None]).astype(jnp.bfloat16)
    return (coadd_image.astype(jnp.bfloat16), depth_norm)


def solution(mesh):
    in_specs = (
        P(("groups", "sky", "epoch"), "band", None, None),
        P(("groups", "sky", "epoch"), None),
        P(("groups", "sky", "epoch"), None),
        P(("groups", "sky", "epoch"), None),
        P(("groups", "sky", "epoch"), "band"),
        P(("groups", "sky", "epoch"), None, None),
        P(("groups", "sky", "epoch")),
        P("band", ("groups", "sky"), None),
        P("band", ("groups", "sky")),
    )
    out_specs = (P("band", ("groups", "sky"), "epoch"), P("band", ("groups", "sky"), "epoch"))
    return jax.shard_map(
        on_device, mesh=mesh, in_specs=in_specs, out_specs=out_specs, check_vma=False
    )
```

time: 382 us -> 264 us (0.69)
  the two profiles are of different devices: /device:TPU:40 before, /device:TPU:34 now
where the time goes in v2:
time: 264 us
  starting transfers between devices  92.2 us (35%)
  waiting for transfers between devices  76.2 us (29%)
  blocking collectives  33.1 us (13%)
  Pallas kernels  28 us (11%)
  between operations  15.2 us (6%)
  local copies, waits for them, and re-layouts  9.93 us (4%)
  other arithmetic  6.57 us (2%)
    all_to_all x1, starting transfers between devices, on_device(): lax.all_to_all(columns, 'epoch', split_axis=0, concat_axis=0, tiled=True)  45.4 us
    all_to_all x2, waiting for transfers between devices, summed_on_arrival(): lax.all_to_all(parts, axis, split_axis=0, concat_axis=0, tiled=True, axis...  37.9 us
    all_gather x1, waiting for transfers between devices, on_device(): whole_template = lax.all_gather(sent, 'sky', axis=0, tiled=False)  33.2 us
    all_gather x1, blocking collectives, on_device(): described = lax.all_gather(described, 'epoch', axis=0, tiled=True)  33.1 us
    all_to_all x1, starting transfers between devices, on_device(): lax.all_to_all(message, 'sky', split_axis=0, concat_axis=0, tiled=True)  30.2 us
    pallas_call x1, Pallas kernels, clip_and_sum(): pl.pallas_call(clip_kernel, grid=(tiles // CLIP_GROUP,), out_shape=jax.Sh...  17.6 us
    all_to_all x2, starting transfers between devices, summed_on_arrival(): lax.all_to_all(parts, axis, split_axis=0, concat_axis=0, tiled=True, axis...  13.8 us
    pallas_call x1, Pallas kernels, warp_columns(): pl.pallas_call(column_kernel, grid=(held // GROUP,), out_shape=jax.ShapeD...  10.3 us
  transfers between devices with their start and end apart: 7, of which 4 were waited for; matrix products, arithmetic and copies ran while one was open for 5% of the time, Pallas kernels for 11%

profile of v2, /device:TPU:34, one launch (start us, length us, event | category | flops | bytes accessed | tf_op | source)
XLA Modules:
  0.0 263.5 jit_solution(14269216350673426499)
XLA Ops:
  7.3 0.8 copy-done
  8.1 0.6 pad.17.after
  8.8 1.2 slice_bitcast_fusion.4.ints
  10.0 0.7 bitcast_convert_fusion
  10.9 0.7 reshape.634.floats
  11.6 10.3 %columns.1 = bf16[4,48,32,384]{3,2,1,0:T(8,128)(2,1)} custom-call(s32[48]{0:T(128)} %slice_bitcast_fusion.4.ints, f32[288]{0:T(512)} %reshape.634.floats, bf16[48,384]{1,0:T(8,128)(2,1)} %pad.17.after, bf16[48,3,32,512]{3,2,1,0:T(8,128)(2,1)} %pixels.1), custom_call_target="tpu_custom_call" | custom-call | flops 2415919104 | bytes 9437184 | tf_op jit(solution)/shard_map/columns/pallas_call | solution.py:100
  22.0 45.4 %all-to-all-start = ((bf16[4,48,32,384]{3,2,1,0:T(8,128)(2,1)}), bf16[4,48,32,384]{3,2,1,0:T(8,128)(2,1)}, u32[]{:S(2)}, u32[]{:S(2)}) async-start(bf16[4,48,32,384]{3,2,1,0:T(8,128)(2,1)} %columns.1), calls=%async_computation | async-start | bytes 9437184 | tf_op jit(solution)/shard_map/all_to_all | solution.py:279
  68.7 33.1 %all_gather.9 = f32[192,128]{1,0:T(8,128)S(1)} all-gather(f32[48,128]{1,0:T(8,128)S(1)} %pad.16), channel_id=1, replica_groups=mesh['groups'=2,'sky'=32,'epoch'=4,'band'=2] {'epoch'}, dimensions={0}, use_global_device_ids=true | all-gather | bytes 122880 | tf_op jit(solution)/shard_map/all_gather | solution.py:294
  101.9 0.4 slice_reduce_fusion.2
  104.0 0.7 clamp_reduce_fusion
  104.9 0.3 fusion.35
  105.8 0.7 pad_bitcast_fusion
  106.5 0.3 fusion.30
  106.9 30.2 %all-to-all-start.3 = ((f32[32,8,128]{2,1,0:T(8,128)}), f32[32,8,128]{2,1,0:T(8,128)S(1)}, u32[]{:S(2)}, u32[]{:S(2)}) async-start(f32[32,8,128]{2,1,0:T(8,128)} %pad_bitcast_fusion), calls=%async_computation.3 | async-start | bytes 262144 | tf_op jit(solution)/shard_map/all_to_all | solution.py:345
  137.9 0.7 fusion.206
  138.6 0.4 copy_multiply_fusion.plane
  138.9 33.2 %all-gather.3.cloned.1.call-done = bf16[1536,384]{1,0:T(8,128)(2,1)} async-done(((bf16[48,384]{1,0:T(8,128)(2,1)}), bf16[1536,384]{1,0:T(8,128)(2,1)}) %all-gather.3.cloned.1.call-update) | async-done | bytes 1179664 | tf_op jit(solution)/shard_map/all_gather | solution.py:275
  172.2 1.3 copy-done.1
  173.4 17.6 %clip.1 = bf16[32,32,384]{2,1,0:T(8,128)(2,1)S(1)} custom-call(s32[384]{0:T(512)S(1)} %pad_add_fusion.ints, f32[2880]{0:T(1024)S(1)} %reshape.621.floats, bf16[192,32,384]{2,1,0:T(8,128)(2,1)} %bitcast.9.columns, f32[192,6,128]{2,1,0:T(8,128)S(1)} %copy_multiply_fusion.plane, bf16[32,48,384]{2,1,0:T(8,128)(2,1)S(1)} %bitcast.106), custom_call_target="tpu_custom_call" | custom-call | flops 106168320 | bytes 4718592 | tf_op jit(solution)/shard_map/clip/pallas_call | solution.py:197
  191.1 1.0 copy.202
  192.1 3.6 %all-to-all-start.1 = ((bf16[4,8,32,384]{3,2,1,0:T(8,128)(2,1)}), bf16[4,8,32,384]{3,2,1,0:T(8,128)(2,1)S(1)}, u32[]{:S(2)}, u32[]{:S(2)}) async-start(bf16[4,8,32,384]{3,2,1,0:T(8,128)(2,1)} %bitcast.99), calls=%async_computation.1 | async-start | bytes 1572864 | tf_op jit(solution)/shard_map/all_to_all | solution.py:231
  197.0 19.7 %all-to-all-done.1 = bf16[4,8,32,384]{3,2,1,0:T(8,128)(2,1)S(1)} async-done(((bf16[4,8,32,384]{3,2,1,0:T(8,128)(2,1)}), bf16[4,8,32,384]{3,2,1,0:T(8,128)(2,1)S(1)}, u32[]{:S(2)}, u32[]{:S(2)}) %all-to-all-start.1) | async-done | bytes 786464 | tf_op jit(solution)/shard_map/all_to_all | solution.py:231
  216.7 0.8 fusion.36
  217.5 10.2 %all-to-all-start.2 = ((bf16[8,32,384]{2,1,0:T(8,128)(2,1)}), bf16[8,32,384]{2,1,0:T(8,128)(2,1)S(1)}, u32[]{:S(2)}, u32[]{:S(2)}) async-start(bf16[8,32,384]{2,1,0:T(8,128)(2,1)} %fusion.36), calls=%async_computation.2 | async-start | bytes 393216 | tf_op jit(solution)/shard_map/all_to_all | solution.py:231
  227.7 0.5 fusion.1
  228.2 0.8 convolution_bitcast_fusion.1
  229.0 1.4 collective-permute-start
  230.5 1.3 collective-permute-start.1
  232.0 5.1 %collective-permute-done.1 = f32[3,8,128]{2,0,1:T(4,128)S(1)} collective-permute-done((f32[3,8,128]{2,0,1:T(4,128)S(1)}, f32[3,8,128]{2,0,1:T(4,128)S(1)}, u32[]{:S(2)}, u32[]{:S(2)}) %collective-permute-start.1) | collective-permute-done | bytes 12320 | tf_op jit(solution)/shard_map/ppermute | solution.py:358
  237.1 18.2 %all-to-all-done.2 = bf16[8,32,384]{2,1,0:T(8,128)(2,1)S(1)} async-done(((bf16[8,32,384]{2,1,0:T(8,128)(2,1)}), bf16[8,32,384]{2,1,0:T(8,128)(2,1)S(1)}, u32[]{:S(2)}, u32[]{:S(2)}) %all-to-all-start.2) | async-done | bytes 196640 | tf_op jit(solution)/shard_map/all_to_all | solution.py:231
  255.4 0.6 copy.181
  256.0 0.6 copy.182
  (105 shorter events, 6.0 us)
Async XLA Ops:
  7.2 0.9 copy-start
  7.2 165.0 %all-gather.3.cloned.1.call-start = ((), (), s32[]{:S(2)}) async-start(), calls=%async_computation.4 | async-start | bytes 1216512 | tf_op jit(solution)/shard_map/all_gather | solution.py:275
  21.9 45.5 %copy-start.5 = (s32[48,2]{0,1:T(2,128)S(1)}, s32[48,2]{0,1:T(2,128)}, u32[]{:S(2)}) copy-start(s32[48,2]{0,1:T(2,128)} %param.18) | copy-start | bytes 1156
  21.9 45.5 %copy-start.6 = (bf16[48,2]{0,1:T(2,128)(2,1)S(1)}, bf16[48,2]{0,1:T(2,128)(2,1)}, u32[]{:S(2)}) copy-start(bf16[48,2]{0,1:T(2,128)(2,1)} %param.19) | copy-start | bytes 580
  21.9 46.3 %copy-start.2 = (s32[48,6,16]{0,2,1:T(8,128)S(1)}, s32[48,6,16]{0,2,1:T(8,128)}, u32[]{:S(2)}) copy-start(s32[48,6,16]{0,2,1:T(8,128)} %param.21) | copy-start | bytes 55300
  21.9 46.4 %copy-start.4 = (bf16[48,3]{0,1:T(4,128)(2,1)S(1)}, bf16[48,3]{0,1:T(4,128)(2,1)}, u32[]{:S(2)}) copy-start(bf16[48,3]{0,1:T(4,128)(2,1)} %param.20) | copy-start | bytes 868
  21.9 46.5 %copy-start.7 = (s32[48,1]{0,1:T(1,128)S(1)}, s32[48,1]{0,1:T(1,128)}, u32[]{:S(2)}) copy-start(s32[48,1]{0,1:T(1,128)} %param.17) | copy-start | bytes 580
  21.9 81.4 %copy-start.3 = (f32[3,32]{1,0:T(4,128)S(1)}, f32[3,32]{1,0:T(4,128)}, u32[]{:S(2)}) copy-start(f32[3,32]{1,0:T(4,128)} %param.24) | copy-start | bytes 1156
  22.0 85.0 %all-to-all-start = ((bf16[4,48,32,384]{3,2,1,0:T(8,128)(2,1)}), bf16[4,48,32,384]{3,2,1,0:T(8,128)(2,1)}, u32[]{:S(2)}, u32[]{:S(2)}) async-start(bf16[4,48,32,384]{3,2,1,0:T(8,128)(2,1)} %columns.1), calls=%async_computation | async-start | bytes 9437184 | tf_op jit(solution)/shard_map/all_to_all | solution.py:279
  106.9 85.1 %all-to-all-start.3 = ((f32[32,8,128]{2,1,0:T(8,128)}), f32[32,8,128]{2,1,0:T(8,128)S(1)}, u32[]{:S(2)}, u32[]{:S(2)}) async-start(f32[32,8,128]{2,1,0:T(8,128)} %pad_bitcast_fusion), calls=%async_computation.3 | async-start | bytes 262144 | tf_op jit(solution)/shard_map/all_to_all | solution.py:345
  172.2 1.3 copy-start.1
  192.1 24.6 %all-to-all-start.1 = ((bf16[4,8,32,384]{3,2,1,0:T(8,128)(2,1)}), bf16[4,8,32,384]{3,2,1,0:T(8,128)(2,1)S(1)}, u32[]{:S(2)}, u32[]{:S(2)}) async-start(bf16[4,8,32,384]{3,2,1,0:T(8,128)(2,1)} %bitcast.99), calls=%async_computation.1 | async-start | bytes 1572864 | tf_op jit(solution)/shard_map/all_to_all | solution.py:231
  217.5 37.8 %all-to-all-start.2 = ((bf16[8,32,384]{2,1,0:T(8,128)(2,1)}), bf16[8,32,384]{2,1,0:T(8,128)(2,1)S(1)}, u32[]{:S(2)}, u32[]{:S(2)}) async-start(bf16[8,32,384]{2,1,0:T(8,128)(2,1)} %fusion.36), calls=%async_computation.2 | async-start | bytes 393216 | tf_op jit(solution)/shard_map/all_to_all | solution.py:231
  229.0 2.9 %collective-permute-start = (f32[3,8,128]{2,0,1:T(4,128)S(1)}, f32[3,8,128]{2,0,1:T(4,128)S(1)}, u32[]{:S(2)}, u32[]{:S(2)}) collective-permute-start(f32[3,8,128]{2,0,1:T(4,128)S(1)} %copy.190), channel_id=1, source_target_pairs={{0,8},{8,16},{16,24},{24,32},{32,40},{40,48},{48,56},{56,64},{64,7... | collective-permute-start | bytes 36872 | tf_op jit(solution)/shard_map/ppermute | solution.py:357
  230.5 6.6 %collective-permute-start.1 = (f32[3,8,128]{2,0,1:T(4,128)S(1)}, f32[3,8,128]{2,0,1:T(4,128)S(1)}, u32[]{:S(2)}, u32[]{:S(2)}) collective-permute-start(f32[3,8,128]{2,0,1:T(4,128)S(1)} %copy.191), channel_id=1, source_target_pairs={{8,0},{16,8},{24,16},{32,24},{40,32},{48,40},{56,48},{64,56},{72,6... | collective-permute-start | bytes 36872 | tf_op jit(solution)/shard_map/ppermute | solution.py:358
Sparse Core Ops, SparseCore 0:
  10.1 161.9 all-gather.2

commit v3 on v2

--- a/solution.py
+++ b/solution.py
@@ -15,7 +15,6 @@
 ROW_BLOCK = 8
 LANES = 128
 GROUP = 8
-CLIP_GROUP = 48
 UNROLL = 4
 NEAR = 4
 
@@ -40,11 +39,12 @@
     return jnp.clip(total, 0.0, 1.0)
 
 
-def column_kernel(ints, floats, after, pixels, out, tables):
+def column_kernel(ints, floats, pixels, out, tables):
     step = pl.program_id(0)
     slots, bands, rows, cols = pixels.shape
     blocks = cols // LANES
     edge = 16
+    turn = ints[pl.num_programs(0) * slots]
     parts = out.shape[0]
     width = cols // parts
 
@@ -82,9 +82,10 @@
         warped = jnp.dot(source, table[...], preferred_element_type=jnp.float32)
         warped = warped.astype(out.dtype)
         for part in range(parts):
+            ahead = lax.rem(part - turn + parts, parts)
             for band in range(bands):
                 piece = warped[band * rows : (band + 1) * rows, part * width : (part + 1) * width]
-                out[part, slot, :, band * width : (band + 1) * width] = piece
+                out[ahead, slot, :, band * width : (band + 1) * width] = piece
 
     def pair(index, carry):
         for half in range(2):
@@ -94,7 +95,7 @@
     lax.fori_loop(0, slots // 2, pair, 0)
 
 
-def warp_columns(pixels, shifts, taps, after, parts):
+def warp_columns(pixels, shifts, taps, turn, parts):
     held, bands, rows, cols = pixels.shape
     width = bands * cols // parts
     return pl.pallas_call(
@@ -104,7 +105,6 @@
         in_specs=[
             pl.BlockSpec(memory_space=pltpu.SMEM),
             pl.BlockSpec(memory_space=pltpu.SMEM),
-            pl.BlockSpec(memory_space=pl.ANY),
             pl.BlockSpec((GROUP, bands, rows, cols), lambda g: (g, 0, 0, 0)),
         ],
         out_specs=pl.BlockSpec((parts, GROUP, rows, width), lambda g: (0, g, 0, 0)),
@@ -116,40 +116,40 @@
             transcendentals=0,
         ),
         name="columns",
-    )(shifts, taps.reshape(-1), after, pixels)
-
-
-def clip_kernel(ints, floats, columns, plane, template, out, framed, sums):
-    step = pl.program_id(0)
-    slots, rows, width = columns.shape
+    )(jnp.append(shifts, turn), taps.reshape(-1), pixels)
+
+
+def clip_kernel(ints, floats, plane, template, *refs):
+    groups, (out, framed, sums) = refs[:-3], refs[-3:]
+    slots, rows, width = groups[0].shape
     owners = out.shape[0]
+    near = template.shape[0]
     bands = width // LANES
     canvas_rows = rows + 2 * MARGIN
-    total = pl.num_programs(0) * slots
-
-    @pl.when(step == 0)
-    def _():
-        ends = framed.shape[0]
-        framed[0:MARGIN, :] = jnp.zeros((MARGIN, width), jnp.float32)
-        framed[ends - MARGIN : ends, :] = jnp.zeros((MARGIN, width), jnp.float32)
-
-        def fill(owner, carry):
-            start = pl.multiple_of(owner * rows + MARGIN, MARGIN)
-            first = pl.multiple_of(owner * rows, rows)
-            framed[pl.ds(start, rows), :] = template[owner, 0:rows, :].astype(jnp.float32)
-            sums[pl.ds(first, rows), :] = jnp.zeros((rows, width), jnp.float32)
-            return carry
-
-        lax.fori_loop(0, owners, fill, 0)
-        sums[ends - 2 * MARGIN : ends, :] = jnp.zeros((2 * MARGIN, width), jnp.float32)
+    total = len(groups) * slots
+    ends = framed.shape[0]
+    framed[0:MARGIN, :] = jnp.zeros((MARGIN, width), jnp.float32)
+    framed[ends - MARGIN : ends, :] = jnp.zeros((MARGIN, width), jnp.float32)
+
+    def fill(owner, carry):
+        start = pl.multiple_of(owner * rows + MARGIN, MARGIN)
+        first = pl.multiple_of(owner * rows, rows)
+        block = template[lax.rem(owner, near), lax.div(owner, near)]
+        framed[pl.ds(start, rows), :] = block.astype(jnp.float32)
+        sums[pl.ds(first, rows), :] = jnp.zeros((rows, width), jnp.float32)
+        return carry
+
+    lax.fori_loop(0, owners, fill, 0)
+    sums[ends - 2 * MARGIN : ends, :] = jnp.zeros((2 * MARGIN, width), jnp.float32)
 
     i = lax.broadcasted_iota(jnp.int32, (canvas_rows, LANES), 0)
     k = lax.broadcasted_iota(jnp.int32, (canvas_rows, LANES), 1)
     base = i - MARGIN - k
-    ones = jnp.ones((rows, LANES), columns.dtype)
-
-    def one(slot):
-        at = step * slots + slot
+    ones = jnp.ones((rows, LANES), out.dtype)
+
+    def one(group, slot):
+        columns = groups[group]
+        at = group * slots + slot
         first = pl.multiple_of(ints[at], ROW_BLOCK)
         gap = base - ints[total + at]
         table = jnp.zeros(gap.shape, jnp.float32)
@@ -163,7 +163,7 @@
             low = block * ROW_BLOCK
             where = pl.ds(first + low, ROW_BLOCK)
             row_cover = jnp.clip(warped[low : low + ROW_BLOCK, width:], 0.0, 1.0)
-            weight = row_cover * plane[slot, block : block + 1, :]
+            weight = row_cover * plane[at, block : block + 1, :]
             for band in range(bands):
                 lanes = slice(band * LANES, (band + 1) * LANES)
                 prior = framed[where, lanes]
@@ -172,54 +172,46 @@
                 value = prior * floats[scale + 1] + jnp.tanh(pull) * floats[scale + 2]
                 sums[where, lanes] += weight * value
 
-    def several(index, carry):
+    def several(group, index, carry):
         for part in range(UNROLL):
-            one(index * UNROLL + part)
+            one(group, index * UNROLL + part)
         return carry
 
-    lax.fori_loop(0, slots // UNROLL, several, 0)
-
-    @pl.when(step == pl.num_programs(0) - 1)
-    def _():
-        def give(owner, carry):
-            start = pl.multiple_of(owner * rows + MARGIN, MARGIN)
-            out[owner] = sums[pl.ds(start, rows), :].astype(out.dtype)
-            return carry
-
-        lax.fori_loop(0, owners, give, 0)
+    for group in range(len(groups)):
+        lax.fori_loop(0, slots // UNROLL, functools.partial(several, group), 0)
+
+    def give(owner, carry):
+        start = pl.multiple_of(owner * rows + MARGIN, MARGIN)
+        out[owner] = sums[pl.ds(start, rows), :].astype(out.dtype)
+        return carry
+
+    lax.fori_loop(0, owners, give, 0)
 
 
 def clip_and_sum(ints, floats, columns, plane, template):
-    tiles, rows, width = columns.shape
-    owners = template.shape[0]
+    rows, width = columns[0].shape[1:]
+    tiles = plane.shape[0]
+    owners = template.shape[0] * template.shape[1]
     height = owners * rows + 2 * MARGIN
     out_shape = (owners, rows, width)
     return pl.pallas_call(
         clip_kernel,
-        grid=(tiles // CLIP_GROUP,),
         out_shape=jax.ShapeDtypeStruct(out_shape, jnp.bfloat16),
-        in_specs=[
-            pl.BlockSpec(memory_space=pltpu.SMEM),
-            pl.BlockSpec(memory_space=pltpu.SMEM),
-            pl.BlockSpec((CLIP_GROUP, rows, width), lambda g: (g, 0, 0)),
-            pl.BlockSpec((CLIP_GROUP,) + plane.shape[1:], lambda g: (g, 0, 0)),
-            pl.BlockSpec(template.shape, lambda g: (0, 0, 0)),
-        ],
-        out_specs=pl.BlockSpec(out_shape, lambda g: (0, 0, 0)),
+        in_specs=[pl.BlockSpec(memory_space=pltpu.SMEM)] * 2
+        + [pl.BlockSpec(memory_space=pltpu.VMEM)] * (2 + len(columns)),
+        out_specs=pl.BlockSpec(memory_space=pltpu.VMEM),
         scratch_shapes=[
             pltpu.VMEM((height, width), jnp.float32),
             pltpu.VMEM((height, width), jnp.float32),
         ],
-        compiler_params=pltpu.CompilerParams(
-            dimension_semantics=("arbitrary",), vmem_limit_bytes=32 * 1024 * 1024
-        ),
+        compiler_params=pltpu.CompilerParams(vmem_limit_bytes=32 * 1024 * 1024),
         cost_estimate=pl.CostEstimate(
             flops=30 * tiles * (rows + 2 * MARGIN) * width,
             bytes_accessed=2 * tiles * rows * width,
             transcendentals=tiles * (rows + 2 * MARGIN) * width,
         ),
         name="clip",
-    )(ints, floats, columns, plane, template)
+    )(ints, floats, plane, template, *columns)
 
 
 def spread(index, block_count, block):
@@ -234,16 +226,42 @@
     return functools.reduce(jnp.add, [part.astype(jnp.float32) for part in arrived])
 
 
+def sky_groups():
+    count = lax.axis_size("sky")
+    near = NEAR if count % NEAR == 0 else 1
+    far = count // near
+    near_groups = [[f * near + n for n in range(near)] for f in range(far)]
+    far_groups = [[f * near + n for f in range(far)] for n in range(near)]
+    return near, far, near_groups, far_groups
+
+
 def sum_over_sky(parts):
-    count = parts.shape[0]
-    if NEAR == 1 or count % NEAR:
-        return summed_on_arrival(parts, "sky")
-    far = count // NEAR
-    near_groups = [[f * NEAR + n for n in range(NEAR)] for f in range(far)]
-    far_groups = [[f * NEAR + n for f in range(far)] for n in range(NEAR)]
-    parts = jnp.swapaxes(parts.reshape((far, NEAR) + parts.shape[1:]), 0, 1)
+    near, far, near_groups, far_groups = sky_groups()
+    parts = jnp.swapaxes(parts.reshape((far, near) + parts.shape[1:]), 0, 1)
     parts = summed_on_arrival(parts, "sky", near_groups).astype(jnp.bfloat16)
     return summed_on_arrival(parts, "sky", far_groups)
+
+
+def gather_over_sky(shard):
+    near, far, near_groups, far_groups = sky_groups()
+
+    def to_all(array, count, groups):
+        copies = jnp.broadcast_to(array[None], (count,) + array.shape)
+        return lax.all_to_all(
+            copies, "sky", split_axis=0, concat_axis=0, tiled=True, axis_index_groups=groups
+        )
+
+    shard = to_all(shard, far, far_groups)
+    return to_all(shard, near, near_groups)
+
+
+def from_epochs(pieces):
+    count = lax.axis_size("epoch")
+    arrived = [pieces[0]]
+    for ahead in range(1, count):
+        route = [(i, (i + ahead) % count) for i in range(count)]
+        arrived.append(lax.ppermute(pieces[ahead], "epoch", route))
+    return arrived
 
 
 def on_device(
@@ -271,13 +289,7 @@
         template, epoch_position * part_width, part_width, 2
     )
     sent = jnp.swapaxes(template_part, 0, 1).reshape(rows, bands * part_width)
-    sent = jnp.pad(sent, ((0, rows // 2), (0, 0)))
-    whole_template = lax.all_gather(sent, "sky", axis=0, tiled=False)
-
-    taps_x = tap_weights(slot_frac[:, 1].astype(jnp.float32))
-    columns = warp_columns(slot_pixels, slot_offset[:, 1], taps_x, sent, epoch_count)
-    columns = lax.all_to_all(columns, "epoch", split_axis=0, concat_axis=0, tiled=True)
-    columns = columns.reshape((-1,) + columns.shape[2:])
+    whole_template = gather_over_sky(sent)
 
     live = (jnp.arange(held, dtype=jnp.int32) < slot_count[0]).astype(jnp.float32)
     described = jnp.concatenate(
@@ -291,8 +303,12 @@
         1,
     )
     described = jnp.pad(described, ((0, 0), (0, LANES - described.shape[1])))
-    described = lax.all_gather(described, "epoch", axis=0, tiled=True)
+    described = jnp.concatenate(from_epochs([described] * epoch_count), 0)
     tiles = described.shape[0]
+
+    taps_x = tap_weights(slot_frac[:, 1].astype(jnp.float32))
+    columns = warp_columns(slot_pixels, slot_offset[:, 1], taps_x, epoch_position, epoch_count)
+    columns = from_epochs(columns)
 
     def unpack(table):
         masks = table[:, :cells].reshape(-1, row_blocks, col_blocks)
@@ -338,12 +354,18 @@
     slots = jnp.arange(sky_count * routes, dtype=jnp.int32)
     chooser = (position[None, :] == slots[:, None]).astype(jnp.float32)
     chosen = jnp.dot(chooser, described[:, : cells + 4 + bands], precision=high)
-    totals = jnp.broadcast_to(band_part[None, :], (chosen.shape[0], bands))
+    pieces = []
+    for _ in range(3):
+        pieces.append(lax.reduce_precision(band_part, 8, 7))
+        band_part = band_part - pieces[-1]
+    totals = jnp.broadcast_to(jnp.concatenate(pieces)[None, :], (chosen.shape[0], 3 * bands))
     message = jnp.concatenate([chosen, totals], 1)
-    message = jnp.pad(message, ((0, 0), (0, LANES - message.shape[1])))
+    message = jnp.pad(message, ((0, 0), (0, LANES - message.shape[1]))).astype(jnp.bfloat16)
     message = message.reshape(sky_count, routes, LANES)
     arrived = lax.all_to_all(message, "sky", split_axis=0, concat_axis=0, tiled=True)
-    band_total = jnp.sum(arrived[:, 0, cells + 4 + bands : cells + 4 + 2 * bands], 0)
+    arrived = arrived.astype(jnp.float32)
+    totals = arrived[:, 0, cells + 4 + bands : cells + 4 + 4 * bands]
+    band_total = jnp.sum(totals.reshape(-1, bands), 0)
 
     own_masks, own_shift, own_taps, own_sigmas = unpack(arrived.reshape(-1, LANES))
     own_over = 1.0 / (own_sigmas * own_sigmas)
@@ -360,7 +382,8 @@
     weight_sum = weight_sum.at[:, :MARGIN].add(from_above)
     weight_sum = weight_sum.at[:, rows - MARGIN :].add(from_below)
 
-    flux = sum_over_sky(clip_and_sum(ints, floats, columns, plane, whole_template))
+    partial = clip_and_sum(ints, floats, columns, plane, whole_template)
+    flux = sum_over_sky(partial)
     flux_sum = jnp.swapaxes(flux.reshape(rows, bands, part_width), 0, 1)
 
     prior = prior_weight[:, :, None]

time: 264 us -> 241 us (0.913)
  the two profiles are of different devices: /device:TPU:34 before, /device:TPU:40 now
where the time goes in v3:
time: 241 us; the launch traced here: 239 us
  starting transfers between devices  118 us (49%)
  waiting for transfers between devices  46.6 us (19%)
  Pallas kernels  27.8 us (12%)
  other arithmetic  27.1 us (11%)
  local copies, waits for them, and re-layouts  13.9 us (6%)
  matrix products  3.77 us (2%)
    all_to_all x2, starting transfers between devices, to_all(): lax.all_to_all(copies, 'sky', split_axis=0, concat_axis=0, tiled=True, ax...  49.2 us
    all_to_all x2, waiting for transfers between devices, summed_on_arrival(): lax.all_to_all(parts, axis, split_axis=0, concat_axis=0, tiled=True, axis...  36.4 us
    all_to_all x2, starting transfers between devices, summed_on_arrival(): lax.all_to_all(parts, axis, split_axis=0, concat_axis=0, tiled=True, axis...  23.1 us
    all_to_all x1, starting transfers between devices, on_device(): lax.all_to_all(message, 'sky', split_axis=0, concat_axis=0, tiled=True)  22.8 us
    ppermute x6, starting transfers between devices, from_epochs(): arrived.append(lax.ppermute(pieces[ahead], 'epoch', route))  20.3 us
    pallas_call x1, Pallas kernels, clip_and_sum(): pl.pallas_call(clip_kernel, out_shape=jax.ShapeDtypeStruct(out_shape, jnp...  17.4 us
    pallas_call x1, Pallas kernels, warp_columns(): pl.pallas_call(column_kernel, grid=(held // GROUP,), out_shape=jax.ShapeD...  10.4 us
    ppermute x1, waiting for transfers between devices, on_device(): from_above = lax.ppermute(weights[:, canvas_rows - MARGIN:], 'sky', ring)  7.41 us
  transfers between devices with their start and end apart: 13, of which 5 were waited for; matrix products, arithmetic and copies ran while one was open for 17% of the time, Pallas kernels for 12%

profile of v3, /device:TPU:40, one launch (start us, length us, event | category | flops | bytes accessed | tf_op | source)
XLA Modules:
  0.0 239.5 jit_solution(9771853259900564060)
XLA Ops:
  4.2 5.1 %collective-permute-start.2 = (f32[48,128]{0,1:T(8,128)S(1)}, f32[48,128]{0,1:T(8,128)S(1)}, u32[]{:S(2)}, u32[]{:S(2)}) collective-permute-start(f32[48,128]{0,1:T(8,128)S(1)} %pad.13), channel_id=1, source_target_pairs={{0,6},{2,0},{4,2},{6,4},{1,7},{3,1},{5,3},{7,5},{8,14},{10,8},{12,... | collective-permute-start | bytes 73736 | tf_op jit(solution)/shard_map/ppermute | solution.py:263
  9.3 2.5 %collective-permute-start.1 = (f32[48,128]{0,1:T(8,128)S(1)}, f32[48,128]{0,1:T(8,128)S(1)}, u32[]{:S(2)}, u32[]{:S(2)}) collective-permute-start(f32[48,128]{0,1:T(8,128)S(1)} %pad.13), channel_id=1, source_target_pairs={{0,4},{2,6},{4,0},{6,2},{1,5},{3,7},{5,1},{7,3},{8,12},{10,14},{12... | collective-permute-start | bytes 73736 | tf_op jit(solution)/shard_map/ppermute | solution.py:263
  11.8 3.0 %collective-permute-start = (f32[48,128]{0,1:T(8,128)S(1)}, f32[48,128]{0,1:T(8,128)S(1)}, u32[]{:S(2)}, u32[]{:S(2)}) collective-permute-start(f32[48,128]{0,1:T(8,128)S(1)} %pad.13), channel_id=1, source_target_pairs={{0,2},{2,4},{4,6},{6,0},{1,3},{3,5},{5,7},{7,1},{8,10},{10,12},{12... | collective-permute-start | bytes 73736 | tf_op jit(solution)/shard_map/ppermute | solution.py:263
  15.5 43.4 %all-to-all-start = ((bf16[8,32,384]{2,1,0:T(8,128)(2,1)}), bf16[8,32,384]{2,1,0:T(8,128)(2,1)S(1)}, u32[]{:S(2)}, u32[]{:S(2)}) async-start(bf16[8,32,384]{2,1,0:T(8,128)(2,1)} %broadcast_in_dim.319), calls=%async_computation | async-start | bytes 393216 | tf_op jit(solution)/shard_map/all_to_all | solution.py:250
  61.9 10.4 %columns.1 = bf16[4,48,32,384]{3,2,1,0:T(8,128)(2,1)} custom-call(s32[49]{0:T(128)} %pad_add_fusion.1.ints, f32[288]{0:T(512)} %reshape.631.floats, bf16[48,3,32,512]{3,2,1,0:T(8,128)(2,1)} %pixels.1), custom_call_target="tpu_custom_call" | custom-call | flops 2415919104 | bytes 9437184 | tf_op jit(solution)/shard_map/columns/pallas_call | solution.py:101
  72.3 4.4 %slice_bitcast_fusion = (bf16[48,32,384]{2,1,0:T(8,128)(2,1)}, bf16[48,32,384]{2,1,0:T(8,128)(2,1)}, bf16[48,32,384]{2,1,0:T(8,128)(2,1)}, bf16[48,32,384]{2,1,0:T(8,128)(2,1)S(1)}) fusion(bf16[4,48,32,384]{3,2,1,0:T(8,128)(2,1)} %columns.1), kind=kLoop, calls=%fused_computation.10 | loop fusion | bytes 9437184 | tf_op jit(solution)/shard_map/squeeze | solution.py:263
  76.7 4.1 %collective-permute-start.5 = (bf16[48,32,384]{2,1,0:T(8,128)(2,1)}, bf16[48,32,384]{2,1,0:T(8,128)(2,1)S(1)}, u32[]{:S(2)}, u32[]{:S(2)}) collective-permute-start(bf16[48,32,384]{2,1,0:T(8,128)(2,1)} %get-tuple-element.48), channel_id=1, source_target_pairs={{0,6},{2,0},{4,2},{6,4},{1,7},{3,1},{5,3},{7,5},{8,14},{10,8},{12,... | collective-permute-start | bytes 3538952 | tf_op jit(solution)/shard_map/ppermute | solution.py:263
  80.8 3.7 %collective-permute-start.4 = (bf16[48,32,384]{2,1,0:T(8,128)(2,1)}, bf16[48,32,384]{2,1,0:T(8,128)(2,1)}, u32[]{:S(2)}, u32[]{:S(2)}) collective-permute-start(bf16[48,32,384]{2,1,0:T(8,128)(2,1)} %get-tuple-element.49), channel_id=1, source_target_pairs={{0,4},{2,6},{4,0},{6,2},{1,5},{3,7},{5,1},{7,3},{8,12},{10,14},{12... | collective-permute-start | bytes 3538952 | tf_op jit(solution)/shard_map/ppermute | solution.py:263
  88.1 1.9 collective-permute-start.3
  91.3 1.2 fusion.256
  92.7 1.0 broadcast_in_dim.320
  93.7 5.8 %all-to-all-start.1 = ((bf16[4,8,32,384]{3,2,1,0:T(8,128)(2,1)}), bf16[4,8,32,384]{3,2,1,0:T(8,128)(2,1)S(1)}, u32[]{:S(2)}, u32[]{:S(2)}) async-start(bf16[4,8,32,384]{3,2,1,0:T(8,128)(2,1)} %broadcast_in_dim.320), calls=%async_computation.1 | async-start | bytes 1572864 | tf_op jit(solution)/shard_map/all_to_all | solution.py:250
  100.3 1.6 reduce_window_sum.11
  102.0 1.1 select_reduce_fusion
  106.9 1.4 clamp_reduce_fusion
  111.3 1.6 fusion.30
  113.0 2.4 fusion.204
  115.4 1.0 fusion.18
  116.4 1.2 fusion.34
  118.0 22.8 %all-to-all-start.4 = ((bf16[32,8,128]{2,1,0:T(8,128)(2,1)}), bf16[32,8,128]{2,1,0:T(8,128)(2,1)S(1)}, u32[]{:S(2)}, u32[]{:S(2)}) async-start(bf16[32,8,128]{2,1,0:T(8,128)(2,1)} %pad_bitcast_fusion), calls=%async_computation.4 | async-start | bytes 131072 | tf_op jit(solution)/shard_map/all_to_all | solution.py:365
  141.3 1.3 fusion.61
  142.5 1.4 copy_multiply_fusion.plane
  144.0 17.4 %clip.1 = bf16[32,32,384]{2,1,0:T(8,128)(2,1)S(1)} custom-call(s32[384]{0:T(512)S(1)} %pad_add_fusion.ints, f32[2880]{0:T(1024)S(1)} %reshape.618.floats, f32[192,6,128]{2,1,0:T(8,128)S(1)} %copy_multiply_fusion.plane, bf16[4,8,32,384]{3,2,1,0:T(8,128)(2,1)S(1)} %all-to-all-done.1.template, bf16[48,32,384]{2,1,0:T(8,128)(2,1)S(1)} %get-tuple-element.51.refs_0_, ...), custom_call_target="tpu_custom_call" | custom-call | flops 106168320 | bytes 4718592 | tf_op jit(solution)/shard_map/clip/pallas_call | solution.py:197
  161.4 1.0 copy.154
  162.4 2.4 %all-to-all-done.4 = bf16[32,8,128]{2,1,0:T(8,128)(2,1)S(1)} async-done(((bf16[32,8,128]{2,1,0:T(8,128)(2,1)}), bf16[32,8,128]{2,1,0:T(8,128)(2,1)S(1)}, u32[]{:S(2)}, u32[]{:S(2)}) %all-to-all-start.4) | async-done | bytes 65568 | tf_op jit(solution)/shard_map/all_to_all | solution.py:365
  164.8 3.7 %all-to-all-start.2 = ((bf16[4,8,32,384]{3,2,1,0:T(8,128)(2,1)}), bf16[4,8,32,384]{3,2,1,0:T(8,128)(2,1)S(1)}, u32[]{:S(2)}, u32[]{:S(2)}) async-start(bf16[4,8,32,384]{3,2,1,0:T(8,128)(2,1)} %bitcast.113), calls=%async_computation.2 | async-start | bytes 1572864 | tf_op jit(solution)/shard_map/all_to_all | solution.py:223
  170.1 16.0 %all-to-all-done.2 = bf16[4,8,32,384]{3,2,1,0:T(8,128)(2,1)S(1)} async-done(((bf16[4,8,32,384]{3,2,1,0:T(8,128)(2,1)}), bf16[4,8,32,384]{3,2,1,0:T(8,128)(2,1)S(1)}, u32[]{:S(2)}, u32[]{:S(2)}) %all-to-all-start.2) | async-done | bytes 786464 | tf_op jit(solution)/shard_map/all_to_all | solution.py:223
  186.9 19.4 %all-to-all-start.3 = ((bf16[8,32,384]{2,1,0:T(8,128)(2,1)}), bf16[8,32,384]{2,1,0:T(8,128)(2,1)S(1)}, u32[]{:S(2)}, u32[]{:S(2)}) async-start(bf16[8,32,384]{2,1,0:T(8,128)(2,1)} %fusion.35), calls=%async_computation.3 | async-start | bytes 393216 | tf_op jit(solution)/shard_map/all_to_all | solution.py:223
  207.6 1.3 collective-permute-start.6
  209.0 1.3 collective-permute-start.7
  210.3 7.4 %collective-permute-done.6 = f32[3,8,128]{2,0,1:T(4,128)S(1)} collective-permute-done((f32[3,8,128]{2,0,1:T(4,128)S(1)}, f32[3,8,128]{2,0,1:T(4,128)S(1)}, u32[]{:S(2)}, u32[]{:S(2)}) %collective-permute-start.6) | collective-permute-done | bytes 12320 | tf_op jit(solution)/shard_map/ppermute | solution.py:379
  217.7 20.3 %all-to-all-done.3 = bf16[8,32,384]{2,1,0:T(8,128)(2,1)S(1)} async-done(((bf16[8,32,384]{2,1,0:T(8,128)(2,1)}), bf16[8,32,384]{2,1,0:T(8,128)(2,1)S(1)}, u32[]{:S(2)}, u32[]{:S(2)}) %all-to-all-start.3) | async-done | bytes 196640 | tf_op jit(solution)/shard_map/all_to_all | solution.py:223
  (150 shorter events, 24.6 us)
Async XLA Ops:
  0.6 14.1 %copy-start = (bf16[3,32,512]{2,1,0:T(8,128)(2,1)S(1)}, bf16[3,32,512]{2,1,0:T(8,128)(2,1)}, u32[]{:S(2)}) copy-start(bf16[3,32,512]{2,1,0:T(8,128)(2,1)} %param.23) | copy-start | bytes 294916
  4.2 83.9 %collective-permute-start.2 = (f32[48,128]{0,1:T(8,128)S(1)}, f32[48,128]{0,1:T(8,128)S(1)}, u32[]{:S(2)}, u32[]{:S(2)}) collective-permute-start(f32[48,128]{0,1:T(8,128)S(1)} %pad.13), channel_id=1, source_target_pairs={{0,6},{2,0},{4,2},{6,4},{1,7},{3,1},{5,3},{7,5},{8,14},{10,8},{12,... | collective-permute-start | bytes 73736 | tf_op jit(solution)/shard_map/ppermute | solution.py:263
  9.3 80.7 %collective-permute-start.1 = (f32[48,128]{0,1:T(8,128)S(1)}, f32[48,128]{0,1:T(8,128)S(1)}, u32[]{:S(2)}, u32[]{:S(2)}) collective-permute-start(f32[48,128]{0,1:T(8,128)S(1)} %pad.13), channel_id=1, source_target_pairs={{0,4},{2,6},{4,0},{6,2},{1,5},{3,7},{5,1},{7,3},{8,12},{10,14},{12... | collective-permute-start | bytes 73736 | tf_op jit(solution)/shard_map/ppermute | solution.py:263
  11.8 78.3 %collective-permute-start = (f32[48,128]{0,1:T(8,128)S(1)}, f32[48,128]{0,1:T(8,128)S(1)}, u32[]{:S(2)}, u32[]{:S(2)}) collective-permute-start(f32[48,128]{0,1:T(8,128)S(1)} %pad.13), channel_id=1, source_target_pairs={{0,2},{2,4},{4,6},{6,0},{1,3},{3,5},{5,7},{7,1},{8,10},{10,12},{12... | collective-permute-start | bytes 73736 | tf_op jit(solution)/shard_map/ppermute | solution.py:263
  15.5 77.2 %all-to-all-start = ((bf16[8,32,384]{2,1,0:T(8,128)(2,1)}), bf16[8,32,384]{2,1,0:T(8,128)(2,1)S(1)}, u32[]{:S(2)}, u32[]{:S(2)}) async-start(bf16[8,32,384]{2,1,0:T(8,128)(2,1)} %broadcast_in_dim.319), calls=%async_computation | async-start | bytes 393216 | tf_op jit(solution)/shard_map/all_to_all | solution.py:250
  59.0 40.5 %copy-start.20 = (f32[6]{0:T(128)}, f32[6]{0:T(128)S(1)}, u32[]{:S(2)}) copy-start(f32[6]{0:T(128)S(1)} %iota_subtract_fusion.1) | copy-start | bytes 76
  72.3 15.2 %copy-start.18 = (f32[3,32]{1,0:T(4,128)S(1)}, f32[3,32]{1,0:T(4,128)}, u32[]{:S(2)}) copy-start(f32[3,32]{1,0:T(4,128)} %param.24) | copy-start | bytes 1156
  76.7 67.3 %collective-permute-start.5 = (bf16[48,32,384]{2,1,0:T(8,128)(2,1)}, bf16[48,32,384]{2,1,0:T(8,128)(2,1)S(1)}, u32[]{:S(2)}, u32[]{:S(2)}) collective-permute-start(bf16[48,32,384]{2,1,0:T(8,128)(2,1)} %get-tuple-element.48), channel_id=1, source_target_pairs={{0,6},{2,0},{4,2},{6,4},{1,7},{3,1},{5,3},{7,5},{8,14},{10,8},{12,... | collective-permute-start | bytes 3538952 | tf_op jit(solution)/shard_map/ppermute | solution.py:263
  80.8 63.1 %collective-permute-start.4 = (bf16[48,32,384]{2,1,0:T(8,128)(2,1)}, bf16[48,32,384]{2,1,0:T(8,128)(2,1)}, u32[]{:S(2)}, u32[]{:S(2)}) collective-permute-start(bf16[48,32,384]{2,1,0:T(8,128)(2,1)} %get-tuple-element.49), channel_id=1, source_target_pairs={{0,4},{2,6},{4,0},{6,2},{1,5},{3,7},{5,1},{7,3},{8,12},{10,14},{12... | collective-permute-start | bytes 3538952 | tf_op jit(solution)/shard_map/ppermute | solution.py:263
  88.1 55.9 %collective-permute-start.3 = (bf16[48,32,384]{2,1,0:T(8,128)(2,1)}, bf16[48,32,384]{2,1,0:T(8,128)(2,1)}, u32[]{:S(2)}, u32[]{:S(2)}) collective-permute-start(bf16[48,32,384]{2,1,0:T(8,128)(2,1)} %get-tuple-element.50), channel_id=1, source_target_pairs={{0,2},{2,4},{4,6},{6,0},{1,3},{3,5},{5,7},{7,1},{8,10},{10,12},{12... | collective-permute-start | bytes 3538952 | tf_op jit(solution)/shard_map/ppermute | solution.py:263
  93.7 24.3 %all-to-all-start.1 = ((bf16[4,8,32,384]{3,2,1,0:T(8,128)(2,1)}), bf16[4,8,32,384]{3,2,1,0:T(8,128)(2,1)S(1)}, u32[]{:S(2)}, u32[]{:S(2)}) async-start(bf16[4,8,32,384]{3,2,1,0:T(8,128)(2,1)} %broadcast_in_dim.320), calls=%async_computation.1 | async-start | bytes 1572864 | tf_op jit(solution)/shard_map/all_to_all | solution.py:250
  105.2 5.0 %copy-start.2 = (s32[192,1]{0,1:T(1,128)}, s32[192,1]{0,1:T(1,128)S(1)}, u32[]{:S(2)}) copy-start(s32[192,1]{0,1:T(1,128)S(1)} %get-tuple-element.96) | copy-start | bytes 2308
  105.3 5.0 %copy-start.4 = (f32[192,1]{0,1:T(1,128)}, f32[192,1]{0,1:T(1,128)S(1)}, u32[]{:S(2)}) copy-start(f32[192,1]{0,1:T(1,128)S(1)} %get-tuple-element.112) | copy-start | bytes 2308
  105.3 5.0 %copy-start.6 = (f32[192,1]{0,1:T(1,128)}, f32[192,1]{0,1:T(1,128)S(1)}, u32[]{:S(2)}) copy-start(f32[192,1]{0,1:T(1,128)S(1)} %get-tuple-element.113) | copy-start | bytes 2308
  105.3 5.0 %copy-start.8 = (f32[192,1]{0,1:T(1,128)}, f32[192,1]{0,1:T(1,128)S(1)}, u32[]{:S(2)}) copy-start(f32[192,1]{0,1:T(1,128)S(1)} %get-tuple-element.114) | copy-start | bytes 2308
  105.3 5.0 %copy-start.10 = (f32[192,1]{0,1:T(1,128)}, f32[192,1]{0,1:T(1,128)S(1)}, u32[]{:S(2)}) copy-start(f32[192,1]{0,1:T(1,128)S(1)} %get-tuple-element.115) | copy-start | bytes 2308
  105.3 5.0 %copy-start.12 = (f32[192,1]{0,1:T(1,128)}, f32[192,1]{0,1:T(1,128)S(1)}, u32[]{:S(2)}) copy-start(f32[192,1]{0,1:T(1,128)S(1)} %get-tuple-element.111) | copy-start | bytes 2308
  110.4 5.9 %copy-start.13 = (f32[192,1]{0,1:T(1,128)S(1)}, f32[192,1]{0,1:T(1,128)}, u32[]{:S(2)}) copy-start(f32[192,1]{0,1:T(1,128)} %copy-done.12) | copy-start | bytes 2308
  110.5 5.9 %copy-start.15 = (f32[192,1]{0,1:T(1,128)S(1)}, f32[192,1]{0,1:T(1,128)}, u32[]{:S(2)}) copy-start(f32[192,1]{0,1:T(1,128)} %copy-done.14) | copy-start | bytes 2308
  112.9 27.9 %copy-start.17 = (s32[192,1]{0,1:T(1,128)S(1)}, s32[192,1]{0,1:T(1,128)}, u32[]{:S(2)}) copy-start(s32[192,1]{0,1:T(1,128)} %copy-done.16) | copy-start | bytes 2308
  112.9 27.9 %copy-start.22 = (s32[192,1]{0,1:T(1,128)S(1)}, s32[192,1]{0,1:T(1,128)}, u32[]{:S(2)}) copy-start(s32[192,1]{0,1:T(1,128)} %get-tuple-element.103) | copy-start | bytes 2308
  112.9 28.3 %copy-start.5 = (f32[192,1]{0,1:T(1,128)S(1)}, f32[192,1]{0,1:T(1,128)}, u32[]{:S(2)}) copy-start(f32[192,1]{0,1:T(1,128)} %copy-done.4) | copy-start | bytes 2308
  112.9 28.3 %copy-start.7 = (f32[192,1]{0,1:T(1,128)S(1)}, f32[192,1]{0,1:T(1,128)}, u32[]{:S(2)}) copy-start(f32[192,1]{0,1:T(1,128)} %copy-done.6) | copy-start | bytes 2308
  112.9 28.3 %copy-start.9 = (f32[192,1]{0,1:T(1,128)S(1)}, f32[192,1]{0,1:T(1,128)}, u32[]{:S(2)}) copy-start(f32[192,1]{0,1:T(1,128)} %copy-done.8) | copy-start | bytes 2308
  112.9 28.3 %copy-start.11 = (f32[192,1]{0,1:T(1,128)S(1)}, f32[192,1]{0,1:T(1,128)}, u32[]{:S(2)}) copy-start(f32[192,1]{0,1:T(1,128)} %copy-done.10) | copy-start | bytes 2308
  118.0 46.9 %all-to-all-start.4 = ((bf16[32,8,128]{2,1,0:T(8,128)(2,1)}), bf16[32,8,128]{2,1,0:T(8,128)(2,1)S(1)}, u32[]{:S(2)}, u32[]{:S(2)}) async-start(bf16[32,8,128]{2,1,0:T(8,128)(2,1)} %pad_bitcast_fusion), calls=%async_computation.4 | async-start | bytes 131072 | tf_op jit(solution)/shard_map/all_to_all | solution.py:365
  162.4 6.1 %copy-start.19 = (f32[3,32]{1,0:T(4,128)S(1)}, f32[3,32]{1,0:T(4,128)}, u32[]{:S(2)}) copy-start(f32[3,32]{1,0:T(4,128)} %param.24) | copy-start | bytes 1156
  164.8 21.3 %all-to-all-start.2 = ((bf16[4,8,32,384]{3,2,1,0:T(8,128)(2,1)}), bf16[4,8,32,384]{3,2,1,0:T(8,128)(2,1)S(1)}, u32[]{:S(2)}, u32[]{:S(2)}) async-start(bf16[4,8,32,384]{3,2,1,0:T(8,128)(2,1)} %bitcast.113), calls=%async_computation.2 | async-start | bytes 1572864 | tf_op jit(solution)/shard_map/all_to_all | solution.py:223
  169.9 36.6 %copy-start.1 = (s32[6,8]{1,0:T(8,128)S(1)}, s32[6,8]{1,0:T(8,128)}, u32[]{:S(2)}) copy-start(s32[6,8]{1,0:T(8,128)} %add_add_fusion.1) | copy-start | bytes 580
  186.9 51.1 %all-to-all-start.3 = ((bf16[8,32,384]{2,1,0:T(8,128)(2,1)}), bf16[8,32,384]{2,1,0:T(8,128)(2,1)S(1)}, u32[]{:S(2)}, u32[]{:S(2)}) async-start(bf16[8,32,384]{2,1,0:T(8,128)(2,1)} %fusion.35), calls=%async_computation.3 | async-start | bytes 393216 | tf_op jit(solution)/shard_map/all_to_all | solution.py:223
  207.6 10.1 %collective-permute-start.6 = (f32[3,8,128]{2,0,1:T(4,128)S(1)}, f32[3,8,128]{2,0,1:T(4,128)S(1)}, u32[]{:S(2)}, u32[]{:S(2)}) collective-permute-start(f32[3,8,128]{2,0,1:T(4,128)S(1)} %copy.142), channel_id=1, source_target_pairs={{0,8},{8,16},{16,24},{24,32},{32,40},{40,48},{48,56},{56,64},{64,7... | collective-permute-start | bytes 36872 | tf_op jit(solution)/shard_map/ppermute | solution.py:379
  209.0 8.7 %collective-permute-start.7 = (f32[3,8,128]{2,0,1:T(4,128)S(1)}, f32[3,8,128]{2,0,1:T(4,128)S(1)}, u32[]{:S(2)}, u32[]{:S(2)}) collective-permute-start(f32[3,8,128]{2,0,1:T(4,128)S(1)} %copy.143), channel_id=1, source_target_pairs={{8,0},{16,8},{24,16},{32,24},{40,32},{48,40},{56,48},{64,56},{72,6... | collective-permute-start | bytes 36872 | tf_op jit(solution)/shard_map/ppermute | solution.py:380
  (6 other events, 21.5 us)

commit v4 on v3

--- a/solution.py
+++ b/solution.py
@@ -15,7 +15,8 @@
 ROW_BLOCK = 8
 LANES = 128
 GROUP = 8
-UNROLL = 4
+UNROLL = 8
+LEFT_OVER = 32
 NEAR = 4
 
 
@@ -39,25 +40,27 @@
     return jnp.clip(total, 0.0, 1.0)
 
 
-def column_kernel(ints, floats, pixels, out, tables):
+def column_kernel(ints, floats, described, pixels, copied, *refs):
     step = pl.program_id(0)
     slots, bands, rows, cols = pixels.shape
     blocks = cols // LANES
     edge = 16
     turn = ints[pl.num_programs(0) * slots]
-    parts = out.shape[0]
+    outs, (tables, turned) = refs[:-2], refs[-2:]
+    parts = len(outs)
     width = cols // parts
 
     @pl.when(step == 0)
     def _():
         tables[...] = jnp.zeros_like(tables)
+        copied[...] = described[...]
 
     def gap_base(first_row, count, offset):
         k = lax.broadcasted_iota(jnp.int32, (count, LANES), 0) + first_row
         j = lax.broadcasted_iota(jnp.int32, (count, LANES), 1)
         return j - k + offset
 
-    def one(slot, table):
+    def one(slot, table, ring):
         at = step * slots + slot
         shift = ints[at]
         weights = [floats[at * TAPS + tap] for tap in range(TAPS)]
@@ -80,35 +83,42 @@
                 table[high : high + edge, low:high] = lower
         source = pixels[slot].reshape(bands * rows, cols)
         warped = jnp.dot(source, table[...], preferred_element_type=jnp.float32)
-        warped = warped.astype(out.dtype)
+        warped = warped.astype(ring.dtype)
         for part in range(parts):
-            ahead = lax.rem(part - turn + parts, parts)
             for band in range(bands):
                 piece = warped[band * rows : (band + 1) * rows, part * width : (part + 1) * width]
-                out[ahead, slot, :, band * width : (band + 1) * width] = piece
+                ring[part, :, band * width : (band + 1) * width] = piece
+        for ahead in range(parts):
+            outs[ahead][slot] = ring[lax.rem(turn + ahead, parts)]
 
     def pair(index, carry):
         for half in range(2):
-            one(index * 2 + half, tables.at[half])
+            one(index * 2 + half, tables.at[half], turned.at[half])
         return carry
 
     lax.fori_loop(0, slots // 2, pair, 0)
 
 
-def warp_columns(pixels, shifts, taps, turn, parts):
+def warp_columns(pixels, shifts, taps, turn, parts, described):
     held, bands, rows, cols = pixels.shape
     width = bands * cols // parts
     return pl.pallas_call(
         column_kernel,
         grid=(held // GROUP,),
-        out_shape=jax.ShapeDtypeStruct((parts, held, rows, width), jnp.bfloat16),
+        out_shape=[jax.ShapeDtypeStruct(described.shape, described.dtype)]
+        + [jax.ShapeDtypeStruct((held, rows, width), jnp.bfloat16)] * parts,
         in_specs=[
             pl.BlockSpec(memory_space=pltpu.SMEM),
             pl.BlockSpec(memory_space=pltpu.SMEM),
+            pl.BlockSpec(described.shape, lambda g: (0, 0)),
             pl.BlockSpec((GROUP, bands, rows, cols), lambda g: (g, 0, 0, 0)),
         ],
-        out_specs=pl.BlockSpec((parts, GROUP, rows, width), lambda g: (0, g, 0, 0)),
-        scratch_shapes=[pltpu.VMEM((2, cols, cols), jnp.bfloat16)],
+        out_specs=[pl.BlockSpec(described.shape, lambda g: (0, 0))]
+        + [pl.BlockSpec((GROUP, rows, width), lambda g: (g, 0, 0))] * parts,
+        scratch_shapes=[
+            pltpu.VMEM((2, cols, cols), jnp.bfloat16),
+            pltpu.VMEM((2, parts, rows, width), jnp.bfloat16),
+        ],
         compiler_params=pltpu.CompilerParams(dimension_semantics=("arbitrary",)),
         cost_estimate=pl.CostEstimate(
             flops=2 * held * bands * rows * cols * cols,
@@ -116,17 +126,22 @@
             transcendentals=0,
         ),
         name="columns",
-    )(jnp.append(shifts, turn), taps.reshape(-1), pixels)
-
-
-def clip_kernel(ints, floats, plane, template, *refs):
-    groups, (out, framed, sums) = refs[:-3], refs[-3:]
+    )(jnp.append(shifts, turn), taps.reshape(-1), described, pixels)
+
+
+def clip_kernel(parts, turn, expand, template, *refs):
+    scalars, vectors, groups = refs[:parts], refs[parts : 2 * parts], refs[2 * parts : 3 * parts]
+    out, framed, sums, planes = refs[3 * parts :]
     slots, rows, width = groups[0].shape
     owners = out.shape[0]
     near = template.shape[0]
     bands = width // LANES
     canvas_rows = rows + 2 * MARGIN
-    total = len(groups) * slots
+    blocks = canvas_rows // ROW_BLOCK
+    cells = vectors[0].shape[1] - LEFT_OVER
+    at_taps, at_column_taps, at_scales = cells, cells + TAPS, cells + 2 * TAPS
+    at_start = at_scales + 3 * bands
+    cols = parts * LANES
     ends = framed.shape[0]
     framed[0:MARGIN, :] = jnp.zeros((MARGIN, width), jnp.float32)
     framed[ends - MARGIN : ends, :] = jnp.zeros((MARGIN, width), jnp.float32)
@@ -142,34 +157,51 @@
     lax.fori_loop(0, owners, fill, 0)
     sums[ends - 2 * MARGIN : ends, :] = jnp.zeros((2 * MARGIN, width), jnp.float32)
 
+    lane = lax.broadcasted_iota(jnp.int32, (slots, LANES), 1) + turn[0] * LANES
+    for group in range(parts):
+        described = vectors[group][...]
+        column = lane - described[:, at_start + 2 : at_start + 3].astype(jnp.int32)
+        covered = jnp.zeros((slots, LANES), jnp.float32)
+        for tap in range(TAPS):
+            source = column + (tap - 3)
+            inside = (source >= 0) & (source < cols)
+            weight = described[:, at_column_taps + tap : at_column_taps + tap + 1]
+            covered = covered + jnp.where(inside, weight, 0.0)
+        covered = jnp.clip(covered, 0.0, 1.0)
+        usable = jnp.dot(
+            described.astype(jnp.bfloat16), expand[...], preferred_element_type=jnp.float32
+        )
+        for block in range(blocks):
+            lanes = slice(block * LANES, (block + 1) * LANES)
+            planes[group * slots : (group + 1) * slots, lanes] = usable[:, lanes] * covered
+
     i = lax.broadcasted_iota(jnp.int32, (canvas_rows, LANES), 0)
     k = lax.broadcasted_iota(jnp.int32, (canvas_rows, LANES), 1)
     base = i - MARGIN - k
     ones = jnp.ones((rows, LANES), out.dtype)
 
     def one(group, slot):
-        columns = groups[group]
-        at = group * slots + slot
-        first = pl.multiple_of(ints[at], ROW_BLOCK)
-        gap = base - ints[total + at]
+        columns, values = groups[group], scalars[group]
+        first = pl.multiple_of(values[slot, at_start].astype(jnp.int32), ROW_BLOCK)
+        gap = base - values[slot, at_start + 1].astype(jnp.int32)
         table = jnp.zeros(gap.shape, jnp.float32)
-        per_slot = TAPS + 3 * bands
         for tap in range(TAPS):
-            table = jnp.where(gap == 3 - tap, floats[at * per_slot + tap], table)
+            table = jnp.where(gap == 3 - tap, values[slot, at_taps + tap], table)
         table = table.astype(columns.dtype)[:, :rows]
         source = jnp.concatenate([columns[slot], ones], axis=1)
         warped = jnp.dot(table, source, preferred_element_type=jnp.float32)
-        for block in range(canvas_rows // ROW_BLOCK):
+        plane = planes[pl.ds(group * slots + slot, 1), :]
+        for block in range(blocks):
             low = block * ROW_BLOCK
             where = pl.ds(first + low, ROW_BLOCK)
             row_cover = jnp.clip(warped[low : low + ROW_BLOCK, width:], 0.0, 1.0)
-            weight = row_cover * plane[at, block : block + 1, :]
+            weight = row_cover * plane[:, block * LANES : (block + 1) * LANES]
             for band in range(bands):
                 lanes = slice(band * LANES, (band + 1) * LANES)
+                scale = at_scales + 3 * band
                 prior = framed[where, lanes]
-                scale = at * per_slot + TAPS + 3 * band
-                pull = (warped[low : low + ROW_BLOCK, lanes] - prior) * floats[scale]
-                value = prior * floats[scale + 1] + jnp.tanh(pull) * floats[scale + 2]
+                pull = (warped[low : low + ROW_BLOCK, lanes] - prior) * values[slot, scale]
+                value = prior * values[slot, scale + 1] + jnp.tanh(pull) * values[slot, scale + 2]
                 sums[where, lanes] += weight * value
 
     def several(group, index, carry):
@@ -177,7 +209,7 @@
             one(group, index * UNROLL + part)
         return carry
 
-    for group in range(len(groups)):
+    for group in range(parts):
         lax.fori_loop(0, slots // UNROLL, functools.partial(several, group), 0)
 
     def give(owner, carry):
@@ -188,21 +220,23 @@
     lax.fori_loop(0, owners, give, 0)
 
 
-def clip_and_sum(ints, floats, columns, plane, template):
-    rows, width = columns[0].shape[1:]
-    tiles = plane.shape[0]
+def clip_and_sum(turn, expand, template, described, columns):
+    parts = len(columns)
+    slots, rows, width = columns[0].shape
+    tiles = parts * slots
     owners = template.shape[0] * template.shape[1]
     height = owners * rows + 2 * MARGIN
-    out_shape = (owners, rows, width)
+    scalar = pl.BlockSpec(memory_space=pltpu.SMEM)
+    vector = pl.BlockSpec(memory_space=pltpu.VMEM)
     return pl.pallas_call(
-        clip_kernel,
-        out_shape=jax.ShapeDtypeStruct(out_shape, jnp.bfloat16),
-        in_specs=[pl.BlockSpec(memory_space=pltpu.SMEM)] * 2
-        + [pl.BlockSpec(memory_space=pltpu.VMEM)] * (2 + len(columns)),
-        out_specs=pl.BlockSpec(memory_space=pltpu.VMEM),
+        functools.partial(clip_kernel, parts),
+        out_shape=jax.ShapeDtypeStruct((owners, rows, width), jnp.bfloat16),
+        in_specs=[scalar, vector, vector] + [scalar] * parts + [vector] * (2 * parts),
+        out_specs=vector,
         scratch_shapes=[
             pltpu.VMEM((height, width), jnp.float32),
             pltpu.VMEM((height, width), jnp.float32),
+            pltpu.VMEM((tiles, expand.shape[1]), jnp.float32),
         ],
         compiler_params=pltpu.CompilerParams(vmem_limit_bytes=32 * 1024 * 1024),
         cost_estimate=pl.CostEstimate(
@@ -211,7 +245,7 @@
             transcendentals=tiles * (rows + 2 * MARGIN) * width,
         ),
         name="clip",
-    )(ints, floats, plane, template, *columns)
+    )(turn, expand, template, *described, *described, *columns)
 
 
 def spread(index, block_count, block):
@@ -291,24 +325,77 @@
     sent = jnp.swapaxes(template_part, 0, 1).reshape(rows, bands * part_width)
     whole_template = gather_over_sky(sent)
 
+    target = slot_tile[:, 0]
+    sigmas = slot_sigma.astype(jnp.float32)
+    over = 1.0 / (sigmas * sigmas)
+    scale = CLIP_WIDTH * sigmas
+    scales = jnp.stack([1.0 / scale, over, scale * over], 2).reshape(held, 3 * bands)
+    taps = tap_weights(slot_frac.astype(jnp.float32))
     live = (jnp.arange(held, dtype=jnp.int32) < slot_count[0]).astype(jnp.float32)
+    masks = clip_mask.astype(jnp.float32) * live[:, None, None]
     described = jnp.concatenate(
         [
-            clip_mask.astype(jnp.float32).reshape(held, cells) * live[:, None],
+            masks.reshape(held, cells),
+            taps[:, 0],
+            taps[:, 1],
+            scales,
+            (target * rows).astype(jnp.float32)[:, None],
+            slot_offset.astype(jnp.float32),
+        ],
+        1,
+    )
+    described = jnp.pad(described, ((0, 0), (0, cells + LEFT_OVER - described.shape[1])))
+
+    described, *columns = warp_columns(
+        slot_pixels, slot_offset[:, 1], taps[:, 1], epoch_position, epoch_count, described
+    )
+    columns = from_epochs(columns)
+    described = from_epochs([described] * epoch_count)
+
+    row_index = jnp.arange(canvas_rows, dtype=jnp.int32) - MARGIN
+    col_index = epoch_position * part_width + jnp.arange(part_width, dtype=jnp.int32)
+    all_index = jnp.arange(cols, dtype=jnp.int32)
+    expand = spread(col_index, col_blocks, cols // col_blocks)
+    cell = jnp.arange(cells + LEFT_OVER, dtype=jnp.int32)[:, None, None]
+    of_row = cell // col_blocks == jnp.arange(row_blocks, dtype=jnp.int32)[None, :, None]
+    of_col = cell % col_blocks == (col_index // (cols // col_blocks))[None, None, :]
+    expand_cells = (of_row & of_col).astype(jnp.bfloat16).reshape(cells + LEFT_OVER, -1)
+
+    row_cover = cover(slot_offset[:, 0], taps[:, 0], row_index, rows)
+    col_cover = cover(slot_offset[:, 1], taps[:, 1], all_index, cols)
+    block_rows = row_cover.reshape(held, row_blocks, canvas_rows // row_blocks).sum(2)
+    block_cols = col_cover.reshape(held, col_blocks, cols // col_blocks).sum(2)
+    block = jnp.arange(row_blocks, dtype=jnp.int32)[None, :]
+    above = (target[:, None] == 0) & (block == 0)
+    below = (target[:, None] == sky_count - 1) & (block == row_blocks - 1)
+    block_rows = jnp.where(above | below, 0.0, block_rows)
+    tile_total = jnp.sum(masks * block_rows[:, :, None] * block_cols[:, None, :], (1, 2))
+    band_part = jnp.sum(tile_total[:, None] * over, 0)
+    band_part = band_part + jnp.sum(prior_weight, 1) * (cols / epoch_count)
+
+    facts = jnp.concatenate(
+        [
+            masks.reshape(held, cells),
             slot_offset.astype(jnp.float32),
             slot_frac.astype(jnp.float32),
-            slot_sigma.astype(jnp.float32),
-            slot_tile.astype(jnp.float32),
+            sigmas,
         ],
         1,
     )
-    described = jnp.pad(described, ((0, 0), (0, LANES - described.shape[1])))
-    described = jnp.concatenate(from_epochs([described] * epoch_count), 0)
-    tiles = described.shape[0]
-
-    taps_x = tap_weights(slot_frac[:, 1].astype(jnp.float32))
-    columns = warp_columns(slot_pixels, slot_offset[:, 1], taps_x, epoch_position, epoch_count)
-    columns = from_epochs(columns)
+    earlier = (target[:, None] == target[None, :]) & (
+        jnp.arange(held)[None, :] < jnp.arange(held)[:, None]
+    )
+    position = target * CAPACITY + jnp.sum(earlier.astype(jnp.int32), 1)
+    routes = jnp.arange(sky_count * CAPACITY, dtype=jnp.int32)
+    chooser = (position[None, :] == routes[:, None]).astype(jnp.float32)
+    chosen = jnp.dot(chooser, facts, precision=high)
+    totals = jnp.broadcast_to(band_part[None, :], (chosen.shape[0], bands))
+    message = jnp.concatenate([chosen, totals], 1)
+    message = jnp.pad(message, ((0, 0), (0, LANES - message.shape[1])))
+    message = message.reshape(sky_count, CAPACITY, LANES)
+    arrived = lax.all_to_all(message, "sky", split_axis=0, concat_axis=0, tiled=True)
+    arrived = jnp.concatenate(from_epochs([arrived] * epoch_count), 0)
+    band_total = jnp.sum(arrived[:, 0, cells + 4 + bands : cells + 4 + 2 * bands], 0)
 
     def unpack(table):
         masks = table[:, :cells].reshape(-1, row_blocks, col_blocks)
@@ -317,55 +404,6 @@
         sigmas = table[:, cells + 4 : cells + 4 + bands]
         sigmas = jnp.where(sigmas > 0.0, sigmas, 1.0)
         return masks, shifts, taps, sigmas
-
-    row_index = jnp.arange(canvas_rows, dtype=jnp.int32) - MARGIN
-    col_index = epoch_position * part_width + jnp.arange(part_width, dtype=jnp.int32)
-    all_index = jnp.arange(cols, dtype=jnp.int32)
-    expand = spread(col_index, col_blocks, cols // col_blocks)
-
-    masks, shifts, taps, sigmas = unpack(described)
-    target = described[:, cells + 4 + bands].astype(jnp.int32)
-    over = 1.0 / (sigmas * sigmas)
-    row_cover = cover(shifts[:, 0], taps[:, 0], row_index, rows)
-    col_cover = cover(shifts[:, 1], taps[:, 1], all_index, cols)
-    own_cover = lax.dynamic_slice_in_dim(col_cover, epoch_position * part_width, part_width, 1)
-    plane = jnp.einsum("sik,kj->sij", masks, expand, precision=high) * own_cover[:, None, :]
-    scale = CLIP_WIDTH * sigmas
-    scales = jnp.stack([1.0 / scale, over, scale * over], 2).reshape(tiles, 3 * bands)
-    floats = jnp.concatenate([taps[:, 0], scales], 1).reshape(-1)
-    ints = jnp.concatenate([target * rows, shifts[:, 0]])
-
-    block_rows = row_cover.reshape(tiles, row_blocks, canvas_rows // row_blocks).sum(2)
-    block_cols = col_cover.reshape(tiles, col_blocks, cols // col_blocks).sum(2)
-    block = jnp.arange(row_blocks, dtype=jnp.int32)[None, :]
-    above = (target[:, None] == 0) & (block == 0)
-    below = (target[:, None] == sky_count - 1) & (block == row_blocks - 1)
-    block_rows = jnp.where(above | below, 0.0, block_rows)
-    tile_total = jnp.sum(masks * block_rows[:, :, None] * block_cols[:, None, :], (1, 2))
-    band_part = jnp.sum(tile_total[:, None] * over, 0) + jnp.sum(prior_weight, 1) * cols
-
-    owners = jnp.arange(sky_count, dtype=jnp.int32)
-    onehot = (target[:, None] == owners[None, :]).astype(jnp.int32)
-    onehot = onehot.reshape(epoch_count, held, sky_count)
-    rank = jnp.sum(jnp.cumsum(onehot, 1) * onehot, 2) - 1
-    rank = rank + CAPACITY * jnp.arange(epoch_count, dtype=jnp.int32)[:, None]
-    routes = CAPACITY * epoch_count
-    position = target * routes + rank.reshape(-1)
-    slots = jnp.arange(sky_count * routes, dtype=jnp.int32)
-    chooser = (position[None, :] == slots[:, None]).astype(jnp.float32)
-    chosen = jnp.dot(chooser, described[:, : cells + 4 + bands], precision=high)
-    pieces = []
-    for _ in range(3):
-        pieces.append(lax.reduce_precision(band_part, 8, 7))
-        band_part = band_part - pieces[-1]
-    totals = jnp.broadcast_to(jnp.concatenate(pieces)[None, :], (chosen.shape[0], 3 * bands))
-    message = jnp.concatenate([chosen, totals], 1)
-    message = jnp.pad(message, ((0, 0), (0, LANES - message.shape[1]))).astype(jnp.bfloat16)
-    message = message.reshape(sky_count, routes, LANES)
-    arrived = lax.all_to_all(message, "sky", split_axis=0, concat_axis=0, tiled=True)
-    arrived = arrived.astype(jnp.float32)
-    totals = arrived[:, 0, cells + 4 + bands : cells + 4 + 4 * bands]
-    band_total = jnp.sum(totals.reshape(-1, bands), 0)
 
     own_masks, own_shift, own_taps, own_sigmas = unpack(arrived.reshape(-1, LANES))
     own_over = 1.0 / (own_sigmas * own_sigmas)
@@ -382,7 +420,7 @@
     weight_sum = weight_sum.at[:, :MARGIN].add(from_above)
     weight_sum = weight_sum.at[:, rows - MARGIN :].add(from_below)
 
-    partial = clip_and_sum(ints, floats, columns, plane, whole_template)
+    partial = clip_and_sum(epoch_position[None], expand_cells, whole_template, described, columns)
     flux = sum_over_sky(partial)
     flux_sum = jnp.swapaxes(flux.reshape(rows, bands, part_width), 0, 1)
 

time: 241 us -> 252 us (1.046)
  blocking collectives: 0 us -> 75.3 us
  starting transfers between devices: 118 us -> 58.3 us
  waiting for transfers between devices: 46.6 us -> 69.2 us
  other arithmetic: 27.1 us -> 4.75 us
    all_to_all x0 -> x1, blocking collectives: none -> 75.3 us  [to_all(): lax.all_to_all(copies, 'sky', split_axis=0, concat_axis=0, tiled=True, ax...]
    all_to_all x2 -> x1, starting transfers between devices: 49.2 us -> 6.14 us  [to_all(): lax.all_to_all(copies, 'sky', split_axis=0, concat_axis=0, tiled=True, ax...]
    ppermute x6 -> x9, waiting for transfers between devices: 0.02 us -> 38.1 us  [from_epochs(): arrived.append(lax.ppermute(pieces[ahead], 'epoch', route))]
    all_to_all x1, starting transfers between devices: 22.8 us -> 9.02 us  [on_device(): lax.all_to_all(message, 'sky', split_axis=0, concat_axis=0, tiled=True)]
    all_to_all x2, starting transfers between devices: 23.1 us -> 10.4 us  [summed_on_arrival(): lax.all_to_all(parts, axis, split_axis=0, concat_axis=0, tiled=True, axis...]
    all_to_all x2, waiting for transfers between devices: 36.4 us -> 24.8 us  [summed_on_arrival(): lax.all_to_all(parts, axis, split_axis=0, concat_axis=0, tiled=True, axis...]
    ppermute x6 -> x9, starting transfers between devices: 20.3 us -> 30.2 us  [from_epochs(): arrived.append(lax.ppermute(pieces[ahead], 'epoch', route))]
    squeeze x3 -> x1, local copies, waits for them, and re-layouts: 5.08 us -> 0.01 us  [on_device(): taps[:, 0]]
  transfers between devices with their start and end apart: 13 -> 15, of which waited for: 5 -> 6; matrix products, arithmetic and copies ran while one was open for 17% -> 5% of each run, Pallas kernels for 12% -> 11%
where the time goes in v4:
time: 252 us; the launch traced here: 249 us
  blocking collectives  75.3 us (30%)
  waiting for transfers between devices  69.2 us (27%)
  starting transfers between devices  58.3 us (23%)
  Pallas kernels  26.3 us (10%)
  local copies, waits for them, and re-layouts  11.7 us (5%)
  other arithmetic  4.75 us (2%)
    all_to_all x1, blocking collectives, to_all(): lax.all_to_all(copies, 'sky', split_axis=0, concat_axis=0, tiled=True, ax...  75.3 us
    ppermute x9, waiting for transfers between devices, from_epochs(): arrived.append(lax.ppermute(pieces[ahead], 'epoch', route))  38.1 us
    ppermute x9, starting transfers between devices, from_epochs(): arrived.append(lax.ppermute(pieces[ahead], 'epoch', route))  30.2 us
    all_to_all x2, waiting for transfers between devices, summed_on_arrival(): lax.all_to_all(parts, axis, split_axis=0, concat_axis=0, tiled=True, axis...  24.8 us
    pallas_call x1, Pallas kernels, clip_and_sum(): pl.pallas_call(functools.partial(clip_kernel, parts), out_shape=jax.Shape...  15.4 us
    pallas_call x1, Pallas kernels, warp_columns(): pl.pallas_call(column_kernel, grid=(held // GROUP,), out_shape=[jax.Shape...  10.9 us
    all_to_all x2, starting transfers between devices, summed_on_arrival(): lax.all_to_all(parts, axis, split_axis=0, concat_axis=0, tiled=True, axis...  10.4 us
    all_to_all x1, starting transfers between devices, on_device(): lax.all_to_all(message, 'sky', split_axis=0, concat_axis=0, tiled=True)  9.02 us
  transfers between devices with their start and end apart: 15, of which 6 were waited for; matrix products, arithmetic and copies ran while one was open for 5% of the time, Pallas kernels for 11%

profile of v4, /device:TPU:40, one launch (start us, length us, event | category | flops | bytes accessed | tf_op | source)
XLA Modules:
  0.0 248.9 jit_solution(6405144664420026552)
XLA Ops:
  0.7 0.9 copy-done
  1.6 75.3 %all_to_all.25 = bf16[8,32,384]{2,1,0:T(8,128)(2,1)S(1)} all-to-all(bf16[8,32,384]{2,1,0:T(8,128)(2,1)S(1)} %broadcast_in_dim.287), channel_id=1, replica_groups={{0,32,64,96,128,160,192,224},{8,40,72,104,136,168,200,232},{16,48,80,11..., dimensions={0} | all-to-all | bytes 393216 | tf_op jit(solution)/shard_map/all_to_all | solution.py:284
  76.9 1.0 broadcast_in_dim.288
  77.9 6.1 %all-to-all-start.1 = ((bf16[4,8,32,384]{3,2,1,0:T(8,128)(2,1)}), bf16[4,8,32,384]{3,2,1,0:T(8,128)(2,1)S(1)}, u32[]{:S(2)}, u32[]{:S(2)}) async-start(bf16[4,8,32,384]{3,2,1,0:T(8,128)(2,1)} %broadcast_in_dim.288), calls=%async_computation.1 | async-start | bytes 1572864 | tf_op jit(solution)/shard_map/all_to_all | solution.py:284
  88.7 10.9 %columns.1 = (f32[48,128]{1,0:T(8,128)}, bf16[48,32,384]{2,1,0:T(8,128)(2,1)}, bf16[48,32,384]{2,1,0:T(8,128)(2,1)}, bf16[48,32,384]{2,1,0:T(8,128)(2,1)}, bf16[48,32,384]{2,1,0:T(8,128)(2,1)}) custom-call(s32[49]{0:T(128)} %pad_add_fusion.ints, f32[288]{0:T(512)} %reshape_squeeze.3.floats, f32[48,128]{1,0:T(8,128)} %pad.12.described, ...), custom_call_target="tpu_custom_call" | custom-call | flops 2415919104 | bytes 9437184 | tf_op jit(solution)/shard_map/columns/pallas_call | solution.py:105
  99.6 3.6 %collective-permute-start = (f32[48,128]{1,0:T(8,128)}, f32[48,128]{1,0:T(8,128)S(1)}, u32[]{:S(2)}, u32[]{:S(2)}) collective-permute-start(f32[48,128]{1,0:T(8,128)} %get-tuple-element.33.refs_0_.refs_4_), channel_id=1, source_target_pairs={{0,2},{2,4},{4,6},{6,0},{1,3},{3,5},{5,7},{7,1},{8,10},{10,12},{12... | collective-permute-start | bytes 73736 | tf_op jit(solution)/shard_map/ppermute | solution.py:297
  103.2 4.8 %collective-permute-start.1 = (f32[48,128]{1,0:T(8,128)}, f32[48,128]{1,0:T(8,128)S(1)}, u32[]{:S(2)}, u32[]{:S(2)}) collective-permute-start(f32[48,128]{1,0:T(8,128)} %get-tuple-element.33.refs_0_.refs_4_), channel_id=1, source_target_pairs={{0,4},{2,6},{4,0},{6,2},{1,5},{3,7},{5,1},{7,3},{8,12},{10,14},{12... | collective-permute-start | bytes 73736 | tf_op jit(solution)/shard_map/ppermute | solution.py:297
  108.0 2.0 collective-permute-start.3
  110.0 4.6 %collective-permute-start.4 = (bf16[48,32,384]{2,1,0:T(8,128)(2,1)}, bf16[48,32,384]{2,1,0:T(8,128)(2,1)S(1)}, u32[]{:S(2)}, u32[]{:S(2)}) collective-permute-start(bf16[48,32,384]{2,1,0:T(8,128)(2,1)} %get-tuple-element.36), channel_id=1, source_target_pairs={{0,4},{2,6},{4,0},{6,2},{1,5},{3,7},{5,1},{7,3},{8,12},{10,14},{12... | collective-permute-start | bytes 3538952 | tf_op jit(solution)/shard_map/ppermute | solution.py:297
  114.6 2.5 %collective-permute-start.5 = (bf16[48,32,384]{2,1,0:T(8,128)(2,1)}, bf16[48,32,384]{2,1,0:T(8,128)(2,1)}, u32[]{:S(2)}, u32[]{:S(2)}) collective-permute-start(bf16[48,32,384]{2,1,0:T(8,128)(2,1)} %get-tuple-element.37), channel_id=1, source_target_pairs={{0,6},{2,0},{4,2},{6,4},{1,7},{3,1},{5,3},{7,5},{8,14},{10,8},{12,... | collective-permute-start | bytes 3538952 | tf_op jit(solution)/shard_map/ppermute | solution.py:297
  118.7 9.0 %all-to-all-start.4 = ((f32[32,2,128]{2,1,0:T(2,128)}), f32[32,2,128]{2,1,0:T(2,128)}, u32[]{:S(2)}, u32[]{:S(2)}) async-start(f32[32,2,128]{2,1,0:T(2,128)} %bitcast.19), calls=%async_computation.4 | async-start | bytes 65536 | tf_op jit(solution)/shard_map/all_to_all | solution.py:396
  127.8 2.8 %collective-permute-start.2 = (f32[48,128]{1,0:T(8,128)}, f32[48,128]{1,0:T(8,128)S(1)}, u32[]{:S(2)}, u32[]{:S(2)}) collective-permute-start(f32[48,128]{1,0:T(8,128)} %get-tuple-element.33.refs_0_.refs_4_), channel_id=1, source_target_pairs={{0,6},{2,0},{4,2},{6,4},{1,7},{3,1},{5,3},{7,5},{8,14},{10,8},{12,... | collective-permute-start | bytes 73736 | tf_op jit(solution)/shard_map/ppermute | solution.py:297
  130.5 0.7 and_convert_fusion
  131.3 1.1 copy.141.expand
  132.3 34.0 %collective-permute-done.2.refs_3_.refs_7_ = f32[48,128]{1,0:T(8,128)S(1)} collective-permute-done((f32[48,128]{1,0:T(8,128)}, f32[48,128]{1,0:T(8,128)S(1)}, u32[]{:S(2)}, u32[]{:S(2)}) %collective-permute-start.2) | collective-permute-done | bytes 24608 | tf_op jit(solution)/shard_map/ppermute | solution.py:297
  167.1 1.3 copy-done.2
  168.4 15.4 %clip.1 = bf16[32,32,384]{2,1,0:T(8,128)(2,1)S(1)} custom-call(s32[1]{0:T(128)} %bitcast.turn, bf16[128,768]{1,0:T(8,128)(2,1)S(1)} %copy.141.expand, bf16[4,8,32,384]{3,2,1,0:T(8,128)(2,1)S(1)} %all-to-all-done.1.template, f32[48,128]{1,0:T(8,128)S(1)} %copy-done.1, f32[48,128]{1,0:T(8,128)S(1)} %collective-permute-done.refs_1_.refs_5_, ...), custom_call_target="tpu_custom_call" | custom-call | flops 106168320 | bytes 4718592 | tf_op jit(solution)/shard_map/clip/pallas_call | solution.py:231
  183.9 1.0 copy.174
  184.8 4.8 %all-to-all-start.2 = ((bf16[4,8,32,384]{3,2,1,0:T(8,128)(2,1)}), bf16[4,8,32,384]{3,2,1,0:T(8,128)(2,1)S(1)}, u32[]{:S(2)}, u32[]{:S(2)}) async-start(bf16[4,8,32,384]{3,2,1,0:T(8,128)(2,1)} %bitcast.81), calls=%async_computation.2 | async-start | bytes 1572864 | tf_op jit(solution)/shard_map/all_to_all | solution.py:257
  189.8 2.2 collective-permute-start.6
  191.9 0.8 constant_dynamic-update-slice_fusion.3
  192.7 5.8 %collective-permute-start.7 = (f32[32,2,128]{2,1,0:T(2,128)}, f32[32,2,128]{2,1,0:T(2,128)S(1)}, u32[]{:S(2)}, u32[]{:S(2)}) collective-permute-start(f32[32,2,128]{2,1,0:T(2,128)} %all-to-all-done.4), channel_id=1, source_target_pairs={{0,4},{2,6},{4,0},{6,2},{1,5},{3,7},{5,1},{7,3},{8,12},{10,14},{12... | collective-permute-start | bytes 98312 | tf_op jit(solution)/shard_map/ppermute | solution.py:297
  198.5 2.0 collective-permute-start.8
  200.6 4.0 %collective-permute-done.8 = f32[32,2,128]{2,1,0:T(2,128)S(1)} collective-permute-done((f32[32,2,128]{2,1,0:T(2,128)}, f32[32,2,128]{2,1,0:T(2,128)S(1)}, u32[]{:S(2)}, u32[]{:S(2)}) %collective-permute-start.8) | collective-permute-done | bytes 32800 | tf_op jit(solution)/shard_map/ppermute | solution.py:297
  205.8 3.1 %all-to-all-done.2 = bf16[4,8,32,384]{3,2,1,0:T(8,128)(2,1)S(1)} async-done(((bf16[4,8,32,384]{3,2,1,0:T(8,128)(2,1)}), bf16[4,8,32,384]{3,2,1,0:T(8,128)(2,1)S(1)}, u32[]{:S(2)}, u32[]{:S(2)}) %all-to-all-start.2) | async-done | bytes 786464 | tf_op jit(solution)/shard_map/all_to_all | solution.py:257
  208.9 0.8 fusion.18
  209.7 5.5 %all-to-all-start.3 = ((bf16[8,32,384]{2,1,0:T(8,128)(2,1)}), bf16[8,32,384]{2,1,0:T(8,128)(2,1)S(1)}, u32[]{:S(2)}, u32[]{:S(2)}) async-start(bf16[8,32,384]{2,1,0:T(8,128)(2,1)} %fusion.18), calls=%async_computation.3 | async-start | bytes 393216 | tf_op jit(solution)/shard_map/all_to_all | solution.py:257
  215.7 0.8 convolution_bitcast_fusion.1
  216.6 1.3 collective-permute-start.9
  217.9 1.3 collective-permute-start.10
  219.5 6.3 %collective-permute-done.9 = f32[3,8,128]{2,0,1:T(4,128)S(1)} collective-permute-done((f32[3,8,128]{2,0,1:T(4,128)S(1)}, f32[3,8,128]{2,0,1:T(4,128)S(1)}, u32[]{:S(2)}, u32[]{:S(2)}) %collective-permute-start.9) | collective-permute-done | bytes 12320 | tf_op jit(solution)/shard_map/ppermute | solution.py:417
  225.8 21.7 %all-to-all-done.3 = bf16[8,32,384]{2,1,0:T(8,128)(2,1)S(1)} async-done(((bf16[8,32,384]{2,1,0:T(8,128)(2,1)}), bf16[8,32,384]{2,1,0:T(8,128)(2,1)S(1)}, u32[]{:S(2)}, u32[]{:S(2)}) %all-to-all-start.3) | async-done | bytes 196640 | tf_op jit(solution)/shard_map/all_to_all | solution.py:257
  (113 shorter events, 9.9 us)
Async XLA Ops:
  0.6 0.9 copy-start
  76.9 7.1 %copy-start.7 = (bf16[48,2]{0,1:T(2,128)(2,1)S(1)}, bf16[48,2]{0,1:T(2,128)(2,1)}, u32[]{:S(2)}) copy-start(bf16[48,2]{0,1:T(2,128)(2,1)} %param.18) | copy-start | bytes 580
  76.9 8.0 %copy-start.5 = (s32[48,2]{0,1:T(2,128)S(1)}, s32[48,2]{0,1:T(2,128)}, u32[]{:S(2)}) copy-start(s32[48,2]{0,1:T(2,128)} %param.17) | copy-start | bytes 1156
  77.9 8.1 %copy-start.8 = (s32[48,1]{0,1:T(1,128)S(1)}, s32[48,1]{0,1:T(1,128)}, u32[]{:S(2)}) copy-start(s32[48,1]{0,1:T(1,128)} %param.16) | copy-start | bytes 580
  77.9 8.2 %copy-start.3 = (s32[48,6,16]{0,2,1:T(8,128)S(1)}, s32[48,6,16]{0,2,1:T(8,128)}, u32[]{:S(2)}) copy-start(s32[48,6,16]{0,2,1:T(8,128)} %param.20) | copy-start | bytes 55300
  77.9 8.3 %copy-start.6 = (bf16[48,3]{0,1:T(4,128)(2,1)S(1)}, bf16[48,3]{0,1:T(4,128)(2,1)}, u32[]{:S(2)}) copy-start(bf16[48,3]{0,1:T(4,128)(2,1)} %param.19) | copy-start | bytes 868
  77.9 40.8 %all-to-all-start.1 = ((bf16[4,8,32,384]{3,2,1,0:T(8,128)(2,1)}), bf16[4,8,32,384]{3,2,1,0:T(8,128)(2,1)S(1)}, u32[]{:S(2)}, u32[]{:S(2)}) async-start(bf16[4,8,32,384]{3,2,1,0:T(8,128)(2,1)} %broadcast_in_dim.288), calls=%async_computation.1 | async-start | bytes 1572864 | tf_op jit(solution)/shard_map/all_to_all | solution.py:284
  88.7 28.6 %copy-start.4 = (f32[3,32]{1,0:T(4,128)S(1)}, f32[3,32]{1,0:T(4,128)}, u32[]{:S(2)}) copy-start(f32[3,32]{1,0:T(4,128)} %param.23) | copy-start | bytes 1156
  88.7 28.8 %copy-start.9 = (s32[48,1]{0,1:T(1,128)S(1)}, s32[48,1]{0,1:T(1,128)}, u32[]{:S(2)}) copy-start(s32[48,1]{0,1:T(1,128)} %param.16) | copy-start | bytes 580
  99.6 28.2 %collective-permute-start = (f32[48,128]{1,0:T(8,128)}, f32[48,128]{1,0:T(8,128)S(1)}, u32[]{:S(2)}, u32[]{:S(2)}) collective-permute-start(f32[48,128]{1,0:T(8,128)} %get-tuple-element.33.refs_0_.refs_4_), channel_id=1, source_target_pairs={{0,2},{2,4},{4,6},{6,0},{1,3},{3,5},{5,7},{7,1},{8,10},{10,12},{12... | collective-permute-start | bytes 73736 | tf_op jit(solution)/shard_map/ppermute | solution.py:297
  103.2 29.1 %collective-permute-start.1 = (f32[48,128]{1,0:T(8,128)}, f32[48,128]{1,0:T(8,128)S(1)}, u32[]{:S(2)}, u32[]{:S(2)}) collective-permute-start(f32[48,128]{1,0:T(8,128)} %get-tuple-element.33.refs_0_.refs_4_), channel_id=1, source_target_pairs={{0,4},{2,6},{4,0},{6,2},{1,5},{3,7},{5,1},{7,3},{8,12},{10,14},{12... | collective-permute-start | bytes 73736 | tf_op jit(solution)/shard_map/ppermute | solution.py:297
  108.0 58.4 %collective-permute-start.3 = (bf16[48,32,384]{2,1,0:T(8,128)(2,1)}, bf16[48,32,384]{2,1,0:T(8,128)(2,1)S(1)}, u32[]{:S(2)}, u32[]{:S(2)}) collective-permute-start(bf16[48,32,384]{2,1,0:T(8,128)(2,1)} %get-tuple-element.35), channel_id=1, source_target_pairs={{0,2},{2,4},{4,6},{6,0},{1,3},{3,5},{5,7},{7,1},{8,10},{10,12},{12... | collective-permute-start | bytes 3538952 | tf_op jit(solution)/shard_map/ppermute | solution.py:297
  110.0 56.4 %collective-permute-start.4 = (bf16[48,32,384]{2,1,0:T(8,128)(2,1)}, bf16[48,32,384]{2,1,0:T(8,128)(2,1)S(1)}, u32[]{:S(2)}, u32[]{:S(2)}) collective-permute-start(bf16[48,32,384]{2,1,0:T(8,128)(2,1)} %get-tuple-element.36), channel_id=1, source_target_pairs={{0,4},{2,6},{4,0},{6,2},{1,5},{3,7},{5,1},{7,3},{8,12},{10,14},{12... | collective-permute-start | bytes 3538952 | tf_op jit(solution)/shard_map/ppermute | solution.py:297
  114.6 51.8 %collective-permute-start.5 = (bf16[48,32,384]{2,1,0:T(8,128)(2,1)}, bf16[48,32,384]{2,1,0:T(8,128)(2,1)}, u32[]{:S(2)}, u32[]{:S(2)}) collective-permute-start(bf16[48,32,384]{2,1,0:T(8,128)(2,1)} %get-tuple-element.37), channel_id=1, source_target_pairs={{0,6},{2,0},{4,2},{6,4},{1,7},{3,1},{5,3},{7,5},{8,14},{10,8},{12,... | collective-permute-start | bytes 3538952 | tf_op jit(solution)/shard_map/ppermute | solution.py:297
  118.7 66.1 %all-to-all-start.4 = ((f32[32,2,128]{2,1,0:T(2,128)}), f32[32,2,128]{2,1,0:T(2,128)}, u32[]{:S(2)}, u32[]{:S(2)}) async-start(f32[32,2,128]{2,1,0:T(2,128)} %bitcast.19), calls=%async_computation.4 | async-start | bytes 65536 | tf_op jit(solution)/shard_map/all_to_all | solution.py:396
  127.8 38.6 %collective-permute-start.2 = (f32[48,128]{1,0:T(8,128)}, f32[48,128]{1,0:T(8,128)S(1)}, u32[]{:S(2)}, u32[]{:S(2)}) collective-permute-start(f32[48,128]{1,0:T(8,128)} %get-tuple-element.33.refs_0_.refs_4_), channel_id=1, source_target_pairs={{0,6},{2,0},{4,2},{6,4},{1,7},{3,1},{5,3},{7,5},{8,14},{10,8},{12,... | collective-permute-start | bytes 73736 | tf_op jit(solution)/shard_map/ppermute | solution.py:297
  166.4 0.7 copy-start.1
  167.1 1.3 copy-start.2
  184.8 24.1 %all-to-all-start.2 = ((bf16[4,8,32,384]{3,2,1,0:T(8,128)(2,1)}), bf16[4,8,32,384]{3,2,1,0:T(8,128)(2,1)S(1)}, u32[]{:S(2)}, u32[]{:S(2)}) async-start(bf16[4,8,32,384]{3,2,1,0:T(8,128)(2,1)} %bitcast.81), calls=%async_computation.2 | async-start | bytes 1572864 | tf_op jit(solution)/shard_map/all_to_all | solution.py:257
  189.8 10.7 %collective-permute-start.6 = (f32[32,2,128]{2,1,0:T(2,128)}, f32[32,2,128]{2,1,0:T(2,128)S(1)}, u32[]{:S(2)}, u32[]{:S(2)}) collective-permute-start(f32[32,2,128]{2,1,0:T(2,128)} %all-to-all-done.4), channel_id=1, source_target_pairs={{0,2},{2,4},{4,6},{6,0},{1,3},{3,5},{5,7},{7,1},{8,10},{10,12},{12... | collective-permute-start | bytes 98312 | tf_op jit(solution)/shard_map/ppermute | solution.py:297
  192.7 7.9 %collective-permute-start.7 = (f32[32,2,128]{2,1,0:T(2,128)}, f32[32,2,128]{2,1,0:T(2,128)S(1)}, u32[]{:S(2)}, u32[]{:S(2)}) collective-permute-start(f32[32,2,128]{2,1,0:T(2,128)} %all-to-all-done.4), channel_id=1, source_target_pairs={{0,4},{2,6},{4,0},{6,2},{1,5},{3,7},{5,1},{7,3},{8,12},{10,14},{12... | collective-permute-start | bytes 98312 | tf_op jit(solution)/shard_map/ppermute | solution.py:297
  198.5 6.0 %collective-permute-start.8 = (f32[32,2,128]{2,1,0:T(2,128)}, f32[32,2,128]{2,1,0:T(2,128)S(1)}, u32[]{:S(2)}, u32[]{:S(2)}) collective-permute-start(f32[32,2,128]{2,1,0:T(2,128)} %all-to-all-done.4), channel_id=1, source_target_pairs={{0,6},{2,0},{4,2},{6,4},{1,7},{3,1},{5,3},{7,5},{8,14},{10,8},{12,... | collective-permute-start | bytes 98312 | tf_op jit(solution)/shard_map/ppermute | solution.py:297
  209.7 37.8 %all-to-all-start.3 = ((bf16[8,32,384]{2,1,0:T(8,128)(2,1)}), bf16[8,32,384]{2,1,0:T(8,128)(2,1)S(1)}, u32[]{:S(2)}, u32[]{:S(2)}) async-start(bf16[8,32,384]{2,1,0:T(8,128)(2,1)} %fusion.18), calls=%async_computation.3 | async-start | bytes 393216 | tf_op jit(solution)/shard_map/all_to_all | solution.py:257
  216.6 9.2 %collective-permute-start.9 = (f32[3,8,128]{2,0,1:T(4,128)S(1)}, f32[3,8,128]{2,0,1:T(4,128)S(1)}, u32[]{:S(2)}, u32[]{:S(2)}) collective-permute-start(f32[3,8,128]{2,0,1:T(4,128)S(1)} %copy.164), channel_id=1, source_target_pairs={{0,8},{8,16},{16,24},{24,32},{32,40},{40,48},{48,56},{56,64},{64,7... | collective-permute-start | bytes 36872 | tf_op jit(solution)/shard_map/ppermute | solution.py:417
  217.9 7.9 %collective-permute-start.10 = (f32[3,8,128]{2,0,1:T(4,128)S(1)}, f32[3,8,128]{2,0,1:T(4,128)S(1)}, u32[]{:S(2)}, u32[]{:S(2)}) collective-permute-start(f32[3,8,128]{2,0,1:T(4,128)S(1)} %copy.165), channel_id=1, source_target_pairs={{8,0},{16,8},{24,16},{32,24},{40,32},{48,40},{56,48},{64,56},{72,6... | collective-permute-start | bytes 36872 | tf_op jit(solution)/shard_map/ppermute | solution.py:418

commit v5 on v4

--- a/solution.py
+++ b/solution.py
@@ -15,7 +15,8 @@
 ROW_BLOCK = 8
 LANES = 128
 GROUP = 8
-UNROLL = 8
+UNROLL = 12
+LAG = 4
 LEFT_OVER = 32
 NEAR = 4
 
@@ -40,7 +41,7 @@
     return jnp.clip(total, 0.0, 1.0)
 
 
-def column_kernel(ints, floats, described, pixels, copied, *refs):
+def column_kernel(ints, floats, pixels, *refs):
     step = pl.program_id(0)
     slots, bands, rows, cols = pixels.shape
     blocks = cols // LANES
@@ -53,7 +54,6 @@
     @pl.when(step == 0)
     def _():
         tables[...] = jnp.zeros_like(tables)
-        copied[...] = described[...]
 
     def gap_base(first_row, count, offset):
         k = lax.broadcasted_iota(jnp.int32, (count, LANES), 0) + first_row
@@ -91,33 +91,32 @@
         for ahead in range(parts):
             outs[ahead][slot] = ring[lax.rem(turn + ahead, parts)]
 
-    def pair(index, carry):
-        for half in range(2):
-            one(index * 2 + half, tables.at[half], turned.at[half])
+    lag = tables.shape[0]
+
+    def several(index, carry):
+        for part in range(lag):
+            one(index * lag + part, tables.at[part], turned.at[part])
         return carry
 
-    lax.fori_loop(0, slots // 2, pair, 0)
-
-
-def warp_columns(pixels, shifts, taps, turn, parts, described):
+    lax.fori_loop(0, slots // lag, several, 0)
+
+
+def warp_columns(pixels, shifts, taps, turn, parts):
     held, bands, rows, cols = pixels.shape
     width = bands * cols // parts
     return pl.pallas_call(
         column_kernel,
         grid=(held // GROUP,),
-        out_shape=[jax.ShapeDtypeStruct(described.shape, described.dtype)]
-        + [jax.ShapeDtypeStruct((held, rows, width), jnp.bfloat16)] * parts,
+        out_shape=[jax.ShapeDtypeStruct((held, rows, width), jnp.bfloat16)] * parts,
         in_specs=[
             pl.BlockSpec(memory_space=pltpu.SMEM),
             pl.BlockSpec(memory_space=pltpu.SMEM),
-            pl.BlockSpec(described.shape, lambda g: (0, 0)),
             pl.BlockSpec((GROUP, bands, rows, cols), lambda g: (g, 0, 0, 0)),
         ],
-        out_specs=[pl.BlockSpec(described.shape, lambda g: (0, 0))]
-        + [pl.BlockSpec((GROUP, rows, width), lambda g: (g, 0, 0))] * parts,
+        out_specs=[pl.BlockSpec((GROUP, rows, width), lambda g: (g, 0, 0))] * parts,
         scratch_shapes=[
-            pltpu.VMEM((2, cols, cols), jnp.bfloat16),
-            pltpu.VMEM((2, parts, rows, width), jnp.bfloat16),
+            pltpu.VMEM((LAG, cols, cols), jnp.bfloat16),
+            pltpu.VMEM((LAG, parts, rows, width), jnp.bfloat16),
         ],
         compiler_params=pltpu.CompilerParams(dimension_semantics=("arbitrary",)),
         cost_estimate=pl.CostEstimate(
@@ -126,15 +125,15 @@
             transcendentals=0,
         ),
         name="columns",
-    )(jnp.append(shifts, turn), taps.reshape(-1), described, pixels)
-
-
-def clip_kernel(parts, turn, expand, template, *refs):
+    )(jnp.append(shifts, turn), taps.reshape(-1), pixels)
+
+
+def clip_kernel(parts, near, turn, expand, *refs):
+    templates, refs = refs[:near], refs[near:]
     scalars, vectors, groups = refs[:parts], refs[parts : 2 * parts], refs[2 * parts : 3 * parts]
     out, framed, sums, planes = refs[3 * parts :]
     slots, rows, width = groups[0].shape
     owners = out.shape[0]
-    near = template.shape[0]
     bands = width // LANES
     canvas_rows = rows + 2 * MARGIN
     blocks = canvas_rows // ROW_BLOCK
@@ -146,15 +145,16 @@
     framed[0:MARGIN, :] = jnp.zeros((MARGIN, width), jnp.float32)
     framed[ends - MARGIN : ends, :] = jnp.zeros((MARGIN, width), jnp.float32)
 
-    def fill(owner, carry):
-        start = pl.multiple_of(owner * rows + MARGIN, MARGIN)
-        first = pl.multiple_of(owner * rows, rows)
-        block = template[lax.rem(owner, near), lax.div(owner, near)]
-        framed[pl.ds(start, rows), :] = block.astype(jnp.float32)
-        sums[pl.ds(first, rows), :] = jnp.zeros((rows, width), jnp.float32)
+    def fill(far, carry):
+        for behind in range(near):
+            owner = far * near + lax.rem(turn[1] - behind + near, near)
+            start = pl.multiple_of(owner * rows + MARGIN, MARGIN)
+            first = pl.multiple_of(owner * rows, rows)
+            framed[pl.ds(start, rows), :] = templates[behind][far].astype(jnp.float32)
+            sums[pl.ds(first, rows), :] = jnp.zeros((rows, width), jnp.float32)
         return carry
 
-    lax.fori_loop(0, owners, fill, 0)
+    lax.fori_loop(0, owners // near, fill, 0)
     sums[ends - 2 * MARGIN : ends, :] = jnp.zeros((2 * MARGIN, width), jnp.float32)
 
     lane = lax.broadcasted_iota(jnp.int32, (slots, LANES), 1) + turn[0] * LANES
@@ -220,18 +220,18 @@
     lax.fori_loop(0, owners, give, 0)
 
 
-def clip_and_sum(turn, expand, template, described, columns):
-    parts = len(columns)
+def clip_and_sum(turn, expand, templates, described, columns):
+    parts, near = len(columns), len(templates)
     slots, rows, width = columns[0].shape
     tiles = parts * slots
-    owners = template.shape[0] * template.shape[1]
+    owners = near * templates[0].shape[0]
     height = owners * rows + 2 * MARGIN
     scalar = pl.BlockSpec(memory_space=pltpu.SMEM)
     vector = pl.BlockSpec(memory_space=pltpu.VMEM)
     return pl.pallas_call(
-        functools.partial(clip_kernel, parts),
+        functools.partial(clip_kernel, parts, near),
         out_shape=jax.ShapeDtypeStruct((owners, rows, width), jnp.bfloat16),
-        in_specs=[scalar, vector, vector] + [scalar] * parts + [vector] * (2 * parts),
+        in_specs=[scalar] + [vector] * (1 + near) + [scalar] * parts + [vector] * (2 * parts),
         out_specs=vector,
         scratch_shapes=[
             pltpu.VMEM((height, width), jnp.float32),
@@ -245,7 +245,7 @@
             transcendentals=tiles * (rows + 2 * MARGIN) * width,
         ),
         name="clip",
-    )(turn, expand, template, *described, *described, *columns)
+    )(turn, expand, *templates, *described, *described, *columns)
 
 
 def spread(index, block_count, block):
@@ -278,15 +278,15 @@
 
 def gather_over_sky(shard):
     near, far, near_groups, far_groups = sky_groups()
-
-    def to_all(array, count, groups):
-        copies = jnp.broadcast_to(array[None], (count,) + array.shape)
-        return lax.all_to_all(
-            copies, "sky", split_axis=0, concat_axis=0, tiled=True, axis_index_groups=groups
-        )
-
-    shard = to_all(shard, far, far_groups)
-    return to_all(shard, near, near_groups)
+    copies = jnp.broadcast_to(shard[None], (far,) + shard.shape)
+    shards = lax.all_to_all(
+        copies, "sky", split_axis=0, concat_axis=0, tiled=True, axis_index_groups=far_groups
+    )
+    arrived = [shards]
+    for ahead in range(1, near):
+        route = [(g[i], g[(i + ahead) % near]) for g in near_groups for i in range(near)]
+        arrived.append(lax.ppermute(shards, "sky", route))
+    return arrived
 
 
 def from_epochs(pieces):
@@ -323,7 +323,7 @@
         template, epoch_position * part_width, part_width, 2
     )
     sent = jnp.swapaxes(template_part, 0, 1).reshape(rows, bands * part_width)
-    whole_template = gather_over_sky(sent)
+    templates = gather_over_sky(sent)
 
     target = slot_tile[:, 0]
     sigmas = slot_sigma.astype(jnp.float32)
@@ -346,9 +346,7 @@
     )
     described = jnp.pad(described, ((0, 0), (0, cells + LEFT_OVER - described.shape[1])))
 
-    described, *columns = warp_columns(
-        slot_pixels, slot_offset[:, 1], taps[:, 1], epoch_position, epoch_count, described
-    )
+    columns = warp_columns(slot_pixels, slot_offset[:, 1], taps[:, 1], epoch_position, epoch_count)
     columns = from_epochs(columns)
     described = from_epochs([described] * epoch_count)
 
@@ -420,7 +418,8 @@
     weight_sum = weight_sum.at[:, :MARGIN].add(from_above)
     weight_sum = weight_sum.at[:, rows - MARGIN :].add(from_below)
 
-    partial = clip_and_sum(epoch_position[None], expand_cells, whole_template, described, columns)
+    turn = jnp.stack([epoch_position, lax.axis_index("sky") % len(templates)])
+    partial = clip_and_sum(turn, expand_cells, templates, described, columns)
     flux = sum_over_sky(partial)
     flux_sum = jnp.swapaxes(flux.reshape(rows, bands, part_width), 0, 1)
 

time: 252 us -> 249 us (0.988)
  starting transfers between devices: 58.3 us -> 134 us
  blocking collectives: 75.3 us -> 0 us
  other arithmetic: 4.75 us -> 8.18 us
  Pallas kernels: 26.3 us -> 23.4 us
  waiting for transfers between devices: 69.2 us -> 66.4 us
    all_to_all x1 -> x0, blocking collectives: 75.3 us -> none  [to_all(): lax.all_to_all(copies, 'sky', split_axis=0, concat_axis=0, tiled=True, ax...]
    all_to_all x1, starting transfers between devices: 6.14 us -> 43.4 us  [gather_over_sky(): lax.all_to_all(copies, 'sky', split_axis=0, concat_axis=0, tiled=True, ax...]
    all_to_all x2, starting transfers between devices: 10.4 us -> 28.2 us  [summed_on_arrival(): lax.all_to_all(parts, axis, split_axis=0, concat_axis=0, tiled=True, axis...]
    ppermute x9, waiting for transfers between devices: 38.1 us -> 22 us  [from_epochs(): arrived.append(lax.ppermute(pieces[ahead], 'epoch', route))]
    ppermute x0 -> x3, starting transfers between devices: none -> 11.6 us  [gather_over_sky(): arrived.append(lax.ppermute(shards, 'sky', route))]
    all_to_all x1, starting transfers between devices: 9.02 us -> 17.2 us  [on_device(): lax.all_to_all(message, 'sky', split_axis=0, concat_axis=0, tiled=True)]
    all_to_all x1, waiting for transfers between devices: 0.01 us -> 6.81 us  [gather_over_sky(): lax.all_to_all(copies, 'sky', split_axis=0, concat_axis=0, tiled=True, ax...]
    ppermute x0 -> x3, waiting for transfers between devices: none -> 5.2 us  [gather_over_sky(): arrived.append(lax.ppermute(shards, 'sky', route))]
  transfers between devices with their start and end apart: 15 -> 18, of which waited for: 6 -> 9; matrix products, arithmetic and copies ran while one was open for 5% -> 4% of each run, Pallas kernels for 11% -> 9%
where the time goes in v5:
time: 249 us; the launch traced here: 247 us
  starting transfers between devices  134 us (54%)
  waiting for transfers between devices  66.4 us (27%)
  Pallas kernels  23.4 us (9%)
  local copies, waits for them, and re-layouts  11.2 us (4%)
  other arithmetic  8.18 us (3%)
    all_to_all x1, starting transfers between devices, gather_over_sky(): lax.all_to_all(copies, 'sky', split_axis=0, concat_axis=0, tiled=True, ax...  43.4 us
    ppermute x9, starting transfers between devices, from_epochs(): arrived.append(lax.ppermute(pieces[ahead], 'epoch', route))  31.3 us
    all_to_all x2, starting transfers between devices, summed_on_arrival(): lax.all_to_all(parts, axis, split_axis=0, concat_axis=0, tiled=True, axis...  28.2 us
    all_to_all x2, waiting for transfers between devices, summed_on_arrival(): lax.all_to_all(parts, axis, split_axis=0, concat_axis=0, tiled=True, axis...  23.1 us
    ppermute x9, waiting for transfers between devices, from_epochs(): arrived.append(lax.ppermute(pieces[ahead], 'epoch', route))  22 us
    all_to_all x1, starting transfers between devices, on_device(): lax.all_to_all(message, 'sky', split_axis=0, concat_axis=0, tiled=True)  17.2 us
    pallas_call x1, Pallas kernels, clip_and_sum(): pl.pallas_call(functools.partial(clip_kernel, parts, near), out_shape=jax...  14 us
    ppermute x3, starting transfers between devices, gather_over_sky(): arrived.append(lax.ppermute(shards, 'sky', route))  11.6 us
  transfers between devices with their start and end apart: 18, of which 9 were waited for; matrix products, arithmetic and copies ran while one was open for 4% of the time, Pallas kernels for 9%

profile of v5, /device:TPU:40, one launch (start us, length us, event | category | flops | bytes accessed | tf_op | source)
XLA Modules:
  0.0 247.1 jit_solution(1706005482716571703)
XLA Ops:
  6.1 0.8 multiply_reduce_fusion
  6.9 0.8 multiply_reduce_fusion.1
  8.2 3.6 %collective-permute-start.3 = (f32[48,128]{1,0:T(8,128)S(1)}, f32[48,128]{1,0:T(8,128)S(1)}, u32[]{:S(2)}, u32[]{:S(2)}) collective-permute-start(f32[48,128]{1,0:T(8,128)S(1)} %pad.12.refs_4_.refs_8_), channel_id=1, source_target_pairs={{0,2},{2,4},{4,6},{6,0},{1,3},{3,5},{5,7},{7,1},{8,10},{10,12},{12... | collective-permute-start | bytes 73736 | tf_op jit(solution)/shard_map/ppermute | solution.py:297
  11.7 4.9 %collective-permute-start.4 = (f32[48,128]{1,0:T(8,128)S(1)}, f32[48,128]{1,0:T(8,128)S(1)}, u32[]{:S(2)}, u32[]{:S(2)}) collective-permute-start(f32[48,128]{1,0:T(8,128)S(1)} %pad.12.refs_4_.refs_8_), channel_id=1, source_target_pairs={{0,4},{2,6},{4,0},{6,2},{1,5},{3,7},{5,1},{7,3},{8,12},{10,14},{12... | collective-permute-start | bytes 73736 | tf_op jit(solution)/shard_map/ppermute | solution.py:297
  18.1 43.4 %all-to-all-start = ((bf16[8,32,384]{2,1,0:T(8,128)(2,1)}), bf16[8,32,384]{2,1,0:T(8,128)(2,1)S(1)}, u32[]{:S(2)}, u32[]{:S(2)}) async-start(bf16[8,32,384]{2,1,0:T(8,128)(2,1)} %broadcast_in_dim.277), calls=%async_computation | async-start | bytes 393216 | tf_op jit(solution)/shard_map/all_to_all | solution.py:282
  62.9 9.4 %columns.1 = (bf16[48,32,384]{2,1,0:T(8,128)(2,1)}, bf16[48,32,384]{2,1,0:T(8,128)(2,1)}, bf16[48,32,384]{2,1,0:T(8,128)(2,1)}, bf16[48,32,384]{2,1,0:T(8,128)(2,1)}) custom-call(s32[49]{0:T(128)} %pad_add_fusion.1.ints, f32[288]{0:T(512)} %reshape_squeeze.3.floats, bf16[48,3,32,512]{3,2,1,0:T(8,128)(2,1)} %pixels.1), custom_call_target="tpu_custom_call" | custom-call | flops 2415919104 | bytes 9437184 | tf_op jit(solution)/shard_map/columns/pallas_call | solution.py:107
  72.3 1.9 collective-permute-start.6
  74.2 4.7 %collective-permute-start.7 = (bf16[48,32,384]{2,1,0:T(8,128)(2,1)}, bf16[48,32,384]{2,1,0:T(8,128)(2,1)S(1)}, u32[]{:S(2)}, u32[]{:S(2)}) collective-permute-start(bf16[48,32,384]{2,1,0:T(8,128)(2,1)} %get-tuple-element.34), channel_id=1, source_target_pairs={{0,4},{2,6},{4,0},{6,2},{1,5},{3,7},{5,1},{7,3},{8,12},{10,14},{12... | collective-permute-start | bytes 3538952 | tf_op jit(solution)/shard_map/ppermute | solution.py:297
  78.9 2.4 collective-permute-start.8
  82.3 2.8 %collective-permute-start.5 = (f32[48,128]{1,0:T(8,128)S(1)}, f32[48,128]{1,0:T(8,128)S(1)}, u32[]{:S(2)}, u32[]{:S(2)}) collective-permute-start(f32[48,128]{1,0:T(8,128)S(1)} %pad.12.refs_4_.refs_8_), channel_id=1, source_target_pairs={{0,6},{2,0},{4,2},{6,4},{1,7},{3,1},{5,3},{7,5},{8,14},{10,8},{12,... | collective-permute-start | bytes 73736 | tf_op jit(solution)/shard_map/ppermute | solution.py:297
  85.8 6.8 %all-to-all-done.refs_0_ = bf16[8,32,384]{2,1,0:T(8,128)(2,1)S(1)} async-done(((bf16[8,32,384]{2,1,0:T(8,128)(2,1)}), bf16[8,32,384]{2,1,0:T(8,128)(2,1)S(1)}, u32[]{:S(2)}, u32[]{:S(2)}) %all-to-all-start) | async-done | bytes 196640 | tf_op jit(solution)/shard_map/all_to_all | solution.py:282
  92.6 17.2 %all-to-all-start.3 = ((f32[32,2,128]{2,1,0:T(2,128)}), f32[32,2,128]{2,1,0:T(2,128)}, u32[]{:S(2)}, u32[]{:S(2)}) async-start(f32[32,2,128]{2,1,0:T(2,128)} %bitcast.20), calls=%async_computation.3 | async-start | bytes 65536 | tf_op jit(solution)/shard_map/all_to_all | solution.py:394
  109.8 3.3 %collective-permute-start = (bf16[8,32,384]{2,1,0:T(8,128)(2,1)S(1)}, bf16[8,32,384]{2,1,0:T(8,128)(2,1)S(1)}, u32[]{:S(2)}, u32[]{:S(2)}) collective-permute-start(bf16[8,32,384]{2,1,0:T(8,128)(2,1)S(1)} %all-to-all-done.refs_0_), channel_id=1, source_target_pairs={{0,8},{8,16},{16,24},{24,0},{32,40},{40,48},{48,56},{56,32},{64,72... | collective-permute-start | bytes 589832 | tf_op jit(solution)/shard_map/ppermute | solution.py:288
  113.0 17.9 %collective-permute-done.5.refs_7_.refs_11_ = f32[48,128]{1,0:T(8,128)S(1)} collective-permute-done((f32[48,128]{1,0:T(8,128)S(1)}, f32[48,128]{1,0:T(8,128)S(1)}, u32[]{:S(2)}, u32[]{:S(2)}) %collective-permute-start.5) | collective-permute-done | bytes 24608 | tf_op jit(solution)/shard_map/ppermute | solution.py:297
  130.9 5.1 %collective-permute-start.1 = (bf16[8,32,384]{2,1,0:T(8,128)(2,1)S(1)}, bf16[8,32,384]{2,1,0:T(8,128)(2,1)S(1)}, u32[]{:S(2)}, u32[]{:S(2)}) collective-permute-start(bf16[8,32,384]{2,1,0:T(8,128)(2,1)S(1)} %all-to-all-done.refs_0_), channel_id=1, source_target_pairs={{0,16},{8,24},{16,0},{24,8},{32,48},{40,56},{48,32},{56,40},{64,80... | collective-permute-start | bytes 589832 | tf_op jit(solution)/shard_map/ppermute | solution.py:288
  136.0 3.3 %collective-permute-start.2 = (bf16[8,32,384]{2,1,0:T(8,128)(2,1)S(1)}, bf16[8,32,384]{2,1,0:T(8,128)(2,1)S(1)}, u32[]{:S(2)}, u32[]{:S(2)}) collective-permute-start(bf16[8,32,384]{2,1,0:T(8,128)(2,1)S(1)} %all-to-all-done.refs_0_), channel_id=1, source_target_pairs={{0,24},{8,0},{16,8},{24,16},{32,56},{40,32},{48,40},{56,48},{64,88... | collective-permute-start | bytes 589832 | tf_op jit(solution)/shard_map/ppermute | solution.py:288
  140.0 1.1 copy.141.expand
  141.2 4.5 %collective-permute-done.1.refs_2_ = bf16[8,32,384]{2,1,0:T(8,128)(2,1)S(1)} collective-permute-done((bf16[8,32,384]{2,1,0:T(8,128)(2,1)S(1)}, bf16[8,32,384]{2,1,0:T(8,128)(2,1)S(1)}, u32[]{:S(2)}, u32[]{:S(2)}) %collective-permute-start.1) | collective-permute-done | bytes 196640 | tf_op jit(solution)/shard_map/ppermute | solution.py:288
  146.4 1.3 copy-done.1
  147.7 14.0 %clip.1 = bf16[32,32,384]{2,1,0:T(8,128)(2,1)S(1)} custom-call(s32[2]{0:T(128)S(1)} %pad_add_fusion.turn, bf16[128,768]{1,0:T(8,128)(2,1)S(1)} %copy.141.expand, bf16[8,32,384]{2,1,0:T(8,128)(2,1)S(1)} %all-to-all-done.refs_0_, bf16[8,32,384]{2,1,0:T(8,128)(2,1)S(1)} %collective-permute-done.refs_1_, bf16[8,32,384]{2,1,0:T(8,128)(2,1)S(1)} %collective-permute-done.1.refs_2_, ...), custom_call_target="tpu_custom_call" | custom-call | flops 106168320 | bytes 4718592 | tf_op jit(solution)/shard_map/clip/pallas_call | solution.py:231
  161.7 1.0 copy.174
  162.6 6.9 %all-to-all-start.1 = ((bf16[4,8,32,384]{3,2,1,0:T(8,128)(2,1)}), bf16[4,8,32,384]{3,2,1,0:T(8,128)(2,1)S(1)}, u32[]{:S(2)}, u32[]{:S(2)}) async-start(bf16[4,8,32,384]{3,2,1,0:T(8,128)(2,1)} %bitcast.82), calls=%async_computation.1 | async-start | bytes 1572864 | tf_op jit(solution)/shard_map/all_to_all | solution.py:257
  169.6 3.2 %collective-permute-start.9 = (f32[32,2,128]{2,1,0:T(2,128)}, f32[32,2,128]{2,1,0:T(2,128)S(1)}, u32[]{:S(2)}, u32[]{:S(2)}) collective-permute-start(f32[32,2,128]{2,1,0:T(2,128)} %all-to-all-done.3), channel_id=1, source_target_pairs={{0,2},{2,4},{4,6},{6,0},{1,3},{3,5},{5,7},{7,1},{8,10},{10,12},{12... | collective-permute-start | bytes 98312 | tf_op jit(solution)/shard_map/ppermute | solution.py:297
  173.6 5.8 %collective-permute-start.10 = (f32[32,2,128]{2,1,0:T(2,128)}, f32[32,2,128]{2,1,0:T(2,128)S(1)}, u32[]{:S(2)}, u32[]{:S(2)}) collective-permute-start(f32[32,2,128]{2,1,0:T(2,128)} %all-to-all-done.3), channel_id=1, source_target_pairs={{0,4},{2,6},{4,0},{6,2},{1,5},{3,7},{5,1},{7,3},{8,12},{10,14},{12... | collective-permute-start | bytes 98312 | tf_op jit(solution)/shard_map/ppermute | solution.py:297
  179.4 2.0 collective-permute-start.11
  181.5 4.0 %collective-permute-done.11 = f32[32,2,128]{2,1,0:T(2,128)S(1)} collective-permute-done((f32[32,2,128]{2,1,0:T(2,128)}, f32[32,2,128]{2,1,0:T(2,128)S(1)}, u32[]{:S(2)}, u32[]{:S(2)}) %collective-permute-start.11) | collective-permute-done | bytes 32800 | tf_op jit(solution)/shard_map/ppermute | solution.py:297
  186.7 3.1 %all-to-all-done.1 = bf16[4,8,32,384]{3,2,1,0:T(8,128)(2,1)S(1)} async-done(((bf16[4,8,32,384]{3,2,1,0:T(8,128)(2,1)}), bf16[4,8,32,384]{3,2,1,0:T(8,128)(2,1)S(1)}, u32[]{:S(2)}, u32[]{:S(2)}) %all-to-all-start.1) | async-done | bytes 786464 | tf_op jit(solution)/shard_map/all_to_all | solution.py:257
  190.6 21.4 %all-to-all-start.2 = ((bf16[8,32,384]{2,1,0:T(8,128)(2,1)}), bf16[8,32,384]{2,1,0:T(8,128)(2,1)S(1)}, u32[]{:S(2)}, u32[]{:S(2)}) async-start(bf16[8,32,384]{2,1,0:T(8,128)(2,1)} %fusion.18), calls=%async_computation.2 | async-start | bytes 393216 | tf_op jit(solution)/shard_map/all_to_all | solution.py:257
  213.3 1.3 collective-permute-start.12
  214.6 1.3 collective-permute-start.13
  216.2 9.4 %collective-permute-done.12 = f32[3,8,128]{2,0,1:T(4,128)S(1)} collective-permute-done((f32[3,8,128]{2,0,1:T(4,128)S(1)}, f32[3,8,128]{2,0,1:T(4,128)S(1)}, u32[]{:S(2)}, u32[]{:S(2)}) %collective-permute-start.12) | collective-permute-done | bytes 12320 | tf_op jit(solution)/shard_map/ppermute | solution.py:415
  225.7 20.0 %all-to-all-done.2 = bf16[8,32,384]{2,1,0:T(8,128)(2,1)S(1)} async-done(((bf16[8,32,384]{2,1,0:T(8,128)(2,1)}), bf16[8,32,384]{2,1,0:T(8,128)(2,1)S(1)}, u32[]{:S(2)}, u32[]{:S(2)}) %all-to-all-start.2) | async-done | bytes 196640 | tf_op jit(solution)/shard_map/all_to_all | solution.py:257
  (114 shorter events, 16.9 us)
Async XLA Ops:
  0.6 16.1 %copy-start = (bf16[3,32,512]{2,1,0:T(8,128)(2,1)S(1)}, bf16[3,32,512]{2,1,0:T(8,128)(2,1)}, u32[]{:S(2)}) copy-start(bf16[3,32,512]{2,1,0:T(8,128)(2,1)} %param.22) | copy-start | bytes 294916
  8.2 74.2 %collective-permute-start.3 = (f32[48,128]{1,0:T(8,128)S(1)}, f32[48,128]{1,0:T(8,128)S(1)}, u32[]{:S(2)}, u32[]{:S(2)}) collective-permute-start(f32[48,128]{1,0:T(8,128)S(1)} %pad.12.refs_4_.refs_8_), channel_id=1, source_target_pairs={{0,2},{2,4},{4,6},{6,0},{1,3},{3,5},{5,7},{7,1},{8,10},{10,12},{12... | collective-permute-start | bytes 73736 | tf_op jit(solution)/shard_map/ppermute | solution.py:297
  11.7 98.0 %collective-permute-start.4 = (f32[48,128]{1,0:T(8,128)S(1)}, f32[48,128]{1,0:T(8,128)S(1)}, u32[]{:S(2)}, u32[]{:S(2)}) collective-permute-start(f32[48,128]{1,0:T(8,128)S(1)} %pad.12.refs_4_.refs_8_), channel_id=1, source_target_pairs={{0,4},{2,6},{4,0},{6,2},{1,5},{3,7},{5,1},{7,3},{8,12},{10,14},{12... | collective-permute-start | bytes 73736 | tf_op jit(solution)/shard_map/ppermute | solution.py:297
  16.7 0.6 copy-start.2
  18.1 74.5 %all-to-all-start = ((bf16[8,32,384]{2,1,0:T(8,128)(2,1)}), bf16[8,32,384]{2,1,0:T(8,128)(2,1)S(1)}, u32[]{:S(2)}, u32[]{:S(2)}) async-start(bf16[8,32,384]{2,1,0:T(8,128)(2,1)} %broadcast_in_dim.277), calls=%async_computation | async-start | bytes 393216 | tf_op jit(solution)/shard_map/all_to_all | solution.py:282
  62.8 18.6 %copy-start.4 = (f32[3,32]{1,0:T(4,128)S(1)}, f32[3,32]{1,0:T(4,128)}, u32[]{:S(2)}) copy-start(f32[3,32]{1,0:T(4,128)} %param.23) | copy-start | bytes 1156
  62.8 18.7 %copy-start.7 = (s32[48,1]{0,1:T(1,128)S(1)}, s32[48,1]{0,1:T(1,128)}, u32[]{:S(2)}) copy-start(s32[48,1]{0,1:T(1,128)} %param.16) | copy-start | bytes 580
  62.8 18.9 %copy-start.6 = (bf16[48,2]{0,1:T(2,128)(2,1)S(1)}, bf16[48,2]{0,1:T(2,128)(2,1)}, u32[]{:S(2)}) copy-start(bf16[48,2]{0,1:T(2,128)(2,1)} %param.18) | copy-start | bytes 580
  62.8 19.0 %copy-start.5 = (bf16[48,3]{0,1:T(4,128)(2,1)S(1)}, bf16[48,3]{0,1:T(4,128)(2,1)}, u32[]{:S(2)}) copy-start(bf16[48,3]{0,1:T(4,128)(2,1)} %param.19) | copy-start | bytes 868
  72.3 63.8 %collective-permute-start.6 = (bf16[48,32,384]{2,1,0:T(8,128)(2,1)}, bf16[48,32,384]{2,1,0:T(8,128)(2,1)S(1)}, u32[]{:S(2)}, u32[]{:S(2)}) collective-permute-start(bf16[48,32,384]{2,1,0:T(8,128)(2,1)} %get-tuple-element.33), channel_id=1, source_target_pairs={{0,2},{2,4},{4,6},{6,0},{1,3},{3,5},{5,7},{7,1},{8,10},{10,12},{12... | collective-permute-start | bytes 3538952 | tf_op jit(solution)/shard_map/ppermute | solution.py:297
  74.2 67.0 %collective-permute-start.7 = (bf16[48,32,384]{2,1,0:T(8,128)(2,1)}, bf16[48,32,384]{2,1,0:T(8,128)(2,1)S(1)}, u32[]{:S(2)}, u32[]{:S(2)}) collective-permute-start(bf16[48,32,384]{2,1,0:T(8,128)(2,1)} %get-tuple-element.34), channel_id=1, source_target_pairs={{0,4},{2,6},{4,0},{6,2},{1,5},{3,7},{5,1},{7,3},{8,12},{10,14},{12... | collective-permute-start | bytes 3538952 | tf_op jit(solution)/shard_map/ppermute | solution.py:297
  78.9 62.3 %collective-permute-start.8 = (bf16[48,32,384]{2,1,0:T(8,128)(2,1)}, bf16[48,32,384]{2,1,0:T(8,128)(2,1)}, u32[]{:S(2)}, u32[]{:S(2)}) collective-permute-start(bf16[48,32,384]{2,1,0:T(8,128)(2,1)} %get-tuple-element.35), channel_id=1, source_target_pairs={{0,6},{2,0},{4,2},{6,4},{1,7},{3,1},{5,3},{7,5},{8,14},{10,8},{12,... | collective-permute-start | bytes 3538952 | tf_op jit(solution)/shard_map/ppermute | solution.py:297
  82.3 48.6 %collective-permute-start.5 = (f32[48,128]{1,0:T(8,128)S(1)}, f32[48,128]{1,0:T(8,128)S(1)}, u32[]{:S(2)}, u32[]{:S(2)}) collective-permute-start(f32[48,128]{1,0:T(8,128)S(1)} %pad.12.refs_4_.refs_8_), channel_id=1, source_target_pairs={{0,6},{2,0},{4,2},{6,4},{1,7},{3,1},{5,3},{7,5},{8,14},{10,8},{12,... | collective-permute-start | bytes 73736 | tf_op jit(solution)/shard_map/ppermute | solution.py:297
  92.6 70.1 %all-to-all-start.3 = ((f32[32,2,128]{2,1,0:T(2,128)}), f32[32,2,128]{2,1,0:T(2,128)}, u32[]{:S(2)}, u32[]{:S(2)}) async-start(f32[32,2,128]{2,1,0:T(2,128)} %bitcast.20), calls=%async_computation.3 | async-start | bytes 65536 | tf_op jit(solution)/shard_map/all_to_all | solution.py:394
  109.8 31.4 %collective-permute-start = (bf16[8,32,384]{2,1,0:T(8,128)(2,1)S(1)}, bf16[8,32,384]{2,1,0:T(8,128)(2,1)S(1)}, u32[]{:S(2)}, u32[]{:S(2)}) collective-permute-start(bf16[8,32,384]{2,1,0:T(8,128)(2,1)S(1)} %all-to-all-done.refs_0_), channel_id=1, source_target_pairs={{0,8},{8,16},{16,24},{24,0},{32,40},{40,48},{48,56},{56,32},{64,72... | collective-permute-start | bytes 589832 | tf_op jit(solution)/shard_map/ppermute | solution.py:288
  130.9 14.8 %collective-permute-start.1 = (bf16[8,32,384]{2,1,0:T(8,128)(2,1)S(1)}, bf16[8,32,384]{2,1,0:T(8,128)(2,1)S(1)}, u32[]{:S(2)}, u32[]{:S(2)}) collective-permute-start(bf16[8,32,384]{2,1,0:T(8,128)(2,1)S(1)} %all-to-all-done.refs_0_), channel_id=1, source_target_pairs={{0,16},{8,24},{16,0},{24,8},{32,48},{40,56},{48,32},{56,40},{64,80... | collective-permute-start | bytes 589832 | tf_op jit(solution)/shard_map/ppermute | solution.py:288
  136.0 10.3 %collective-permute-start.2 = (bf16[8,32,384]{2,1,0:T(8,128)(2,1)S(1)}, bf16[8,32,384]{2,1,0:T(8,128)(2,1)S(1)}, u32[]{:S(2)}, u32[]{:S(2)}) collective-permute-start(bf16[8,32,384]{2,1,0:T(8,128)(2,1)S(1)} %all-to-all-done.refs_0_), channel_id=1, source_target_pairs={{0,24},{8,0},{16,8},{24,16},{32,56},{40,32},{48,40},{56,48},{64,88... | collective-permute-start | bytes 589832 | tf_op jit(solution)/shard_map/ppermute | solution.py:288
  146.4 1.3 copy-start.1
  162.6 27.2 %all-to-all-start.1 = ((bf16[4,8,32,384]{3,2,1,0:T(8,128)(2,1)}), bf16[4,8,32,384]{3,2,1,0:T(8,128)(2,1)S(1)}, u32[]{:S(2)}, u32[]{:S(2)}) async-start(bf16[4,8,32,384]{3,2,1,0:T(8,128)(2,1)} %bitcast.82), calls=%async_computation.1 | async-start | bytes 1572864 | tf_op jit(solution)/shard_map/all_to_all | solution.py:257
  169.6 11.8 %collective-permute-start.9 = (f32[32,2,128]{2,1,0:T(2,128)}, f32[32,2,128]{2,1,0:T(2,128)S(1)}, u32[]{:S(2)}, u32[]{:S(2)}) collective-permute-start(f32[32,2,128]{2,1,0:T(2,128)} %all-to-all-done.3), channel_id=1, source_target_pairs={{0,2},{2,4},{4,6},{6,0},{1,3},{3,5},{5,7},{7,1},{8,10},{10,12},{12... | collective-permute-start | bytes 98312 | tf_op jit(solution)/shard_map/ppermute | solution.py:297
  173.6 7.9 %collective-permute-start.10 = (f32[32,2,128]{2,1,0:T(2,128)}, f32[32,2,128]{2,1,0:T(2,128)S(1)}, u32[]{:S(2)}, u32[]{:S(2)}) collective-permute-start(f32[32,2,128]{2,1,0:T(2,128)} %all-to-all-done.3), channel_id=1, source_target_pairs={{0,4},{2,6},{4,0},{6,2},{1,5},{3,7},{5,1},{7,3},{8,12},{10,14},{12... | collective-permute-start | bytes 98312 | tf_op jit(solution)/shard_map/ppermute | solution.py:297
  179.4 6.0 %collective-permute-start.11 = (f32[32,2,128]{2,1,0:T(2,128)}, f32[32,2,128]{2,1,0:T(2,128)S(1)}, u32[]{:S(2)}, u32[]{:S(2)}) collective-permute-start(f32[32,2,128]{2,1,0:T(2,128)} %all-to-all-done.3), channel_id=1, source_target_pairs={{0,6},{2,0},{4,2},{6,4},{1,7},{3,1},{5,3},{7,5},{8,14},{10,8},{12,... | collective-permute-start | bytes 98312 | tf_op jit(solution)/shard_map/ppermute | solution.py:297
  190.6 55.1 %all-to-all-start.2 = ((bf16[8,32,384]{2,1,0:T(8,128)(2,1)}), bf16[8,32,384]{2,1,0:T(8,128)(2,1)S(1)}, u32[]{:S(2)}, u32[]{:S(2)}) async-start(bf16[8,32,384]{2,1,0:T(8,128)(2,1)} %fusion.18), calls=%async_computation.2 | async-start | bytes 393216 | tf_op jit(solution)/shard_map/all_to_all | solution.py:257
  212.5 33.2 %copy-start.3 = (bf16[3,32,128]{2,1,0:T(8,128)(2,1)S(1)}, bf16[3,32,128]{2,1,0:T(8,128)(2,1)}, u32[]{:S(2)}) copy-start(bf16[3,32,128]{2,1,0:T(8,128)(2,1)} %copy-done.2) | copy-start | bytes 73732
  213.3 12.3 %collective-permute-start.12 = (f32[3,8,128]{2,0,1:T(4,128)S(1)}, f32[3,8,128]{2,0,1:T(4,128)S(1)}, u32[]{:S(2)}, u32[]{:S(2)}) collective-permute-start(f32[3,8,128]{2,0,1:T(4,128)S(1)} %copy.164), channel_id=1, source_target_pairs={{0,8},{8,16},{16,24},{24,32},{32,40},{40,48},{48,56},{56,64},{64,7... | collective-permute-start | bytes 36872 | tf_op jit(solution)/shard_map/ppermute | solution.py:415
  214.6 11.0 %collective-permute-start.13 = (f32[3,8,128]{2,0,1:T(4,128)S(1)}, f32[3,8,128]{2,0,1:T(4,128)S(1)}, u32[]{:S(2)}, u32[]{:S(2)}) collective-permute-start(f32[3,8,128]{2,0,1:T(4,128)S(1)} %copy.165), channel_id=1, source_target_pairs={{8,0},{16,8},{24,16},{32,24},{40,32},{48,40},{56,48},{64,56},{72,6... | collective-permute-start | bytes 36872 | tf_op jit(solution)/shard_map/ppermute | solution.py:416

commit v6 on v5

--- a/solution.py
+++ b/solution.py
@@ -41,7 +41,7 @@
     return jnp.clip(total, 0.0, 1.0)
 
 
-def column_kernel(ints, floats, pixels, *refs):
+def column_kernel(ints, floats, facts, pixels, *refs):
     step = pl.program_id(0)
     slots, bands, rows, cols = pixels.shape
     blocks = cols // LANES
@@ -54,6 +54,9 @@
     @pl.when(step == 0)
     def _():
         tables[...] = jnp.zeros_like(tables)
+        for piece in outs:
+            piece[piece.shape[0] - 1, 0 : facts.shape[0], :] = facts[...]
+            piece[piece.shape[0] - 1, facts.shape[0] :, :] = jnp.zeros_like(facts)
 
     def gap_base(first_row, count, offset):
         k = lax.broadcasted_iota(jnp.int32, (count, LANES), 0) + first_row
@@ -89,7 +92,7 @@
                 piece = warped[band * rows : (band + 1) * rows, part * width : (part + 1) * width]
                 ring[part, :, band * width : (band + 1) * width] = piece
         for ahead in range(parts):
-            outs[ahead][slot] = ring[lax.rem(turn + ahead, parts)]
+            outs[ahead][at] = ring[lax.rem(turn + ahead, parts)]
 
     lag = tables.shape[0]
 
@@ -101,19 +104,20 @@
     lax.fori_loop(0, slots // lag, several, 0)
 
 
-def warp_columns(pixels, shifts, taps, turn, parts):
+def warp_columns(pixels, shifts, taps, turn, parts, facts):
     held, bands, rows, cols = pixels.shape
     width = bands * cols // parts
     return pl.pallas_call(
         column_kernel,
         grid=(held // GROUP,),
-        out_shape=[jax.ShapeDtypeStruct((held, rows, width), jnp.bfloat16)] * parts,
+        out_shape=[jax.ShapeDtypeStruct((held + 1, rows, width), jnp.bfloat16)] * parts,
         in_specs=[
             pl.BlockSpec(memory_space=pltpu.SMEM),
             pl.BlockSpec(memory_space=pltpu.SMEM),
+            pl.BlockSpec(facts.shape, lambda g: (0, 0)),
             pl.BlockSpec((GROUP, bands, rows, cols), lambda g: (g, 0, 0, 0)),
         ],
-        out_specs=[pl.BlockSpec((GROUP, rows, width), lambda g: (g, 0, 0))] * parts,
+        out_specs=[pl.BlockSpec((held + 1, rows, width), lambda g: (0, 0, 0))] * parts,
         scratch_shapes=[
             pltpu.VMEM((LAG, cols, cols), jnp.bfloat16),
             pltpu.VMEM((LAG, parts, rows, width), jnp.bfloat16),
@@ -125,22 +129,39 @@
             transcendentals=0,
         ),
         name="columns",
-    )(jnp.append(shifts, turn), taps.reshape(-1), pixels)
+    )(jnp.append(shifts, turn), taps.reshape(-1), facts, pixels)
 
 
 def clip_kernel(parts, near, turn, expand, *refs):
     templates, refs = refs[:near], refs[near:]
-    scalars, vectors, groups = refs[:parts], refs[parts : 2 * parts], refs[2 * parts : 3 * parts]
-    out, framed, sums, planes = refs[3 * parts :]
+    groups = refs[:parts]
+    out, framed, sums, planes, vectors, scalars, arrival = refs[parts:]
     slots, rows, width = groups[0].shape
+    slots -= 1
     owners = out.shape[0]
     bands = width // LANES
     canvas_rows = rows + 2 * MARGIN
     blocks = canvas_rows // ROW_BLOCK
-    cells = vectors[0].shape[1] - LEFT_OVER
+    cells = vectors.shape[1] - LEFT_OVER
     at_taps, at_column_taps, at_scales = cells, cells + TAPS, cells + 2 * TAPS
     at_start = at_scales + 3 * bands
+    at_sigmas = at_start + 3
     cols = parts * LANES
+
+    share = slots // bands
+    place = lax.broadcasted_iota(jnp.int32, (share, LANES), 1)
+    for group in range(parts):
+        for third in range(bands):
+            lanes = slice(third * LANES, (third + 1) * LANES)
+            facts = groups[group][slots, 0:share, lanes].astype(jnp.float32)
+            for band in range(bands):
+                sigma = facts[:, at_sigmas + band : at_sigmas + band + 1]
+                scale = CLIP_WIDTH * sigma
+                over = 1.0 / (sigma * sigma)
+                for number, value in enumerate((1.0 / scale, over, scale * over)):
+                    facts = jnp.where(place == at_scales + 3 * band + number, value, facts)
+            low = group * slots + third * share
+            vectors[low : low + share, :] = facts
     ends = framed.shape[0]
     framed[0:MARGIN, :] = jnp.zeros((MARGIN, width), jnp.float32)
     framed[ends - MARGIN : ends, :] = jnp.zeros((MARGIN, width), jnp.float32)
@@ -159,7 +180,7 @@
 
     lane = lax.broadcasted_iota(jnp.int32, (slots, LANES), 1) + turn[0] * LANES
     for group in range(parts):
-        described = vectors[group][...]
+        described = vectors[group * slots : (group + 1) * slots, :]
         column = lane - described[:, at_start + 2 : at_start + 3].astype(jnp.int32)
         covered = jnp.zeros((slots, LANES), jnp.float32)
         for tap in range(TAPS):
@@ -175,22 +196,26 @@
             lanes = slice(block * LANES, (block + 1) * LANES)
             planes[group * slots : (group + 1) * slots, lanes] = usable[:, lanes] * covered
 
+    copy = pltpu.make_async_copy(vectors, scalars, arrival)
+    copy.start()
+    copy.wait()
+
     i = lax.broadcasted_iota(jnp.int32, (canvas_rows, LANES), 0)
     k = lax.broadcasted_iota(jnp.int32, (canvas_rows, LANES), 1)
     base = i - MARGIN - k
     ones = jnp.ones((rows, LANES), out.dtype)
 
     def one(group, slot):
-        columns, values = groups[group], scalars[group]
-        first = pl.multiple_of(values[slot, at_start].astype(jnp.int32), ROW_BLOCK)
-        gap = base - values[slot, at_start + 1].astype(jnp.int32)
+        columns, at = groups[group], group * slots + slot
+        first = pl.multiple_of(scalars[at, at_start].astype(jnp.int32), ROW_BLOCK)
+        gap = base - scalars[at, at_start + 1].astype(jnp.int32)
         table = jnp.zeros(gap.shape, jnp.float32)
         for tap in range(TAPS):
-            table = jnp.where(gap == 3 - tap, values[slot, at_taps + tap], table)
+            table = jnp.where(gap == 3 - tap, scalars[at, at_taps + tap], table)
         table = table.astype(columns.dtype)[:, :rows]
         source = jnp.concatenate([columns[slot], ones], axis=1)
         warped = jnp.dot(table, source, preferred_element_type=jnp.float32)
-        plane = planes[pl.ds(group * slots + slot, 1), :]
+        plane = planes[pl.ds(at, 1), :]
         for block in range(blocks):
             low = block * ROW_BLOCK
             where = pl.ds(first + low, ROW_BLOCK)
@@ -200,8 +225,8 @@
                 lanes = slice(band * LANES, (band + 1) * LANES)
                 scale = at_scales + 3 * band
                 prior = framed[where, lanes]
-                pull = (warped[low : low + ROW_BLOCK, lanes] - prior) * values[slot, scale]
-                value = prior * values[slot, scale + 1] + jnp.tanh(pull) * values[slot, scale + 2]
+                pull = (warped[low : low + ROW_BLOCK, lanes] - prior) * scalars[at, scale]
+                value = prior * scalars[at, scale + 1] + jnp.tanh(pull) * scalars[at, scale + 2]
                 sums[where, lanes] += weight * value
 
     def several(group, index, carry):
@@ -220,10 +245,10 @@
     lax.fori_loop(0, owners, give, 0)
 
 
-def clip_and_sum(turn, expand, templates, described, columns):
+def clip_and_sum(turn, expand, templates, columns):
     parts, near = len(columns), len(templates)
     slots, rows, width = columns[0].shape
-    tiles = parts * slots
+    tiles = parts * (slots - 1)
     owners = near * templates[0].shape[0]
     height = owners * rows + 2 * MARGIN
     scalar = pl.BlockSpec(memory_space=pltpu.SMEM)
@@ -231,12 +256,15 @@
     return pl.pallas_call(
         functools.partial(clip_kernel, parts, near),
         out_shape=jax.ShapeDtypeStruct((owners, rows, width), jnp.bfloat16),
-        in_specs=[scalar] + [vector] * (1 + near) + [scalar] * parts + [vector] * (2 * parts),
+        in_specs=[scalar] + [vector] * (1 + near + parts),
         out_specs=vector,
         scratch_shapes=[
             pltpu.VMEM((height, width), jnp.float32),
             pltpu.VMEM((height, width), jnp.float32),
             pltpu.VMEM((tiles, expand.shape[1]), jnp.float32),
+            pltpu.VMEM((tiles, expand.shape[0]), jnp.float32),
+            pltpu.SMEM((tiles, expand.shape[0]), jnp.float32),
+            pltpu.SemaphoreType.DMA,
         ],
         compiler_params=pltpu.CompilerParams(vmem_limit_bytes=32 * 1024 * 1024),
         cost_estimate=pl.CostEstimate(
@@ -245,7 +273,7 @@
             transcendentals=tiles * (rows + 2 * MARGIN) * width,
         ),
         name="clip",
-    )(turn, expand, *templates, *described, *described, *columns)
+    )(turn, expand, *templates, *columns)
 
 
 def spread(index, block_count, block):
@@ -328,8 +356,6 @@
     target = slot_tile[:, 0]
     sigmas = slot_sigma.astype(jnp.float32)
     over = 1.0 / (sigmas * sigmas)
-    scale = CLIP_WIDTH * sigmas
-    scales = jnp.stack([1.0 / scale, over, scale * over], 2).reshape(held, 3 * bands)
     taps = tap_weights(slot_frac.astype(jnp.float32))
     live = (jnp.arange(held, dtype=jnp.int32) < slot_count[0]).astype(jnp.float32)
     masks = clip_mask.astype(jnp.float32) * live[:, None, None]
@@ -338,17 +364,21 @@
             masks.reshape(held, cells),
             taps[:, 0],
             taps[:, 1],
-            scales,
+            jnp.zeros((held, 3 * bands), jnp.float32),
             (target * rows).astype(jnp.float32)[:, None],
             slot_offset.astype(jnp.float32),
+            sigmas,
         ],
         1,
     )
     described = jnp.pad(described, ((0, 0), (0, cells + LEFT_OVER - described.shape[1])))
-
-    columns = warp_columns(slot_pixels, slot_offset[:, 1], taps[:, 1], epoch_position, epoch_count)
+    described = described.astype(jnp.bfloat16).reshape(bands, held // bands, -1)
+    described = jnp.swapaxes(described, 0, 1).reshape(held // bands, -1)
+
+    columns = warp_columns(
+        slot_pixels, slot_offset[:, 1], taps[:, 1], epoch_position, epoch_count, described
+    )
     columns = from_epochs(columns)
-    described = from_epochs([described] * epoch_count)
 
     row_index = jnp.arange(canvas_rows, dtype=jnp.int32) - MARGIN
     col_index = epoch_position * part_width + jnp.arange(part_width, dtype=jnp.int32)
@@ -419,7 +449,7 @@
     weight_sum = weight_sum.at[:, rows - MARGIN :].add(from_below)
 
     turn = jnp.stack([epoch_position, lax.axis_index("sky") % len(templates)])
-    partial = clip_and_sum(turn, expand_cells, templates, described, columns)
+    partial = clip_and_sum(turn, expand_cells, templates, columns)
     flux = sum_over_sky(partial)
     flux_sum = jnp.swapaxes(flux.reshape(rows, bands, part_width), 0, 1)
 

time: 249 us -> 237 us (0.952)
  starting transfers between devices: 134 us -> 112 us
  waiting for transfers between devices: 66.4 us -> 75.9 us
    all_to_all x1, waiting for transfers between devices: 6.81 us -> 28.9 us  [gather_over_sky(): lax.all_to_all(copies, 'sky', split_axis=0, concat_axis=0, tiled=True, ax...]
    ppermute x9 -> x6, waiting for transfers between devices: 22 us -> 2.53 us  [from_epochs(): arrived.append(lax.ppermute(pieces[ahead], 'epoch', route))]
    ppermute x9 -> x6, starting transfers between devices: 31.3 us -> 20.9 us  [from_epochs(): arrived.append(lax.ppermute(pieces[ahead], 'epoch', route))]
    all_to_all x1, starting transfers between devices: 17.2 us -> 8.93 us  [on_device(): lax.all_to_all(message, 'sky', split_axis=0, concat_axis=0, tiled=True)]
    all_to_all x2, waiting for transfers between devices: 23.1 us -> 27.7 us  [summed_on_arrival(): lax.all_to_all(parts, axis, split_axis=0, concat_axis=0, tiled=True, axis...]
    all_to_all x2, starting transfers between devices: 28.2 us -> 25.4 us  [summed_on_arrival(): lax.all_to_all(parts, axis, split_axis=0, concat_axis=0, tiled=True, axis...]
    ppermute x3, waiting for transfers between devices: 5.2 us -> 7.9 us  [gather_over_sky(): arrived.append(lax.ppermute(shards, 'sky', route))]
  transfers between devices with their start and end apart: 18 -> 15, of which waited for: 9 -> 7; matrix products, arithmetic and copies ran while one was open for 4% -> 4% of each run, Pallas kernels for 9% -> 7%
where the time goes in v6:
time: 237 us; the launch traced here: 236 us
  starting transfers between devices  112 us (47%)
  waiting for transfers between devices  75.9 us (32%)
  Pallas kernels  25.5 us (11%)
  local copies, waits for them, and re-layouts  10.8 us (5%)
  other arithmetic  8.16 us (3%)
    all_to_all x1, starting transfers between devices, gather_over_sky(): lax.all_to_all(copies, 'sky', split_axis=0, concat_axis=0, tiled=True, ax...  43.4 us
    all_to_all x1, waiting for transfers between devices, gather_over_sky(): lax.all_to_all(copies, 'sky', split_axis=0, concat_axis=0, tiled=True, ax...  28.9 us
    all_to_all x2, waiting for transfers between devices, summed_on_arrival(): lax.all_to_all(parts, axis, split_axis=0, concat_axis=0, tiled=True, axis...  27.7 us
    all_to_all x2, starting transfers between devices, summed_on_arrival(): lax.all_to_all(parts, axis, split_axis=0, concat_axis=0, tiled=True, axis...  25.4 us
    ppermute x6, starting transfers between devices, from_epochs(): arrived.append(lax.ppermute(pieces[ahead], 'epoch', route))  20.9 us
    pallas_call x1, Pallas kernels, clip_and_sum(): pl.pallas_call(functools.partial(clip_kernel, parts, near), out_shape=jax...  15.5 us
    ppermute x3, starting transfers between devices, gather_over_sky(): arrived.append(lax.ppermute(shards, 'sky', route))  11 us
    pallas_call x1, Pallas kernels, warp_columns(): pl.pallas_call(column_kernel, grid=(held // GROUP,), out_shape=[jax.Shape...  10 us
  transfers between devices with their start and end apart: 15, of which 7 were waited for; matrix products, arithmetic and copies ran while one was open for 4% of the time, Pallas kernels for 7%

profile of v6, /device:TPU:40, one launch (start us, length us, event | category | flops | bytes accessed | tf_op | source)
XLA Modules:
  0.0 236.0 jit_solution(9145382810022111199)
XLA Ops:
  1.6 0.8 slice_bitcast_fusion.3
  6.1 0.8 multiply_reduce_fusion
  7.2 0.8 copy.114
  10.0 10.0 %columns.1 = (bf16[49,32,384]{2,1,0:T(8,128)(2,1)}, bf16[49,32,384]{2,1,0:T(8,128)(2,1)}, bf16[49,32,384]{2,1,0:T(8,128)(2,1)}, bf16[49,32,384]{2,1,0:T(8,128)(2,1)}) custom-call(s32[49]{0:T(128)} %pad_add_fusion.1.ints, f32[288]{0:T(512)} %reshape_squeeze.3.floats, bf16[16,384]{1,0:T(8,128)(2,1)} %bitcast.102, bf16[48,3,32,512]{3,2,1,0:T(8,128)(2,1)} %pixels.1), custom_call_target="tpu_custom_call" | custom-call | flops 2415919104 | bytes 9437184 | tf_op jit(solution)/shard_map/columns/pallas_call | solution.py:110
  20.1 3.6 %collective-permute-start.3 = (bf16[49,32,384]{2,1,0:T(8,128)(2,1)}, bf16[49,32,384]{2,1,0:T(8,128)(2,1)S(1)}, u32[]{:S(2)}, u32[]{:S(2)}) collective-permute-start(bf16[49,32,384]{2,1,0:T(8,128)(2,1)} %get-tuple-element.33), channel_id=1, source_target_pairs={{0,2},{2,4},{4,6},{6,0},{1,3},{3,5},{5,7},{7,1},{8,10},{10,12},{12... | collective-permute-start | bytes 3612680 | tf_op jit(solution)/shard_map/ppermute | solution.py:325
  23.6 4.9 %collective-permute-start.4 = (bf16[49,32,384]{2,1,0:T(8,128)(2,1)}, bf16[49,32,384]{2,1,0:T(8,128)(2,1)S(1)}, u32[]{:S(2)}, u32[]{:S(2)}) collective-permute-start(bf16[49,32,384]{2,1,0:T(8,128)(2,1)} %get-tuple-element.34), channel_id=1, source_target_pairs={{0,4},{2,6},{4,0},{6,2},{1,5},{3,7},{5,1},{7,3},{8,12},{10,14},{12... | collective-permute-start | bytes 3612680 | tf_op jit(solution)/shard_map/ppermute | solution.py:325
  28.5 3.2 %collective-permute-start.5 = (bf16[49,32,384]{2,1,0:T(8,128)(2,1)}, bf16[49,32,384]{2,1,0:T(8,128)(2,1)}, u32[]{:S(2)}, u32[]{:S(2)}) collective-permute-start(bf16[49,32,384]{2,1,0:T(8,128)(2,1)} %get-tuple-element.35), channel_id=1, source_target_pairs={{0,6},{2,0},{4,2},{6,4},{1,7},{3,1},{5,3},{7,5},{8,14},{10,8},{12,... | collective-permute-start | bytes 3612680 | tf_op jit(solution)/shard_map/ppermute | solution.py:325
  32.6 43.4 %all-to-all-start = ((bf16[8,32,384]{2,1,0:T(8,128)(2,1)}), bf16[8,32,384]{2,1,0:T(8,128)(2,1)S(1)}, u32[]{:S(2)}, u32[]{:S(2)}) async-start(bf16[8,32,384]{2,1,0:T(8,128)(2,1)} %broadcast_in_dim.280), calls=%async_computation | async-start | bytes 393216 | tf_op jit(solution)/shard_map/all_to_all | solution.py:310
  77.9 28.9 %all-to-all-done.refs_0_ = bf16[8,32,384]{2,1,0:T(8,128)(2,1)S(1)} async-done(((bf16[8,32,384]{2,1,0:T(8,128)(2,1)}), bf16[8,32,384]{2,1,0:T(8,128)(2,1)S(1)}, u32[]{:S(2)}, u32[]{:S(2)}) %all-to-all-start) | async-done | bytes 196640 | tf_op jit(solution)/shard_map/all_to_all | solution.py:310
  106.8 8.9 %all-to-all-start.3 = ((f32[32,2,128]{2,1,0:T(2,128)}), f32[32,2,128]{2,1,0:T(2,128)S(1)}, u32[]{:S(2)}, u32[]{:S(2)}) async-start(f32[32,2,128]{2,1,0:T(2,128)} %bitcast.20), calls=%async_computation.3 | async-start | bytes 65536 | tf_op jit(solution)/shard_map/all_to_all | solution.py:424
  115.7 3.3 %collective-permute-start = (bf16[8,32,384]{2,1,0:T(8,128)(2,1)S(1)}, bf16[8,32,384]{2,1,0:T(8,128)(2,1)S(1)}, u32[]{:S(2)}, u32[]{:S(2)}) collective-permute-start(bf16[8,32,384]{2,1,0:T(8,128)(2,1)S(1)} %all-to-all-done.refs_0_), channel_id=1, source_target_pairs={{0,8},{8,16},{16,24},{24,0},{32,40},{40,48},{48,56},{56,32},{64,72... | collective-permute-start | bytes 589832 | tf_op jit(solution)/shard_map/ppermute | solution.py:316
  119.0 4.3 %collective-permute-start.1 = (bf16[8,32,384]{2,1,0:T(8,128)(2,1)S(1)}, bf16[8,32,384]{2,1,0:T(8,128)(2,1)S(1)}, u32[]{:S(2)}, u32[]{:S(2)}) collective-permute-start(bf16[8,32,384]{2,1,0:T(8,128)(2,1)S(1)} %all-to-all-done.refs_0_), channel_id=1, source_target_pairs={{0,16},{8,24},{16,0},{24,8},{32,48},{40,56},{48,32},{56,40},{64,80... | collective-permute-start | bytes 589832 | tf_op jit(solution)/shard_map/ppermute | solution.py:316
  123.3 3.4 %collective-permute-start.2 = (bf16[8,32,384]{2,1,0:T(8,128)(2,1)S(1)}, bf16[8,32,384]{2,1,0:T(8,128)(2,1)S(1)}, u32[]{:S(2)}, u32[]{:S(2)}) collective-permute-start(bf16[8,32,384]{2,1,0:T(8,128)(2,1)S(1)} %all-to-all-done.refs_0_), channel_id=1, source_target_pairs={{0,24},{8,0},{16,8},{24,16},{32,56},{40,32},{48,40},{56,48},{64,88... | collective-permute-start | bytes 589832 | tf_op jit(solution)/shard_map/ppermute | solution.py:316
  127.5 1.1 copy.116.expand
  128.6 7.9 %collective-permute-done.1.refs_2_ = bf16[8,32,384]{2,1,0:T(8,128)(2,1)S(1)} collective-permute-done((bf16[8,32,384]{2,1,0:T(8,128)(2,1)S(1)}, bf16[8,32,384]{2,1,0:T(8,128)(2,1)S(1)}, u32[]{:S(2)}, u32[]{:S(2)}) %collective-permute-start.1) | collective-permute-done | bytes 196640 | tf_op jit(solution)/shard_map/ppermute | solution.py:316
  136.5 1.3 copy-done.1
  137.8 15.5 %clip.1 = bf16[32,32,384]{2,1,0:T(8,128)(2,1)S(1)} custom-call(s32[2]{0:T(128)S(1)} %pad_add_fusion.turn, bf16[128,768]{1,0:T(8,128)(2,1)S(1)} %copy.116.expand, bf16[8,32,384]{2,1,0:T(8,128)(2,1)S(1)} %all-to-all-done.refs_0_, bf16[8,32,384]{2,1,0:T(8,128)(2,1)S(1)} %collective-permute-done.refs_1_, bf16[8,32,384]{2,1,0:T(8,128)(2,1)S(1)} %collective-permute-done.1.refs_2_, ...), custom_call_target="tpu_custom_call" | custom-call | flops 106168320 | bytes 4718592 | tf_op jit(solution)/shard_map/clip/pallas_call | solution.py:256
  153.3 1.0 copy.152
  154.3 6.6 %all-to-all-start.1 = ((bf16[4,8,32,384]{3,2,1,0:T(8,128)(2,1)}), bf16[4,8,32,384]{3,2,1,0:T(8,128)(2,1)S(1)}, u32[]{:S(2)}, u32[]{:S(2)}) async-start(bf16[4,8,32,384]{3,2,1,0:T(8,128)(2,1)} %bitcast.84), calls=%async_computation.1 | async-start | bytes 1572864 | tf_op jit(solution)/shard_map/all_to_all | solution.py:285
  161.0 2.7 %collective-permute-start.6 = (f32[32,2,128]{2,1,0:T(2,128)S(1)}, f32[32,2,128]{2,1,0:T(2,128)S(1)}, u32[]{:S(2)}, u32[]{:S(2)}) collective-permute-start(f32[32,2,128]{2,1,0:T(2,128)S(1)} %all-to-all-done.3), channel_id=1, source_target_pairs={{0,2},{2,4},{4,6},{6,0},{1,3},{3,5},{5,7},{7,1},{8,10},{10,12},{12... | collective-permute-start | bytes 98312 | tf_op jit(solution)/shard_map/ppermute | solution.py:325
  163.6 3.0 %collective-permute-start.7 = (f32[32,2,128]{2,1,0:T(2,128)S(1)}, f32[32,2,128]{2,1,0:T(2,128)S(1)}, u32[]{:S(2)}, u32[]{:S(2)}) collective-permute-start(f32[32,2,128]{2,1,0:T(2,128)S(1)} %all-to-all-done.3), channel_id=1, source_target_pairs={{0,4},{2,6},{4,0},{6,2},{1,5},{3,7},{5,1},{7,3},{8,12},{10,14},{12... | collective-permute-start | bytes 98312 | tf_op jit(solution)/shard_map/ppermute | solution.py:325
  166.6 3.6 %collective-permute-start.8 = (f32[32,2,128]{2,1,0:T(2,128)S(1)}, f32[32,2,128]{2,1,0:T(2,128)S(1)}, u32[]{:S(2)}, u32[]{:S(2)}) collective-permute-start(f32[32,2,128]{2,1,0:T(2,128)S(1)} %all-to-all-done.3), channel_id=1, source_target_pairs={{0,6},{2,0},{4,2},{6,4},{1,7},{3,1},{5,3},{7,5},{8,14},{10,8},{12,... | collective-permute-start | bytes 98312 | tf_op jit(solution)/shard_map/ppermute | solution.py:325
  170.2 0.7 collective-permute-done.7
  171.0 1.8 collective-permute-done.8
  174.1 6.7 %all-to-all-done.1 = bf16[4,8,32,384]{3,2,1,0:T(8,128)(2,1)S(1)} async-done(((bf16[4,8,32,384]{3,2,1,0:T(8,128)(2,1)}), bf16[4,8,32,384]{3,2,1,0:T(8,128)(2,1)S(1)}, u32[]{:S(2)}, u32[]{:S(2)}) %all-to-all-start.1) | async-done | bytes 786464 | tf_op jit(solution)/shard_map/all_to_all | solution.py:285
  180.7 0.8 fusion.18
  181.5 18.8 %all-to-all-start.2 = ((bf16[8,32,384]{2,1,0:T(8,128)(2,1)}), bf16[8,32,384]{2,1,0:T(8,128)(2,1)S(1)}, u32[]{:S(2)}, u32[]{:S(2)}) async-start(bf16[8,32,384]{2,1,0:T(8,128)(2,1)} %fusion.18), calls=%async_computation.2 | async-start | bytes 393216 | tf_op jit(solution)/shard_map/all_to_all | solution.py:285
  200.8 0.8 convolution_bitcast_fusion.1
  201.6 1.3 collective-permute-start.9
  203.0 1.3 collective-permute-start.10
  204.6 8.9 %collective-permute-done.9 = f32[3,8,128]{2,0,1:T(4,128)S(1)} collective-permute-done((f32[3,8,128]{2,0,1:T(4,128)S(1)}, f32[3,8,128]{2,0,1:T(4,128)S(1)}, u32[]{:S(2)}, u32[]{:S(2)}) %collective-permute-start.9) | collective-permute-done | bytes 12320 | tf_op jit(solution)/shard_map/ppermute | solution.py:445
  213.5 21.0 %all-to-all-done.2 = bf16[8,32,384]{2,1,0:T(8,128)(2,1)S(1)} async-done(((bf16[8,32,384]{2,1,0:T(8,128)(2,1)}), bf16[8,32,384]{2,1,0:T(8,128)(2,1)S(1)}, u32[]{:S(2)}, u32[]{:S(2)}) %all-to-all-start.2) | async-done | bytes 196640 | tf_op jit(solution)/shard_map/all_to_all | solution.py:285
  (113 shorter events, 13.2 us)
Async XLA Ops:
  0.6 31.2 %copy-start = (bf16[3,32,512]{2,1,0:T(8,128)(2,1)S(1)}, bf16[3,32,512]{2,1,0:T(8,128)(2,1)}, u32[]{:S(2)}) copy-start(bf16[3,32,512]{2,1,0:T(8,128)(2,1)} %param.22) | copy-start | bytes 294916
  0.7 0.7 copy-start.6
  10.0 66.0 %copy-start.9 = (s32[48,1]{0,1:T(1,128)S(1)}, s32[48,1]{0,1:T(1,128)}, u32[]{:S(2)}) copy-start(s32[48,1]{0,1:T(1,128)} %param.16) | copy-start | bytes 580
  10.0 66.2 %copy-start.2 = (bf16[48,3]{0,1:T(4,128)(2,1)S(1)}, bf16[48,3]{0,1:T(4,128)(2,1)}, u32[]{:S(2)}) copy-start(bf16[48,3]{0,1:T(4,128)(2,1)} %param.19) | copy-start | bytes 868
  10.0 66.3 %copy-start.3 = (f32[3,32]{1,0:T(4,128)S(1)}, f32[3,32]{1,0:T(4,128)}, u32[]{:S(2)}) copy-start(f32[3,32]{1,0:T(4,128)} %param.23) | copy-start | bytes 1156
  10.0 66.5 %copy-start.8 = (bf16[48,2]{0,1:T(2,128)(2,1)S(1)}, bf16[48,2]{0,1:T(2,128)(2,1)}, u32[]{:S(2)}) copy-start(bf16[48,2]{0,1:T(2,128)(2,1)} %param.18) | copy-start | bytes 580
  20.1 103.3 %collective-permute-start.3 = (bf16[49,32,384]{2,1,0:T(8,128)(2,1)}, bf16[49,32,384]{2,1,0:T(8,128)(2,1)S(1)}, u32[]{:S(2)}, u32[]{:S(2)}) collective-permute-start(bf16[49,32,384]{2,1,0:T(8,128)(2,1)} %get-tuple-element.33), channel_id=1, source_target_pairs={{0,2},{2,4},{4,6},{6,0},{1,3},{3,5},{5,7},{7,1},{8,10},{10,12},{12... | collective-permute-start | bytes 3612680 | tf_op jit(solution)/shard_map/ppermute | solution.py:325
  23.6 105.0 %collective-permute-start.4 = (bf16[49,32,384]{2,1,0:T(8,128)(2,1)}, bf16[49,32,384]{2,1,0:T(8,128)(2,1)S(1)}, u32[]{:S(2)}, u32[]{:S(2)}) collective-permute-start(bf16[49,32,384]{2,1,0:T(8,128)(2,1)} %get-tuple-element.34), channel_id=1, source_target_pairs={{0,4},{2,6},{4,0},{6,2},{1,5},{3,7},{5,1},{7,3},{8,12},{10,14},{12... | collective-permute-start | bytes 3612680 | tf_op jit(solution)/shard_map/ppermute | solution.py:325
  28.5 100.1 %collective-permute-start.5 = (bf16[49,32,384]{2,1,0:T(8,128)(2,1)}, bf16[49,32,384]{2,1,0:T(8,128)(2,1)}, u32[]{:S(2)}, u32[]{:S(2)}) collective-permute-start(bf16[49,32,384]{2,1,0:T(8,128)(2,1)} %get-tuple-element.35), channel_id=1, source_target_pairs={{0,6},{2,0},{4,2},{6,4},{1,7},{3,1},{5,3},{7,5},{8,14},{10,8},{12,... | collective-permute-start | bytes 3612680 | tf_op jit(solution)/shard_map/ppermute | solution.py:325
  32.6 74.2 %all-to-all-start = ((bf16[8,32,384]{2,1,0:T(8,128)(2,1)}), bf16[8,32,384]{2,1,0:T(8,128)(2,1)S(1)}, u32[]{:S(2)}, u32[]{:S(2)}) async-start(bf16[8,32,384]{2,1,0:T(8,128)(2,1)} %broadcast_in_dim.280), calls=%async_computation | async-start | bytes 393216 | tf_op jit(solution)/shard_map/all_to_all | solution.py:310
  77.8 29.0 %copy-start.4 = (s32[128]{0:T(128)}, s32[128]{0:T(128)S(1)}, u32[]{:S(2)}) copy-start(s32[128]{0:T(128)S(1)} %get-tuple-element.99) | copy-start | bytes 1540
  106.8 47.5 %all-to-all-start.3 = ((f32[32,2,128]{2,1,0:T(2,128)}), f32[32,2,128]{2,1,0:T(2,128)S(1)}, u32[]{:S(2)}, u32[]{:S(2)}) async-start(f32[32,2,128]{2,1,0:T(2,128)} %bitcast.20), calls=%async_computation.3 | async-start | bytes 65536 | tf_op jit(solution)/shard_map/all_to_all | solution.py:424
  115.7 12.9 %collective-permute-start = (bf16[8,32,384]{2,1,0:T(8,128)(2,1)S(1)}, bf16[8,32,384]{2,1,0:T(8,128)(2,1)S(1)}, u32[]{:S(2)}, u32[]{:S(2)}) collective-permute-start(bf16[8,32,384]{2,1,0:T(8,128)(2,1)S(1)} %all-to-all-done.refs_0_), channel_id=1, source_target_pairs={{0,8},{8,16},{16,24},{24,0},{32,40},{40,48},{48,56},{56,32},{64,72... | collective-permute-start | bytes 589832 | tf_op jit(solution)/shard_map/ppermute | solution.py:316
  119.0 17.5 %collective-permute-start.1 = (bf16[8,32,384]{2,1,0:T(8,128)(2,1)S(1)}, bf16[8,32,384]{2,1,0:T(8,128)(2,1)S(1)}, u32[]{:S(2)}, u32[]{:S(2)}) collective-permute-start(bf16[8,32,384]{2,1,0:T(8,128)(2,1)S(1)} %all-to-all-done.refs_0_), channel_id=1, source_target_pairs={{0,16},{8,24},{16,0},{24,8},{32,48},{40,56},{48,32},{56,40},{64,80... | collective-permute-start | bytes 589832 | tf_op jit(solution)/shard_map/ppermute | solution.py:316
  123.3 13.2 %collective-permute-start.2 = (bf16[8,32,384]{2,1,0:T(8,128)(2,1)S(1)}, bf16[8,32,384]{2,1,0:T(8,128)(2,1)S(1)}, u32[]{:S(2)}, u32[]{:S(2)}) collective-permute-start(bf16[8,32,384]{2,1,0:T(8,128)(2,1)S(1)} %all-to-all-done.refs_0_), channel_id=1, source_target_pairs={{0,24},{8,0},{16,8},{24,16},{32,56},{40,32},{48,40},{56,48},{64,88... | collective-permute-start | bytes 589832 | tf_op jit(solution)/shard_map/ppermute | solution.py:316
  136.5 1.3 copy-start.1
  154.3 18.7 %copy-start.7 = (f32[6]{0:T(128)S(1)}, f32[6]{0:T(128)}, u32[]{:S(2)}) copy-start(f32[6]{0:T(128)} %copy-done.6) | copy-start | bytes 76
  154.3 26.4 %all-to-all-start.1 = ((bf16[4,8,32,384]{3,2,1,0:T(8,128)(2,1)}), bf16[4,8,32,384]{3,2,1,0:T(8,128)(2,1)S(1)}, u32[]{:S(2)}, u32[]{:S(2)}) async-start(bf16[4,8,32,384]{3,2,1,0:T(8,128)(2,1)} %bitcast.84), calls=%async_computation.1 | async-start | bytes 1572864 | tf_op jit(solution)/shard_map/all_to_all | solution.py:285
  161.0 9.3 %collective-permute-start.6 = (f32[32,2,128]{2,1,0:T(2,128)S(1)}, f32[32,2,128]{2,1,0:T(2,128)S(1)}, u32[]{:S(2)}, u32[]{:S(2)}) collective-permute-start(f32[32,2,128]{2,1,0:T(2,128)S(1)} %all-to-all-done.3), channel_id=1, source_target_pairs={{0,2},{2,4},{4,6},{6,0},{1,3},{3,5},{5,7},{7,1},{8,10},{10,12},{12... | collective-permute-start | bytes 98312 | tf_op jit(solution)/shard_map/ppermute | solution.py:325
  163.6 7.3 %collective-permute-start.7 = (f32[32,2,128]{2,1,0:T(2,128)S(1)}, f32[32,2,128]{2,1,0:T(2,128)S(1)}, u32[]{:S(2)}, u32[]{:S(2)}) collective-permute-start(f32[32,2,128]{2,1,0:T(2,128)S(1)} %all-to-all-done.3), channel_id=1, source_target_pairs={{0,4},{2,6},{4,0},{6,2},{1,5},{3,7},{5,1},{7,3},{8,12},{10,14},{12... | collective-permute-start | bytes 98312 | tf_op jit(solution)/shard_map/ppermute | solution.py:325
  166.6 6.2 %collective-permute-start.8 = (f32[32,2,128]{2,1,0:T(2,128)S(1)}, f32[32,2,128]{2,1,0:T(2,128)S(1)}, u32[]{:S(2)}, u32[]{:S(2)}) collective-permute-start(f32[32,2,128]{2,1,0:T(2,128)S(1)} %all-to-all-done.3), channel_id=1, source_target_pairs={{0,6},{2,0},{4,2},{6,4},{1,7},{3,1},{5,3},{7,5},{8,14},{10,8},{12,... | collective-permute-start | bytes 98312 | tf_op jit(solution)/shard_map/ppermute | solution.py:325
  173.2 27.0 %copy-start.5 = (s32[128]{0:T(128)S(1)}, s32[128]{0:T(128)}, u32[]{:S(2)}) copy-start(s32[128]{0:T(128)} %copy-done.4) | copy-start | bytes 1540
  181.5 53.1 %all-to-all-start.2 = ((bf16[8,32,384]{2,1,0:T(8,128)(2,1)}), bf16[8,32,384]{2,1,0:T(8,128)(2,1)S(1)}, u32[]{:S(2)}, u32[]{:S(2)}) async-start(bf16[8,32,384]{2,1,0:T(8,128)(2,1)} %fusion.18), calls=%async_computation.2 | async-start | bytes 393216 | tf_op jit(solution)/shard_map/all_to_all | solution.py:285
  201.6 11.8 %collective-permute-start.9 = (f32[3,8,128]{2,0,1:T(4,128)S(1)}, f32[3,8,128]{2,0,1:T(4,128)S(1)}, u32[]{:S(2)}, u32[]{:S(2)}) collective-permute-start(f32[3,8,128]{2,0,1:T(4,128)S(1)} %copy.140), channel_id=1, source_target_pairs={{0,8},{8,16},{16,24},{24,32},{32,40},{40,48},{48,56},{56,64},{64,7... | collective-permute-start | bytes 36872 | tf_op jit(solution)/shard_map/ppermute | solution.py:445
  203.0 10.5 %collective-permute-start.10 = (f32[3,8,128]{2,0,1:T(4,128)S(1)}, f32[3,8,128]{2,0,1:T(4,128)S(1)}, u32[]{:S(2)}, u32[]{:S(2)}) collective-permute-start(f32[3,8,128]{2,0,1:T(4,128)S(1)} %copy.141), channel_id=1, source_target_pairs={{8,0},{16,8},{24,16},{32,24},{40,32},{48,40},{56,48},{64,56},{72,6... | collective-permute-start | bytes 36872 | tf_op jit(solution)/shard_map/ppermute | solution.py:446

commit v7 on v5

--- a/solution.py
+++ b/solution.py
@@ -128,7 +128,7 @@
     )(jnp.append(shifts, turn), taps.reshape(-1), pixels)
 
 
-def clip_kernel(parts, near, turn, expand, *refs):
+def clip_kernel(parts, near, col_blocks, turn, *refs):
     templates, refs = refs[:near], refs[near:]
     scalars, vectors, groups = refs[:parts], refs[parts : 2 * parts], refs[2 * parts : 3 * parts]
     out, framed, sums, planes = refs[3 * parts :]
@@ -157,6 +157,19 @@
     lax.fori_loop(0, owners // near, fill, 0)
     sums[ends - 2 * MARGIN : ends, :] = jnp.zeros((2 * MARGIN, width), jnp.float32)
 
+    per_part = col_blocks // parts
+    cell = lax.broadcasted_iota(jnp.int32, (cells + LEFT_OVER, LANES), 0)
+    column = lax.broadcasted_iota(jnp.int32, (cells + LEFT_OVER, LANES), 1)
+    col_block = jnp.zeros_like(column) + turn[0] * per_part
+    for number in range(1, per_part):
+        col_block += (column >= number * (LANES // per_part)).astype(jnp.int32)
+    expand = jnp.concatenate(
+        [
+            (cell - block * col_blocks == col_block).astype(jnp.float32).astype(jnp.bfloat16)
+            for block in range(blocks)
+        ],
+        axis=1,
+    )
     lane = lax.broadcasted_iota(jnp.int32, (slots, LANES), 1) + turn[0] * LANES
     for group in range(parts):
         described = vectors[group][...]
@@ -169,7 +182,7 @@
             covered = covered + jnp.where(inside, weight, 0.0)
         covered = jnp.clip(covered, 0.0, 1.0)
         usable = jnp.dot(
-            described.astype(jnp.bfloat16), expand[...], preferred_element_type=jnp.float32
+            described.astype(jnp.bfloat16), expand, preferred_element_type=jnp.float32
         )
         for block in range(blocks):
             lanes = slice(block * LANES, (block + 1) * LANES)
@@ -220,7 +233,7 @@
     lax.fori_loop(0, owners, give, 0)
 
 
-def clip_and_sum(turn, expand, templates, described, columns):
+def clip_and_sum(turn, row_blocks, col_blocks, templates, described, columns):
     parts, near = len(columns), len(templates)
     slots, rows, width = columns[0].shape
     tiles = parts * slots
@@ -229,14 +242,14 @@
     scalar = pl.BlockSpec(memory_space=pltpu.SMEM)
     vector = pl.BlockSpec(memory_space=pltpu.VMEM)
     return pl.pallas_call(
-        functools.partial(clip_kernel, parts, near),
+        functools.partial(clip_kernel, parts, near, col_blocks),
         out_shape=jax.ShapeDtypeStruct((owners, rows, width), jnp.bfloat16),
-        in_specs=[scalar] + [vector] * (1 + near) + [scalar] * parts + [vector] * (2 * parts),
+        in_specs=[scalar] + [vector] * near + [scalar] * parts + [vector] * (2 * parts),
         out_specs=vector,
         scratch_shapes=[
             pltpu.VMEM((height, width), jnp.float32),
             pltpu.VMEM((height, width), jnp.float32),
-            pltpu.VMEM((tiles, expand.shape[1]), jnp.float32),
+            pltpu.VMEM((tiles, row_blocks * LANES), jnp.float32),
         ],
         compiler_params=pltpu.CompilerParams(vmem_limit_bytes=32 * 1024 * 1024),
         cost_estimate=pl.CostEstimate(
@@ -245,7 +258,7 @@
             transcendentals=tiles * (rows + 2 * MARGIN) * width,
         ),
         name="clip",
-    )(turn, expand, *templates, *described, *described, *columns)
+    )(turn, *templates, *described, *described, *columns)
 
 
 def spread(index, block_count, block):
@@ -291,11 +304,11 @@
 
 def from_epochs(pieces):
     count = lax.axis_size("epoch")
-    arrived = [pieces[0]]
-    for ahead in range(1, count):
+    arrived = {0: pieces[0]}
+    for ahead in sorted(range(1, count), key=lambda ahead: -min(ahead, count - ahead)):
         route = [(i, (i + ahead) % count) for i in range(count)]
-        arrived.append(lax.ppermute(pieces[ahead], "epoch", route))
-    return arrived
+        arrived[ahead] = lax.ppermute(pieces[ahead], "epoch", route)
+    return [arrived[ahead] for ahead in range(count)]
 
 
 def on_device(
@@ -354,10 +367,6 @@
     col_index = epoch_position * part_width + jnp.arange(part_width, dtype=jnp.int32)
     all_index = jnp.arange(cols, dtype=jnp.int32)
     expand = spread(col_index, col_blocks, cols // col_blocks)
-    cell = jnp.arange(cells + LEFT_OVER, dtype=jnp.int32)[:, None, None]
-    of_row = cell // col_blocks == jnp.arange(row_blocks, dtype=jnp.int32)[None, :, None]
-    of_col = cell % col_blocks == (col_index // (cols // col_blocks))[None, None, :]
-    expand_cells = (of_row & of_col).astype(jnp.bfloat16).reshape(cells + LEFT_OVER, -1)
 
     row_cover = cover(slot_offset[:, 0], taps[:, 0], row_index, rows)
     col_cover = cover(slot_offset[:, 1], taps[:, 1], all_index, cols)
@@ -419,7 +428,7 @@
     weight_sum = weight_sum.at[:, rows - MARGIN :].add(from_below)
 
     turn = jnp.stack([epoch_position, lax.axis_index("sky") % len(templates)])
-    partial = clip_and_sum(turn, expand_cells, templates, described, columns)
+    partial = clip_and_sum(turn, row_blocks, col_blocks, templates, described, columns)
     flux = sum_over_sky(partial)
     flux_sum = jnp.swapaxes(flux.reshape(rows, bands, part_width), 0, 1)
 

time: 249 us -> 242 us (0.972)
  waiting for transfers between devices: 66.4 us -> 53.1 us
  starting transfers between devices: 134 us -> 146 us
  other arithmetic: 8.18 us -> 4.54 us
    ppermute x9, waiting for transfers between devices: 22 us -> 15.7 us  [from_epochs(): arrived[ahead] = lax.ppermute(pieces[ahead], 'epoch', route)]
    all_to_all x1, waiting for transfers between devices: 6.81 us -> 0.64 us  [gather_over_sky(): lax.all_to_all(copies, 'sky', split_axis=0, concat_axis=0, tiled=True, ax...]
    all_to_all x1, starting transfers between devices: 17.2 us -> 23.3 us  [on_device(): lax.all_to_all(message, 'sky', split_axis=0, concat_axis=0, tiled=True)]
    ppermute x9, starting transfers between devices: 31.3 us -> 35.3 us  [from_epochs(): arrived[ahead] = lax.ppermute(pieces[ahead], 'epoch', route)]
  transfers between devices with their start and end apart: 18 -> 18, of which waited for: 9 -> 10; matrix products, arithmetic and copies ran while one was open for 4% -> 4% of each run, Pallas kernels for 9% -> 10%
where the time goes in v7:
time: 242 us; the launch traced here: 240 us
  starting transfers between devices  146 us (60%)
  waiting for transfers between devices  53.1 us (22%)
  Pallas kernels  23.4 us (10%)
  local copies, waits for them, and re-layouts  9.02 us (4%)
  other arithmetic  4.54 us (2%)
    all_to_all x1, starting transfers between devices, gather_over_sky(): lax.all_to_all(copies, 'sky', split_axis=0, concat_axis=0, tiled=True, ax...  43.4 us
    ppermute x9, starting transfers between devices, from_epochs(): arrived[ahead] = lax.ppermute(pieces[ahead], 'epoch', route)  35.3 us
    all_to_all x2, starting transfers between devices, summed_on_arrival(): lax.all_to_all(parts, axis, split_axis=0, concat_axis=0, tiled=True, axis...  28.2 us
    all_to_all x1, starting transfers between devices, on_device(): lax.all_to_all(message, 'sky', split_axis=0, concat_axis=0, tiled=True)  23.3 us
    all_to_all x2, waiting for transfers between devices, summed_on_arrival(): lax.all_to_all(parts, axis, split_axis=0, concat_axis=0, tiled=True, axis...  21.6 us
    ppermute x9, waiting for transfers between devices, from_epochs(): arrived[ahead] = lax.ppermute(pieces[ahead], 'epoch', route)  15.7 us
    pallas_call x1, Pallas kernels, clip_and_sum(): pl.pallas_call(functools.partial(clip_kernel, parts, near, col_blocks), o...  14 us
    ppermute x3, starting transfers between devices, gather_over_sky(): arrived.append(lax.ppermute(shards, 'sky', route))  12.2 us
  transfers between devices with their start and end apart: 18, of which 10 were waited for; matrix products, arithmetic and copies ran while one was open for 4% of the time, Pallas kernels for 10%

profile of v7, /device:TPU:40, one launch (start us, length us, event | category | flops | bytes accessed | tf_op | source)
XLA Modules:
  0.0 239.6 jit_solution(6686171882082615341)
XLA Ops:
  0.7 0.9 copy-done
  2.3 43.4 %all-to-all-start = ((bf16[8,32,384]{2,1,0:T(8,128)(2,1)}), bf16[8,32,384]{2,1,0:T(8,128)(2,1)S(1)}, u32[]{:S(2)}, u32[]{:S(2)}) async-start(bf16[8,32,384]{2,1,0:T(8,128)(2,1)} %broadcast_in_dim.274), calls=%async_computation | async-start | bytes 393216 | tf_op jit(solution)/shard_map/all_to_all | solution.py:295
  48.6 9.4 %columns.1 = (bf16[48,32,384]{2,1,0:T(8,128)(2,1)}, bf16[48,32,384]{2,1,0:T(8,128)(2,1)}, bf16[48,32,384]{2,1,0:T(8,128)(2,1)}, bf16[48,32,384]{2,1,0:T(8,128)(2,1)}) custom-call(s32[49]{0:T(128)} %pad_add_fusion.1.ints, f32[288]{0:T(512)} %reshape_squeeze.3.floats, bf16[48,3,32,512]{3,2,1,0:T(8,128)(2,1)} %pixels.1), custom_call_target="tpu_custom_call" | custom-call | flops 2415919104 | bytes 9437184 | tf_op jit(solution)/shard_map/columns/pallas_call | solution.py:107
  58.1 3.7 %collective-permute-start.6 = (bf16[48,32,384]{2,1,0:T(8,128)(2,1)}, bf16[48,32,384]{2,1,0:T(8,128)(2,1)S(1)}, u32[]{:S(2)}, u32[]{:S(2)}) collective-permute-start(bf16[48,32,384]{2,1,0:T(8,128)(2,1)} %get-tuple-element.33), channel_id=1, source_target_pairs={{0,2},{2,4},{4,6},{6,0},{1,3},{3,5},{5,7},{7,1},{8,10},{10,12},{12... | collective-permute-start | bytes 3538952 | tf_op jit(solution)/shard_map/ppermute | solution.py:310
  64.2 3.5 %collective-permute-start.3 = (f32[48,128]{1,0:T(8,128)S(1)}, f32[48,128]{1,0:T(8,128)S(1)}, u32[]{:S(2)}, u32[]{:S(2)}) collective-permute-start(f32[48,128]{1,0:T(8,128)S(1)} %pad.12.refs_4_.refs_8_), channel_id=1, source_target_pairs={{0,2},{2,4},{4,6},{6,0},{1,3},{3,5},{5,7},{7,1},{8,10},{10,12},{12... | collective-permute-start | bytes 73736 | tf_op jit(solution)/shard_map/ppermute | solution.py:310
  67.8 3.4 %collective-permute-start.7 = (bf16[48,32,384]{2,1,0:T(8,128)(2,1)}, bf16[48,32,384]{2,1,0:T(8,128)(2,1)S(1)}, u32[]{:S(2)}, u32[]{:S(2)}) collective-permute-start(bf16[48,32,384]{2,1,0:T(8,128)(2,1)} %get-tuple-element.34), channel_id=1, source_target_pairs={{0,4},{2,6},{4,0},{6,2},{1,5},{3,7},{5,1},{7,3},{8,12},{10,14},{12... | collective-permute-start | bytes 3538952 | tf_op jit(solution)/shard_map/ppermute | solution.py:310
  71.2 4.5 %collective-permute-start.8 = (bf16[48,32,384]{2,1,0:T(8,128)(2,1)}, bf16[48,32,384]{2,1,0:T(8,128)(2,1)}, u32[]{:S(2)}, u32[]{:S(2)}) collective-permute-start(bf16[48,32,384]{2,1,0:T(8,128)(2,1)} %get-tuple-element.35), channel_id=1, source_target_pairs={{0,6},{2,0},{4,2},{6,4},{1,7},{3,1},{5,3},{7,5},{8,14},{10,8},{12,... | collective-permute-start | bytes 3538952 | tf_op jit(solution)/shard_map/ppermute | solution.py:310
  77.8 23.3 %all-to-all-start.3 = ((f32[32,2,128]{2,1,0:T(2,128)}), f32[32,2,128]{2,1,0:T(2,128)S(1)}, u32[]{:S(2)}, u32[]{:S(2)}) async-start(f32[32,2,128]{2,1,0:T(2,128)} %bitcast.19), calls=%async_computation.3 | async-start | bytes 65536 | tf_op jit(solution)/shard_map/all_to_all | solution.py:403
  101.1 2.5 %collective-permute-start.4 = (f32[48,128]{1,0:T(8,128)S(1)}, f32[48,128]{1,0:T(8,128)S(1)}, u32[]{:S(2)}, u32[]{:S(2)}) collective-permute-start(f32[48,128]{1,0:T(8,128)S(1)} %pad.12.refs_4_.refs_8_), channel_id=1, source_target_pairs={{0,4},{2,6},{4,0},{6,2},{1,5},{3,7},{5,1},{7,3},{8,12},{10,14},{12... | collective-permute-start | bytes 73736 | tf_op jit(solution)/shard_map/ppermute | solution.py:310
  103.6 3.5 %collective-permute-start.5 = (f32[48,128]{1,0:T(8,128)S(1)}, f32[48,128]{1,0:T(8,128)S(1)}, u32[]{:S(2)}, u32[]{:S(2)}) collective-permute-start(f32[48,128]{1,0:T(8,128)S(1)} %pad.12.refs_4_.refs_8_), channel_id=1, source_target_pairs={{0,6},{2,0},{4,2},{6,4},{1,7},{3,1},{5,3},{7,5},{8,14},{10,8},{12,... | collective-permute-start | bytes 73736 | tf_op jit(solution)/shard_map/ppermute | solution.py:310
  107.2 9.5 %collective-permute-done.4.refs_6_.refs_10_ = f32[48,128]{1,0:T(8,128)S(1)} collective-permute-done((f32[48,128]{1,0:T(8,128)S(1)}, f32[48,128]{1,0:T(8,128)S(1)}, u32[]{:S(2)}, u32[]{:S(2)}) %collective-permute-start.4) | collective-permute-done | bytes 24608 | tf_op jit(solution)/shard_map/ppermute | solution.py:310
  116.7 3.8 %collective-permute-start = (bf16[8,32,384]{2,1,0:T(8,128)(2,1)S(1)}, bf16[8,32,384]{2,1,0:T(8,128)(2,1)S(1)}, u32[]{:S(2)}, u32[]{:S(2)}) collective-permute-start(bf16[8,32,384]{2,1,0:T(8,128)(2,1)S(1)} %all-to-all-done.refs_0_), channel_id=1, source_target_pairs={{0,8},{8,16},{16,24},{24,0},{32,40},{40,48},{48,56},{56,32},{64,72... | collective-permute-start | bytes 589832 | tf_op jit(solution)/shard_map/ppermute | solution.py:301
  120.5 3.2 %collective-permute-done.5.refs_7_.refs_11_ = f32[48,128]{1,0:T(8,128)S(1)} collective-permute-done((f32[48,128]{1,0:T(8,128)S(1)}, f32[48,128]{1,0:T(8,128)S(1)}, u32[]{:S(2)}, u32[]{:S(2)}) %collective-permute-start.5) | collective-permute-done | bytes 24608 | tf_op jit(solution)/shard_map/ppermute | solution.py:310
  123.7 5.1 %collective-permute-start.1 = (bf16[8,32,384]{2,1,0:T(8,128)(2,1)S(1)}, bf16[8,32,384]{2,1,0:T(8,128)(2,1)S(1)}, u32[]{:S(2)}, u32[]{:S(2)}) collective-permute-start(bf16[8,32,384]{2,1,0:T(8,128)(2,1)S(1)} %all-to-all-done.refs_0_), channel_id=1, source_target_pairs={{0,16},{8,24},{16,0},{24,8},{32,48},{40,56},{48,32},{56,40},{64,80... | collective-permute-start | bytes 589832 | tf_op jit(solution)/shard_map/ppermute | solution.py:301
  128.8 3.3 %collective-permute-start.2 = (bf16[8,32,384]{2,1,0:T(8,128)(2,1)S(1)}, bf16[8,32,384]{2,1,0:T(8,128)(2,1)S(1)}, u32[]{:S(2)}, u32[]{:S(2)}) collective-permute-start(bf16[8,32,384]{2,1,0:T(8,128)(2,1)S(1)} %all-to-all-done.refs_0_), channel_id=1, source_target_pairs={{0,24},{8,0},{16,8},{24,16},{32,56},{40,32},{48,40},{56,48},{64,88... | collective-permute-start | bytes 589832 | tf_op jit(solution)/shard_map/ppermute | solution.py:301
  132.2 6.0 %collective-permute-done.1.refs_2_ = bf16[8,32,384]{2,1,0:T(8,128)(2,1)S(1)} collective-permute-done((bf16[8,32,384]{2,1,0:T(8,128)(2,1)S(1)}, bf16[8,32,384]{2,1,0:T(8,128)(2,1)S(1)}, u32[]{:S(2)}, u32[]{:S(2)}) %collective-permute-start.1) | collective-permute-done | bytes 196640 | tf_op jit(solution)/shard_map/ppermute | solution.py:301
  138.9 1.3 copy-done.1
  140.2 14.0 %clip.1 = bf16[32,32,384]{2,1,0:T(8,128)(2,1)S(1)} custom-call(s32[2]{0:T(128)S(1)} %pad_add_fusion.turn, bf16[8,32,384]{2,1,0:T(8,128)(2,1)S(1)} %all-to-all-done.refs_0_, bf16[8,32,384]{2,1,0:T(8,128)(2,1)S(1)} %collective-permute-done.refs_1_, bf16[8,32,384]{2,1,0:T(8,128)(2,1)S(1)} %collective-permute-done.1.refs_2_, ...), custom_call_target="tpu_custom_call" | custom-call | flops 106168320 | bytes 4718592 | tf_op jit(solution)/shard_map/clip/pallas_call | solution.py:244
  154.2 1.0 copy.168
  155.2 6.9 %all-to-all-start.1 = ((bf16[4,8,32,384]{3,2,1,0:T(8,128)(2,1)}), bf16[4,8,32,384]{3,2,1,0:T(8,128)(2,1)S(1)}, u32[]{:S(2)}, u32[]{:S(2)}) async-start(bf16[4,8,32,384]{3,2,1,0:T(8,128)(2,1)} %bitcast.81), calls=%async_computation.1 | async-start | bytes 1572864 | tf_op jit(solution)/shard_map/all_to_all | solution.py:270
  162.2 7.6 %collective-permute-start.9 = (f32[32,2,128]{2,1,0:T(2,128)S(1)}, f32[32,2,128]{2,1,0:T(2,128)S(1)}, u32[]{:S(2)}, u32[]{:S(2)}) collective-permute-start(f32[32,2,128]{2,1,0:T(2,128)S(1)} %all-to-all-done.3), channel_id=1, source_target_pairs={{0,2},{2,4},{4,6},{6,0},{1,3},{3,5},{5,7},{7,1},{8,10},{10,12},{12... | collective-permute-start | bytes 98312 | tf_op jit(solution)/shard_map/ppermute | solution.py:310
  169.8 3.7 %collective-permute-start.10 = (f32[32,2,128]{2,1,0:T(2,128)S(1)}, f32[32,2,128]{2,1,0:T(2,128)S(1)}, u32[]{:S(2)}, u32[]{:S(2)}) collective-permute-start(f32[32,2,128]{2,1,0:T(2,128)S(1)} %all-to-all-done.3), channel_id=1, source_target_pairs={{0,4},{2,6},{4,0},{6,2},{1,5},{3,7},{5,1},{7,3},{8,12},{10,14},{12... | collective-permute-start | bytes 98312 | tf_op jit(solution)/shard_map/ppermute | solution.py:310
  173.6 2.8 %collective-permute-start.11 = (f32[32,2,128]{2,1,0:T(2,128)S(1)}, f32[32,2,128]{2,1,0:T(2,128)S(1)}, u32[]{:S(2)}, u32[]{:S(2)}) collective-permute-start(f32[32,2,128]{2,1,0:T(2,128)S(1)} %all-to-all-done.3), channel_id=1, source_target_pairs={{0,6},{2,0},{4,2},{6,4},{1,7},{3,1},{5,3},{7,5},{8,14},{10,8},{12,... | collective-permute-start | bytes 98312 | tf_op jit(solution)/shard_map/ppermute | solution.py:310
  177.2 2.2 collective-permute-done.11
  180.7 1.6 all-to-all-done.1
  182.3 0.8 fusion.18
  183.1 21.4 %all-to-all-start.2 = ((bf16[8,32,384]{2,1,0:T(8,128)(2,1)}), bf16[8,32,384]{2,1,0:T(8,128)(2,1)S(1)}, u32[]{:S(2)}, u32[]{:S(2)}) async-start(bf16[8,32,384]{2,1,0:T(8,128)(2,1)} %fusion.18), calls=%async_computation.2 | async-start | bytes 393216 | tf_op jit(solution)/shard_map/all_to_all | solution.py:270
  205.0 0.8 convolution_bitcast_fusion.1
  205.8 2.3 collective-permute-start.12
  208.2 1.3 collective-permute-start.13
  209.8 8.4 %collective-permute-done.12 = f32[3,8,128]{2,0,1:T(4,128)S(1)} collective-permute-done((f32[3,8,128]{2,0,1:T(4,128)S(1)}, f32[3,8,128]{2,0,1:T(4,128)S(1)}, u32[]{:S(2)}, u32[]{:S(2)}) %collective-permute-start.12) | collective-permute-done | bytes 12320 | tf_op jit(solution)/shard_map/ppermute | solution.py:424
  218.2 20.0 %all-to-all-done.2 = bf16[8,32,384]{2,1,0:T(8,128)(2,1)S(1)} async-done(((bf16[8,32,384]{2,1,0:T(8,128)(2,1)}), bf16[8,32,384]{2,1,0:T(8,128)(2,1)S(1)}, u32[]{:S(2)}, u32[]{:S(2)}) %all-to-all-start.2) | async-done | bytes 196640 | tf_op jit(solution)/shard_map/all_to_all | solution.py:270
  (108 shorter events, 12.5 us)
Async XLA Ops:
  0.6 0.9 copy-start
  2.3 75.5 %all-to-all-start = ((bf16[8,32,384]{2,1,0:T(8,128)(2,1)}), bf16[8,32,384]{2,1,0:T(8,128)(2,1)S(1)}, u32[]{:S(2)}, u32[]{:S(2)}) async-start(bf16[8,32,384]{2,1,0:T(8,128)(2,1)} %broadcast_in_dim.274), calls=%async_computation | async-start | bytes 393216 | tf_op jit(solution)/shard_map/all_to_all | solution.py:295
  48.6 13.2 %copy-start.7 = (s32[48,1]{0,1:T(1,128)S(1)}, s32[48,1]{0,1:T(1,128)}, u32[]{:S(2)}) copy-start(s32[48,1]{0,1:T(1,128)} %param.16) | copy-start | bytes 580
  48.6 14.9 %copy-start.2 = (s32[48,6,16]{0,2,1:T(8,128)S(1)}, s32[48,6,16]{0,2,1:T(8,128)}, u32[]{:S(2)}) copy-start(s32[48,6,16]{0,2,1:T(8,128)} %param.20) | copy-start | bytes 55300
  48.6 15.0 %copy-start.5 = (bf16[48,3]{0,1:T(4,128)(2,1)S(1)}, bf16[48,3]{0,1:T(4,128)(2,1)}, u32[]{:S(2)}) copy-start(bf16[48,3]{0,1:T(4,128)(2,1)} %param.19) | copy-start | bytes 868
  48.6 15.1 %copy-start.4 = (s32[48,2]{0,1:T(2,128)S(1)}, s32[48,2]{0,1:T(2,128)}, u32[]{:S(2)}) copy-start(s32[48,2]{0,1:T(2,128)} %param.17) | copy-start | bytes 1156
  48.6 27.1 %copy-start.6 = (bf16[48,2]{0,1:T(2,128)(2,1)S(1)}, bf16[48,2]{0,1:T(2,128)(2,1)}, u32[]{:S(2)}) copy-start(bf16[48,2]{0,1:T(2,128)(2,1)} %param.18) | copy-start | bytes 580
  58.1 17.8 %copy-start.3 = (f32[3,32]{1,0:T(4,128)S(1)}, f32[3,32]{1,0:T(4,128)}, u32[]{:S(2)}) copy-start(f32[3,32]{1,0:T(4,128)} %param.23) | copy-start | bytes 1156
  58.1 70.8 %collective-permute-start.6 = (bf16[48,32,384]{2,1,0:T(8,128)(2,1)}, bf16[48,32,384]{2,1,0:T(8,128)(2,1)S(1)}, u32[]{:S(2)}, u32[]{:S(2)}) collective-permute-start(bf16[48,32,384]{2,1,0:T(8,128)(2,1)} %get-tuple-element.33), channel_id=1, source_target_pairs={{0,2},{2,4},{4,6},{6,0},{1,3},{3,5},{5,7},{7,1},{8,10},{10,12},{12... | collective-permute-start | bytes 3538952 | tf_op jit(solution)/shard_map/ppermute | solution.py:310
  64.2 39.4 %collective-permute-start.3 = (f32[48,128]{1,0:T(8,128)S(1)}, f32[48,128]{1,0:T(8,128)S(1)}, u32[]{:S(2)}, u32[]{:S(2)}) collective-permute-start(f32[48,128]{1,0:T(8,128)S(1)} %pad.12.refs_4_.refs_8_), channel_id=1, source_target_pairs={{0,2},{2,4},{4,6},{6,0},{1,3},{3,5},{5,7},{7,1},{8,10},{10,12},{12... | collective-permute-start | bytes 73736 | tf_op jit(solution)/shard_map/ppermute | solution.py:310
  67.8 64.4 %collective-permute-start.7 = (bf16[48,32,384]{2,1,0:T(8,128)(2,1)}, bf16[48,32,384]{2,1,0:T(8,128)(2,1)S(1)}, u32[]{:S(2)}, u32[]{:S(2)}) collective-permute-start(bf16[48,32,384]{2,1,0:T(8,128)(2,1)} %get-tuple-element.34), channel_id=1, source_target_pairs={{0,4},{2,6},{4,0},{6,2},{1,5},{3,7},{5,1},{7,3},{8,12},{10,14},{12... | collective-permute-start | bytes 3538952 | tf_op jit(solution)/shard_map/ppermute | solution.py:310
  71.2 61.0 %collective-permute-start.8 = (bf16[48,32,384]{2,1,0:T(8,128)(2,1)}, bf16[48,32,384]{2,1,0:T(8,128)(2,1)}, u32[]{:S(2)}, u32[]{:S(2)}) collective-permute-start(bf16[48,32,384]{2,1,0:T(8,128)(2,1)} %get-tuple-element.35), channel_id=1, source_target_pairs={{0,6},{2,0},{4,2},{6,4},{1,7},{3,1},{5,3},{7,5},{8,14},{10,8},{12,... | collective-permute-start | bytes 3538952 | tf_op jit(solution)/shard_map/ppermute | solution.py:310
  77.8 77.4 %all-to-all-start.3 = ((f32[32,2,128]{2,1,0:T(2,128)}), f32[32,2,128]{2,1,0:T(2,128)S(1)}, u32[]{:S(2)}, u32[]{:S(2)}) async-start(f32[32,2,128]{2,1,0:T(2,128)} %bitcast.19), calls=%async_computation.3 | async-start | bytes 65536 | tf_op jit(solution)/shard_map/all_to_all | solution.py:403
  101.1 15.6 %collective-permute-start.4 = (f32[48,128]{1,0:T(8,128)S(1)}, f32[48,128]{1,0:T(8,128)S(1)}, u32[]{:S(2)}, u32[]{:S(2)}) collective-permute-start(f32[48,128]{1,0:T(8,128)S(1)} %pad.12.refs_4_.refs_8_), channel_id=1, source_target_pairs={{0,4},{2,6},{4,0},{6,2},{1,5},{3,7},{5,1},{7,3},{8,12},{10,14},{12... | collective-permute-start | bytes 73736 | tf_op jit(solution)/shard_map/ppermute | solution.py:310
  103.6 20.1 %collective-permute-start.5 = (f32[48,128]{1,0:T(8,128)S(1)}, f32[48,128]{1,0:T(8,128)S(1)}, u32[]{:S(2)}, u32[]{:S(2)}) collective-permute-start(f32[48,128]{1,0:T(8,128)S(1)} %pad.12.refs_4_.refs_8_), channel_id=1, source_target_pairs={{0,6},{2,0},{4,2},{6,4},{1,7},{3,1},{5,3},{7,5},{8,14},{10,8},{12,... | collective-permute-start | bytes 73736 | tf_op jit(solution)/shard_map/ppermute | solution.py:310
  116.7 15.5 %collective-permute-start = (bf16[8,32,384]{2,1,0:T(8,128)(2,1)S(1)}, bf16[8,32,384]{2,1,0:T(8,128)(2,1)S(1)}, u32[]{:S(2)}, u32[]{:S(2)}) collective-permute-start(bf16[8,32,384]{2,1,0:T(8,128)(2,1)S(1)} %all-to-all-done.refs_0_), channel_id=1, source_target_pairs={{0,8},{8,16},{16,24},{24,0},{32,40},{40,48},{48,56},{56,32},{64,72... | collective-permute-start | bytes 589832 | tf_op jit(solution)/shard_map/ppermute | solution.py:301
  123.7 14.5 %collective-permute-start.1 = (bf16[8,32,384]{2,1,0:T(8,128)(2,1)S(1)}, bf16[8,32,384]{2,1,0:T(8,128)(2,1)S(1)}, u32[]{:S(2)}, u32[]{:S(2)}) collective-permute-start(bf16[8,32,384]{2,1,0:T(8,128)(2,1)S(1)} %all-to-all-done.refs_0_), channel_id=1, source_target_pairs={{0,16},{8,24},{16,0},{24,8},{32,48},{40,56},{48,32},{56,40},{64,80... | collective-permute-start | bytes 589832 | tf_op jit(solution)/shard_map/ppermute | solution.py:301
  128.8 10.1 %collective-permute-start.2 = (bf16[8,32,384]{2,1,0:T(8,128)(2,1)S(1)}, bf16[8,32,384]{2,1,0:T(8,128)(2,1)S(1)}, u32[]{:S(2)}, u32[]{:S(2)}) collective-permute-start(bf16[8,32,384]{2,1,0:T(8,128)(2,1)S(1)} %all-to-all-done.refs_0_), channel_id=1, source_target_pairs={{0,24},{8,0},{16,8},{24,16},{32,56},{40,32},{48,40},{56,48},{64,88... | collective-permute-start | bytes 589832 | tf_op jit(solution)/shard_map/ppermute | solution.py:301
  138.9 1.3 copy-start.1
  155.2 27.1 %all-to-all-start.1 = ((bf16[4,8,32,384]{3,2,1,0:T(8,128)(2,1)}), bf16[4,8,32,384]{3,2,1,0:T(8,128)(2,1)S(1)}, u32[]{:S(2)}, u32[]{:S(2)}) async-start(bf16[4,8,32,384]{3,2,1,0:T(8,128)(2,1)} %bitcast.81), calls=%async_computation.1 | async-start | bytes 1572864 | tf_op jit(solution)/shard_map/all_to_all | solution.py:270
  162.2 14.2 %collective-permute-start.9 = (f32[32,2,128]{2,1,0:T(2,128)S(1)}, f32[32,2,128]{2,1,0:T(2,128)S(1)}, u32[]{:S(2)}, u32[]{:S(2)}) collective-permute-start(f32[32,2,128]{2,1,0:T(2,128)S(1)} %all-to-all-done.3), channel_id=1, source_target_pairs={{0,2},{2,4},{4,6},{6,0},{1,3},{3,5},{5,7},{7,1},{8,10},{10,12},{12... | collective-permute-start | bytes 98312 | tf_op jit(solution)/shard_map/ppermute | solution.py:310
  169.8 7.3 %collective-permute-start.10 = (f32[32,2,128]{2,1,0:T(2,128)S(1)}, f32[32,2,128]{2,1,0:T(2,128)S(1)}, u32[]{:S(2)}, u32[]{:S(2)}) collective-permute-start(f32[32,2,128]{2,1,0:T(2,128)S(1)} %all-to-all-done.3), channel_id=1, source_target_pairs={{0,4},{2,6},{4,0},{6,2},{1,5},{3,7},{5,1},{7,3},{8,12},{10,14},{12... | collective-permute-start | bytes 98312 | tf_op jit(solution)/shard_map/ppermute | solution.py:310
  173.6 5.8 %collective-permute-start.11 = (f32[32,2,128]{2,1,0:T(2,128)S(1)}, f32[32,2,128]{2,1,0:T(2,128)S(1)}, u32[]{:S(2)}, u32[]{:S(2)}) collective-permute-start(f32[32,2,128]{2,1,0:T(2,128)S(1)} %all-to-all-done.3), channel_id=1, source_target_pairs={{0,6},{2,0},{4,2},{6,4},{1,7},{3,1},{5,3},{7,5},{8,14},{10,8},{12,... | collective-permute-start | bytes 98312 | tf_op jit(solution)/shard_map/ppermute | solution.py:310
  183.1 55.1 %all-to-all-start.2 = ((bf16[8,32,384]{2,1,0:T(8,128)(2,1)}), bf16[8,32,384]{2,1,0:T(8,128)(2,1)S(1)}, u32[]{:S(2)}, u32[]{:S(2)}) async-start(bf16[8,32,384]{2,1,0:T(8,128)(2,1)} %fusion.18), calls=%async_computation.2 | async-start | bytes 393216 | tf_op jit(solution)/shard_map/all_to_all | solution.py:270
  205.8 12.4 %collective-permute-start.12 = (f32[3,8,128]{2,0,1:T(4,128)S(1)}, f32[3,8,128]{2,0,1:T(4,128)S(1)}, u32[]{:S(2)}, u32[]{:S(2)}) collective-permute-start(f32[3,8,128]{2,0,1:T(4,128)S(1)} %copy.158), channel_id=1, source_target_pairs={{0,8},{8,16},{16,24},{24,32},{32,40},{40,48},{48,56},{56,64},{64,7... | collective-permute-start | bytes 36872 | tf_op jit(solution)/shard_map/ppermute | solution.py:424
  208.2 10.1 %collective-permute-start.13 = (f32[3,8,128]{2,0,1:T(4,128)S(1)}, f32[3,8,128]{2,0,1:T(4,128)S(1)}, u32[]{:S(2)}, u32[]{:S(2)}) collective-permute-start(f32[3,8,128]{2,0,1:T(4,128)S(1)} %copy.159), channel_id=1, source_target_pairs={{8,0},{16,8},{24,16},{32,24},{40,32},{48,40},{56,48},{64,56},{72,6... | collective-permute-start | bytes 36872 | tf_op jit(solution)/shard_map/ppermute | solution.py:425
